TPU v7x, 128 devices: a whole 4x4x4 slice. The times are simulated.
128 devices in a mesh: peer: 32 (over z_hi, x, y), zero: 4 (over z_lo, core).
Axes of the slice: x: 4, y: 4, z: 4 (z_hi: 2, z_lo: 2; z = z_hi * 2 + z_lo), core: 2. Of those that a mesh axis runs over, the one named last changes fastest.
Arguments:
- tokens: bfloat16 [32, 2048, 1024], P('peer', 'zero'), may hold values from -6 to 6
- out_grad: bfloat16 [32, 2048, 1024], P('peer', 'zero'), may hold values from -6 to 6
- step: int32 [1], replicated, may hold values from 0 to 3999
- up_param: float32 [32, 1024, 2048], P('peer', 'zero'), may hold values from -0.2 to 0.2
- down_param: float32 [32, 2048, 1024], P('peer', 'zero'), may hold values from -0.2 to 0.2
- up_first: float32 [32, 1024, 2048], P('peer', 'zero'), may hold values from -27.1529 to 27.1529
- down_first: float32 [32, 2048, 1024], P('peer', 'zero'), may hold values from -27.1529 to 27.1529
- up_second: float32 [32, 1024, 2048], P('peer', 'zero'), may hold values from 0.8192 to 819.2
- down_second: float32 [32, 2048, 1024], P('peer', 'zero'), may hold values from 0.8192 to 819.2
Outputs:
- new_up: float32 [32, 1024, 2048], P('peer', 'zero')
- new_down: float32 [32, 2048, 1024], P('peer', 'zero')
- new_up_first: float32 [32, 1024, 2048], P('peer', 'zero')
- new_down_first: float32 [32, 2048, 1024], P('peer', 'zero')
- new_up_second: float32 [32, 1024, 2048], P('peer', 'zero')
- new_down_second: float32 [32, 2048, 1024], P('peer', 'zero')
All inputs are finite; a program needn't handle non-finite values.
Results may differ from a plain program's by a relative error of at most 0.0065.
Values may be sent and summed in bfloat16 or wider, within the bound.
No kernel may reach another device: no remote copies, remote signals or barrier semaphores. Data moves between devices by JAX's collectives and lax.ppermute only.
A program may use at most 128 MiB of HBM per device.

v0:
```python
from functools import partial

import jax
import jax.numpy as jnp
from jax import lax
from jax.sharding import PartitionSpec as P


def for_sending(array):
    return jax.tree.map(lambda a: a.astype(jnp.bfloat16) if a.dtype == jnp.float32 else a, array)


def passed_along(array, axis, by):
    size = lax.axis_size(axis)
    return lax.ppermute(array, axis, [(i, (i + by) % size) for i in range(size)])


def gelu_tanh(values):
    return (
        0.5
        * values
        * (1.0 + jnp.tanh(0.7978845608 * (values + 0.044715 * values * values * values)))
    )


def adam_update(param, first, second, grad, first_fix, second_fix):
    first_new = 0.9 * first + 0.1 * grad
    second_new = 0.999 * second + 0.001 * grad * grad
    local = param - 0.01 * (first_new / first_fix) / (jnp.sqrt(second_new / second_fix) + 1e-08)
    return (local, first_new, second_new)


def across_rows(left, right):
    return lax.dot_general(
        left, right, (((0,), (0,)), ((), ())), preferred_element_type=jnp.float32
    )


def from_partner(pair, by):
    return jax.tree.map(
        lambda part, own: part.astype(own.dtype), passed_along(for_sending(pair), "peer", -by), pair
    )


def body(
    tokens, out_grad, step, up_param, down_param, up_first, down_first, up_second, down_second
):
    grad_rows = out_grad[0]
    widened = tokens[0].astype(jnp.float32)
    center = jnp.mean(widened, axis=1, keepdims=True)
    spread = jnp.mean((widened - center) * (widened - center), axis=1, keepdims=True)
    normed = ((widened - center) * lax.rsqrt(spread + 1e-05)).astype(jnp.bfloat16)
    up_low = up_param[0].astype(jnp.bfloat16)
    down_low = down_param[0].astype(jnp.bfloat16)
    up_whole, down_whole = (
        lax.all_gather(up_low, "zero", axis=0, tiled=True),
        lax.all_gather(down_low, "zero", axis=0, tiled=True),
    )
    pre = jnp.dot(normed, up_whole, preferred_element_type=jnp.float32)
    active, backward = jax.vjp(gelu_tanh, pre)
    act_grad = lax.dot_general(
        grad_rows, down_whole, (((1,), (1,)), ((), ())), preferred_element_type=jnp.float32
    )
    act = active.astype(jnp.bfloat16)
    pre_grad = backward(act_grad)[0].astype(jnp.bfloat16)
    columns = normed
    up_grad = lax.psum_scatter(
        across_rows(columns, pre_grad).astype(jnp.bfloat16), "zero", scatter_dimension=0, tiled=True
    ).astype(jnp.float32)
    columns = act
    down_grad = lax.psum_scatter(
        across_rows(columns, grad_rows).astype(jnp.bfloat16),
        "zero",
        scatter_dimension=0,
        tiled=True,
    ).astype(jnp.float32)
    count = (step[0] + 1).astype(jnp.float32)
    first_fix = 1.0 - jnp.power(jnp.float32(0.9), count)
    second_fix = 1.0 - jnp.power(jnp.float32(0.999), count)
    up_local, up_first_new, up_second_new = adam_update(
        up_param[0], up_first[0], up_second[0], up_grad, first_fix, second_fix
    )
    down_local, down_first_new, down_second_new = adam_update(
        down_param[0], down_first[0], down_second[0], down_grad, first_fix, second_fix
    )
    levels = lax.axis_size("peer").bit_length() - 1
    branches = [partial(from_partner, by=2**level) for level in range(levels)]
    up_other, down_other = lax.switch(step[0] % levels, branches, (up_local, down_local))
    new_up = 0.5 * (up_local + up_other)
    new_down = 0.5 * (down_local + down_other)
    return (
        new_up[None],
        new_down[None],
        up_first_new[None],
        down_first_new[None],
        up_second_new[None],
        down_second_new[None],
    )


def solution(mesh):
    in_specs = (
        P("peer", "zero", None),
        P("peer", "zero", None),
        P(),
        P("peer", "zero", None),
        P("peer", "zero", None),
        P("peer", "zero", None),
        P("peer", "zero", None),
        P("peer", "zero", None),
        P("peer", "zero", None),
    )
    out_specs = (
        P("peer", "zero", None),
        P("peer", "zero", None),
        P("peer", "zero", None),
        P("peer", "zero", None),
        P("peer", "zero", None),
        P("peer", "zero", None),
    )
    return jax.shard_map(body, mesh=mesh, in_specs=in_specs, out_specs=out_specs, check_vma=False)
```

profile of v0, /device:TPU:1, one launch (start us, length us, event | category | flops | bytes accessed | tf_op | source)
XLA Modules:
  0.0 289.3 jit_solution(9134113312605311750)
XLA Ops:
  7.2 2.9 bitcast_convert_fusion.1
  10.2 1.1 bitcast_convert_fusion
  11.4 1.5 convert_reduce_fusion
  12.9 0.4 fusion.9
  13.4 47.1 %all-gather.3.cloned.1.call-done = bf16[1024,2048]{1,0:T(8,128)(2,1)} async-done(((bf16[256,2048]{1,0:T(8,128)(2,1)}), bf16[1024,2048]{1,0:T(8,128)(2,1)}) %all-gather.3.cloned.1.call-update) | async-done | bytes 4194320 | tf_op jit(solution)/shard_map/all_gather | solution.py:56
  60.5 6.6 %fusion.40 = f32[512,2048]{1,0:T(8,128)} fusion(bf16[1024,2048]{1,0:T(8,128)(2,1)} %all-gather.3.cloned.1.call-done, bf16[1,512,1024]{2,1,0:T(8,128)(2,1)S(1)} %copy-done.3, f32[512]{0:T(512)S(1)} %add_rsqrt_fusion, f32[512]{0:T(512)S(1)} %broadcast_multiply_fusion), kind=kOutput, calls=%fused_computation.55 | convolution fusion | flops 2149580800 | bytes 9441280 | tf_op jit(solution)/shard_map/dot_general | solution.py:59
  67.1 43.1 %all-gather.5.cloned.1.call-done = bf16[2048,1024]{1,0:T(8,128)(2,1)} async-done(((bf16[512,1024]{1,0:T(8,128)(2,1)}), bf16[2048,1024]{1,0:T(8,128)(2,1)}) %all-gather.5.cloned.1.call-update) | async-done | bytes 4194320 | tf_op jit(solution)/shard_map/all_gather | solution.py:57
  110.2 11.0 %convolution_convert_fusion.1 = bf16[1024,2048]{1,0:T(8,128)(2,1)} fusion(f32[512,2048]{1,0:T(8,128)} %fusion.40, bf16[2048,1024]{1,0:T(8,128)(2,1)} %all-gather.5.cloned.1.call-done, bf16[1,512,1024]{2,1,0:T(8,128)(2,1)S(1)} %copy-done, bf16[1,512,1024]{2,1,0:T(8,128)(2,1)S(1)} %copy-done.3, f32[512]{0:T(512)S(1)} %add_rsqrt_fusion, ...), kind=kOutput, calls=%fused_computation.12 | convolution fusion | flops 4324327424 | bytes 14684160 | tf_op jit(solution)/shard_map/dot_general | solution.py:34
  121.2 0.2 reduce-scatter.5.cloned.1.call-start
  121.5 7.1 %convolution_convert_fusion = bf16[2048,1024]{1,0:T(8,128)(2,1)} fusion(f32[512,2048]{1,0:T(8,128)} %fusion.40, bf16[1,512,1024]{2,1,0:T(8,128)(2,1)S(1)} %copy-done), kind=kOutput, calls=%fused_computation.11 | convolution fusion | flops 2159017984 | bytes 9437184 | tf_op jit(solution)/shard_map/dot_general | solution.py:34
  129.3 38.2 %reduce-scatter.3.cloned.1.call-done = bf16[256,2048]{1,0:T(8,128)(2,1)} async-done(((bf16[1024,2048]{1,0:T(8,128)(2,1)}), bf16[256,2048]{1,0:T(8,128)(2,1)}) %reduce-scatter.3.cloned.1.call-update) | async-done | bytes 1048592 | tf_op jit(solution)/shard_map/reduce_scatter | solution.py:67
  167.5 6.7 %fusion.23 = (f32[1,256,2048]{2,1,0:T(8,128)}, f32[256,2048]{1,0:T(8,128)S(1)}, f32[1,256,2048]{2,1,0:T(8,128)}) fusion(bf16[256,2048]{1,0:T(8,128)(2,1)} %reduce-scatter.3.cloned.1.call-done, f32[1,256,2048]{2,1,0:T(8,128)} %param.21, f32[]{:T(128)} %bitcast.7, f32[]{:T(128)} %bitcast.5, f32[1,256,2048]{2,1,0:T(8,128)} %param.19, f32[1,256,2048]{2,1,0:T(8,128)} %param.17), kind=kLoop, calls=%fused_computation.41 | loop fusion | flops 7340032 | bytes 13631496 | tf_op jit(solution)/shard_map/broadcast_in_dim | solution.py:96
  174.2 41.9 %reduce-scatter.5.cloned.1.call-done = bf16[512,1024]{1,0:T(8,128)(2,1)} async-done(((bf16[2048,1024]{1,0:T(8,128)(2,1)}), bf16[512,1024]{1,0:T(8,128)(2,1)}) %reduce-scatter.5.cloned.1.call-update) | async-done | bytes 1048592 | tf_op jit(solution)/shard_map/reduce_scatter | solution.py:71
  216.1 7.5 %fusion.22 = (f32[1,512,1024]{2,1,0:T(8,128)}, f32[512,1024]{1,0:T(8,128)}, f32[1,512,1024]{2,1,0:T(8,128)}) fusion(bf16[512,1024]{1,0:T(8,128)(2,1)} %reduce-scatter.5.cloned.1.call-done, f32[1,512,1024]{2,1,0:T(8,128)} %param.22, f32[]{:T(128)} %bitcast.7, f32[]{:T(128)} %bitcast.5, f32[1,512,1024]{2,1,0:T(8,128)} %param.20, f32[1,512,1024]{2,1,0:T(8,128)} %param.18), kind=kLoop, calls=%fused_computation.40 | loop fusion | flops 7340032 | bytes 13631496 | tf_op jit(solution)/shard_map/broadcast_in_dim | solution.py:97
  223.5 51.7 %conditional.4 = (f32[256,2048]{1,0:T(8,128)}, f32[512,1024]{1,0:T(8,128)}) conditional(s32[]{:T(128)} %clamp.3, (f32[256,2048]{1,0:T(8,128)S(1)}, f32[512,1024]{1,0:T(8,128)}) %tuple.60, (f32[256,2048]{1,0:T(8,128)S(1)}, f32[512,1024]{1,0:T(8,128)}) %tuple.60, (f32[256,2048]{1,0:T(8,128)S(1)}, ...), branch_computations={%region_4.5_spmd, %region_5.6_spmd, %region_6.7_spmd, %region_7.8_... | conditional | flops 2097152 | bytes 20971616
  223.5 1.7 convert_element_type.107
  225.3 2.7 collective-permute-start.9
  228.1 0.5 collective-permute-start.8
  228.6 22.7 %collective-permute-done.9 = bf16[512,1024]{1,0:T(8,128)(2,1)S(1)} collective-permute-done((bf16[512,1024]{1,0:T(8,128)(2,1)S(1)}, bf16[512,1024]{1,0:T(8,128)(2,1)S(1)}, u32[]{:S(2)}, u32[]{:S(2)}) %collective-permute-start.9) | collective-permute-done | bytes 1048608 | tf_op jit(solution)/shard_map/cond/branch_4_fun/ppermute | solution.py:15
  251.2 1.6 convert_element_type.144
  252.8 20.9 %collective-permute-done.8 = bf16[256,2048]{1,0:T(8,128)(2,1)S(1)} collective-permute-done((bf16[256,2048]{1,0:T(8,128)(2,1)S(1)}, bf16[256,2048]{1,0:T(8,128)(2,1)S(1)}, u32[]{:S(2)}, u32[]{:S(2)}) %collective-permute-start.8) | collective-permute-done | bytes 1048608 | tf_op jit(solution)/shard_map/cond/branch_4_fun/ppermute | solution.py:15
  273.7 1.6 convert_element_type.139
  275.3 4.2 %multiply_bitcast_fusion = f32[1,512,1024]{2,1,0:T(8,128)} fusion(f32[512,1024]{1,0:T(8,128)} %get-tuple-element.59, f32[512,1024]{1,0:T(8,128)} %get-tuple-element.57), kind=kLoop, calls=%fused_computation.32 | loop fusion | flops 1048576 | bytes 6291456 | tf_op jit(solution)/shard_map/broadcast_in_dim | solution.py:93
  279.4 3.3 %multiply_bitcast_fusion.1 = f32[1,256,2048]{2,1,0:T(8,128)} fusion(f32[256,2048]{1,0:T(8,128)S(1)} %get-tuple-element.62, f32[256,2048]{1,0:T(8,128)} %get-tuple-element.56), kind=kLoop, calls=%fused_computation.33 | loop fusion | flops 1048576 | bytes 6291456 | tf_op jit(solution)/shard_map/broadcast_in_dim | solution.py:92
  (18 shorter events, 0.4 us)
Async XLA Ops:
  7.2 103.0 %copy-start = (bf16[1,512,1024]{2,1,0:T(8,128)(2,1)S(1)}, bf16[1,512,1024]{2,1,0:T(8,128)(2,1)}, u32[]{:S(2)}) copy-start(bf16[1,512,1024]{2,1,0:T(8,128)(2,1)} %param.15) | copy-start | bytes 3145732
  7.2 3.0 %copy-start.2 = (f32[1,512,1024]{2,1,0:T(8,128)S(1)}, f32[1,512,1024]{2,1,0:T(8,128)}, u32[]{:S(2)}) copy-start(f32[1,512,1024]{2,1,0:T(8,128)} %param.18) | copy-start | bytes 6291460
  7.2 53.3 %all-gather.3.cloned.1.call-start = ((), (), s32[]{:S(2)}) async-start(), calls=%async_computation.2 | async-start | bytes 5242880 | tf_op jit(solution)/shard_map/all_gather | solution.py:56
  10.1 100.1 %all-gather.5.cloned.1.call-start = ((), (), s32[]{:S(2)}) async-start(), calls=%async_computation.3 | async-start | bytes 5242880 | tf_op jit(solution)/shard_map/all_gather | solution.py:57
  11.3 1.6 copy-start.3
  11.4 156.1 %reduce-scatter.3.cloned.1.call-start = ((), (), s32[]{:S(2)}) async-start(), calls=%async_computation.4 | async-start | bytes 5242880 | tf_op jit(solution)/shard_map/reduce_scatter | solution.py:67
  121.2 94.8 %reduce-scatter.5.cloned.1.call-start = ((), (), s32[]{:S(2)}) async-start(), calls=%async_computation.5 | async-start | bytes 5242880 | tf_op jit(solution)/shard_map/reduce_scatter | solution.py:71
  225.3 25.9 %collective-permute-start.9 = (bf16[512,1024]{1,0:T(8,128)(2,1)S(1)}, bf16[512,1024]{1,0:T(8,128)(2,1)S(1)}, u32[]{:S(2)}, u32[]{:S(2)}) collective-permute-start(bf16[512,1024]{1,0:T(8,128)(2,1)S(1)} %convert_element_type.107), channel_id=1, source_target_pairs={{0,64},{4,68},{8,72},{12,76},{16,80},{20,84},{24,88},{28,92},{32,9... | collective-permute-start | bytes 3145736 | tf_op jit(solution)/shard_map/cond/branch_4_fun/ppermute | solution.py:15
  228.1 45.6 %collective-permute-start.8 = (bf16[256,2048]{1,0:T(8,128)(2,1)S(1)}, bf16[256,2048]{1,0:T(8,128)(2,1)S(1)}, u32[]{:S(2)}, u32[]{:S(2)}) collective-permute-start(bf16[256,2048]{1,0:T(8,128)(2,1)S(1)} %convert_element_type.105), channel_id=1, source_target_pairs={{0,64},{4,68},{8,72},{12,76},{16,80},{20,84},{24,88},{28,92},{32,9... | collective-permute-start | bytes 3145736 | tf_op jit(solution)/shard_map/cond/branch_4_fun/ppermute | solution.py:15
  279.4 3.3 %copy-start.1 = (bf16[1,512,1024]{2,1,0:T(8,128)(2,1)S(1)}, bf16[1,512,1024]{2,1,0:T(8,128)(2,1)}, u32[]{:S(2)}) copy-start(bf16[1,512,1024]{2,1,0:T(8,128)(2,1)} %param.15) | copy-start | bytes 3145732
Sparse Core Ops, SparseCore 0:
  10.3 50.1 all-gather.2
  62.7 47.4 all-gather.4
  121.3 46.0 reduce-scatter.2
  169.8 46.2 reduce-scatter.4
where the time goes:
time: 290 us; the launch traced here: 289 us
  waiting for transfers between devices  214 us (74%)
  other arithmetic  32.6 us (11%)
  matrix products  24.7 us (9%)
  between operations  14.6 us (5%)
  starting transfers between devices  3.47 us (1%)
    all_gather x1, waiting for transfers between devices, body(): lax.all_gather(up_low, 'zero', axis=0, tiled=True)  47.1 us
    ppermute x2, waiting for transfers between devices, passed_along(): lax.ppermute(array, axis, [(i, (i + by) % size) for i in range(size)])  43.5 us
    all_gather x1, waiting for transfers between devices, body(): lax.all_gather(down_low, 'zero', axis=0, tiled=True)  43.1 us
    reduce_scatter x1, waiting for transfers between devices, body(): lax.psum_scatter(across_rows(columns, grad_rows).astype(jnp.bfloat16), 'z...  41.9 us
    reduce_scatter x1, waiting for transfers between devices, body(): lax.psum_scatter(across_rows(columns, pre_grad).astype(jnp.bfloat16), 'ze...  38.2 us
    dot_general x2, matrix products, across_rows(): lax.dot_general(left, right, (((0,), (0,)), ((), ())), preferred_element_...  18.1 us
    broadcast_in_dim x1, other arithmetic, body(): down_second_new[None]  7.47 us
    broadcast_in_dim x1, other arithmetic, body(): up_second_new[None]  6.69 us
  transfers between devices with their start and end apart: 6, of which 6 were waited for; matrix products, arithmetic and copies ran while one was open for 9% of the time, Pallas kernels for 0%

commit v1 on v0

v1 whole, which is shorter than its diff:
```python
from functools import partial

import jax
import jax.numpy as jnp
from jax import lax
from jax.experimental import pallas as pl
from jax.experimental.pallas import tpu as pltpu
from jax.sharding import PartitionSpec as P


WIDTHS = (640, 384)
STARTS = tuple(sum(WIDTHS[:c]) for c in range(len(WIDTHS)))
CHUNKS = len(WIDTHS)
LOW = jnp.bfloat16
WIDE = jnp.float32
VMEM = pl.BlockSpec(memory_space=pltpu.VMEM)
HBM = pl.BlockSpec(memory_space=pltpu.HBM)
ANY = pl.BlockSpec(memory_space=pl.ANY)
SMEM = pl.BlockSpec(memory_space=pltpu.SMEM)
LIMIT = 20 * 2**20


def shape(*sizes, dtype=LOW):
    return jax.ShapeDtypeStruct(sizes, dtype)


def params(limit=LIMIT):
    return pltpu.CompilerParams(vmem_limit_bytes=limit)


def swap(array, mask):
    size = lax.axis_size("zero")
    return lax.ppermute(array, "zero", [(i, i ^ mask) for i in range(size)])


def from_partner(array, by):
    size = lax.axis_size("peer")
    return lax.ppermute(array, "peer", [(i, (i - by) % size) for i in range(size)])


def dot(left, right, over=((1,), (0,))):
    return lax.dot_general(left, right, (over, ((), ())), preferred_element_type=WIDE)


def adam(param, first, second, grad, fixes):
    first_new = 0.9 * first + 0.1 * grad
    second_new = 0.999 * second + 0.001 * grad * grad
    scaled = first_new * (0.01 / fixes[0])
    local = param - scaled / (jnp.sqrt(second_new * (1.0 / fixes[1])) + 1e-08)
    return local, first_new, second_new


def cut_kernel(place, up, *outs):
    step = 32
    width = outs[0].shape[1]

    def rows(i, _):
        at = pl.ds(pl.multiple_of(i * step, step), step)
        for k in range(4):
            col = pl.multiple_of((place[0] ^ k) * width, width)
            outs[k][at, :] = up[at, pl.ds(col, width)].astype(LOW)
        return 0

    lax.fori_loop(0, up.shape[0] // step, rows, 0)


def cut(place, up):
    return pl.pallas_call(
        cut_kernel,
        out_shape=[shape(up.shape[0], up.shape[1] // 4)] * 4,
        in_specs=[SMEM, VMEM],
        out_specs=[VMEM] * 4,
        compiler_params=params(),
        name="cut",
    )(place, up)


def norm_kernel(tokens, grads, _, normed, *pieces):
    step = 64

    def rows(i, _):
        at = pl.ds(pl.multiple_of(i * step, step), step)
        wide = tokens[at, :].astype(WIDE)
        centered = wide - jnp.mean(wide, axis=1, keepdims=True)
        spread = jnp.mean(centered * centered, axis=1, keepdims=True)
        normed[at, :] = (centered * lax.rsqrt(spread + 1e-05)).astype(LOW)
        for c, piece in enumerate(pieces):
            piece[at, :] = grads[at, STARTS[c] : STARTS[c] + WIDTHS[c]]
        return 0

    lax.fori_loop(0, tokens.shape[0] // step, rows, 0)


def norm(tokens, grads, after):
    rows, cols = tokens.shape
    return pl.pallas_call(
        norm_kernel,
        out_shape=[shape(rows, cols)] + [shape(rows, width) for width in WIDTHS],
        in_specs=[VMEM] * 2 + [ANY],
        out_specs=[VMEM] * (1 + CHUNKS),
        compiler_params=params(),
        name="norm",
    )(tokens, grads, after)


def hidden_kernel(place, u0, u1, u2, u3, left, right, act, slope, up, both):
    size = u0.shape[0]
    for k, u in enumerate((u0, u1, u2, u3)):
        up[pl.ds(pl.multiple_of((place[0] ^ k) * size, size), size), :] = u[...]
    half = left.shape[0]
    both[:half, :] = left[...]
    both[half:, :] = right[...]
    step = 256

    def rows(i, _):
        at = pl.ds(pl.multiple_of(i * step, step), step)
        pre = dot(both[at, :], up[...])
        square = pre * pre
        bent = jnp.tanh(0.7978845608 * (pre + 0.044715 * square * pre))
        lift = 0.5 * (1.0 + bent)
        act[:, at] = (pre * lift).T.astype(LOW)
        slope[at, :] = lift + 0.5 * pre * (1.0 - bent * bent) * (
            0.7978845608 + 0.1070322243 * square
        )
        return 0

    lax.fori_loop(0, 2 * half // step, rows, 0)


def hidden(place, ups, left, right):
    rows, full = left.shape
    width = ups[0].shape[1]
    return pl.pallas_call(
        hidden_kernel,
        out_shape=[shape(width, 2 * rows), shape(2 * rows, width, dtype=WIDE)],
        in_specs=[SMEM] + [VMEM] * 6,
        out_specs=[VMEM] * 2,
        scratch_shapes=[pltpu.VMEM((full, width), LOW), pltpu.VMEM((2 * rows, full), LOW)],
        compiler_params=params(),
        name="hidden",
    )(place, *ups, left, right)


def down_kernel(c, fixes, near, far, o0, o1, o2, o3, param, first, second, *rest):
    wholes, kept, (p, m, v, sems) = rest[-12:-8], rest[-8:-4], rest[-4:]
    local, send, mn, vn = kept
    cols = pl.ds(STARTS[c], WIDTHS[c])
    loads = [
        pltpu.make_async_copy(whole.at[:, cols], part, sems.at[i])
        for i, (whole, part) in enumerate(((param, p), (first, m), (second, v)))
    ]
    for load in loads:
        load.start()
    rows = o0.shape[0]
    local[...] = dot(near[:, :rows], o0[...])
    local[...] += dot(near[:, rows:], o1[:, STARTS[c] : STARTS[c] + WIDTHS[c]])
    local[...] += dot(far[:, :rows], o2[...])
    local[...] += dot(far[:, rows:], o3[...])
    for load in loads:
        load.wait()
    step = 64

    def some(i, _):
        at = pl.ds(pl.multiple_of(i * step, step), step)
        after, mn[at, :], vn[at, :] = adam(p[at, :], m[at, :], v[at, :], local[at, :], fixes)
        local[at, :] = after
        send[at, :] = after.astype(LOW)
        return 0

    lax.fori_loop(0, rows // step, some, 0)
    stores = [
        pltpu.make_async_copy(part, whole.at[:, cols], sems.at[i])
        for i, (whole, part) in enumerate(zip(wholes, kept))
    ]
    for store in stores:
        store.start()
    for store in stores:
        store.wait()


def down(c, fixes, near, far, ogs, param, first, second, news, after):
    rows, cols = param.shape
    part = (rows, WIDTHS[c])
    ins = [fixes, near, far, *ogs, param, first, second, after]
    in_specs = [SMEM] + [VMEM] * 6 + [HBM] * 3 + [ANY]
    aliases = {}
    if news is not None:
        aliases = {len(ins) + i: i for i in range(4)}
        ins += news
        in_specs += [HBM] * 4
    kinds = (WIDE, LOW, WIDE, WIDE)
    return pl.pallas_call(
        partial(down_kernel, c),
        out_shape=[shape(rows, cols, dtype=kind) for kind in kinds],
        in_specs=in_specs,
        out_specs=[HBM] * 4,
        input_output_aliases=aliases,
        scratch_shapes=[pltpu.VMEM(part, kind) for kind in kinds + (WIDE,) * 3]
        + [pltpu.SemaphoreType.DMA((4,))],
        compiler_params=params(),
        name="down",
    )(*ins)


def back_kernel(place, param, sa, sb, *refs):
    ogs, side, outs = refs[: 3 * CHUNKS], refs[3 * CHUNKS], refs[-6:-2]
    normed = refs[3 * CHUNKS + 1 : 3 * CHUNKS + 5]
    low, pre_grad = refs[-2:]
    rows = normed[0].shape[0]
    low[...] = param[...].astype(LOW)
    for k in range(4):
        got = None
        for c in range(CHUNKS):
            cols = slice(STARTS[c], STARTS[c] + WIDTHS[c])
            piece = side[:, cols] if k == 1 else ogs[(0, 0, 1, 2)[k] * CHUNKS + c][...]
            part = dot(piece, low[:, cols], ((1,), (1,)))
            got = part if got is None else got + part
        slope = (sa, sb)[k // 2][(k % 2) * rows : (k % 2 + 1) * rows, :]
        pre_grad[k * rows : (k + 1) * rows, :] = (got * slope).astype(LOW)
    size = outs[0].shape[0]
    for k in range(4):
        at = pl.ds(pl.multiple_of((place[0] ^ k) * size, size), size)
        total = None
        for j in range(4):
            part = dot(normed[j][:, at], pre_grad[j * rows : (j + 1) * rows, :], ((0,), (0,)))
            total = part if total is None else total + part
        outs[k][...] = total.astype(LOW)


def back(place, param, slopes, own, side, far, last, normed):
    hidden_size = param.shape[0]
    rows, full = normed[0].shape
    return pl.pallas_call(
        back_kernel,
        out_shape=[shape(full // 4, hidden_size)] * 4,
        in_specs=[SMEM] + [VMEM] * (3 + 3 * CHUNKS + 5),
        out_specs=[VMEM] * 4,
        scratch_shapes=[pltpu.VMEM(param.shape, LOW), pltpu.VMEM((4 * rows, hidden_size), LOW)],
        compiler_params=params(),
        name="back",
    )(place, param, *slopes, *own, *far, *last, side, *normed)


def up_kernel(base, place, fixes, left, right, param, first, second, *rest):
    local, send, first_new, second_new, p, m, v, mn, vn, sems = rest[-10:]
    rows, width = left.shape
    cols = [
        pl.ds(pl.multiple_of((place[0] ^ (base + i)) * width, width), width) for i in range(2)
    ]
    loads = [
        [
            pltpu.make_async_copy(whole.at[:, cols[i]], part.at[i], sems.at[3 * i + j])
            for j, (whole, part) in enumerate(((param, p), (first, m), (second, v)))
        ]
        for i in range(2)
    ]
    for load in loads[0] + loads[1]:
        load.start()
    stores = []
    step = 32
    for i, grads in enumerate((left, right)):
        for load in loads[i]:
            load.wait()

        def some(r, _):
            at = pl.ds(pl.multiple_of(r * step, step), step)
            to = pl.ds(pl.multiple_of(i * rows + r * step, step), step)
            after, mn[i, at, :], vn[i, at, :] = adam(
                p[i, at, :], m[i, at, :], v[i, at, :], grads[at, :].astype(WIDE), fixes
            )
            local[to, :] = after
            send[to, :] = after.astype(LOW)
            return 0

        lax.fori_loop(0, rows // step, some, 0)
        stores += [
            pltpu.make_async_copy(part.at[i], whole.at[:, cols[i]], sems.at[6 + 2 * i + j])
            for j, (whole, part) in enumerate(((first_new, mn), (second_new, vn)))
        ]
        for store in stores[-2:]:
            store.start()
    for store in stores:
        store.wait()


def up(base, place, fixes, left, right, param, first, second, news):
    rows, width = left.shape
    ins = [place, fixes, left, right, param, first, second]
    in_specs = [SMEM, SMEM, VMEM, VMEM, HBM, HBM, HBM]
    aliases = {}
    if news is not None:
        aliases = {len(ins): 2, len(ins) + 1: 3}
        ins += news
        in_specs += [HBM] * 2
    return pl.pallas_call(
        partial(up_kernel, base),
        in_specs=in_specs,
        out_specs=[VMEM, VMEM, HBM, HBM],
        out_shape=[
            shape(2 * rows, width, dtype=WIDE),
            shape(2 * rows, width),
            shape(*param.shape, dtype=WIDE),
            shape(*param.shape, dtype=WIDE),
        ],
        scratch_shapes=[pltpu.VMEM((2, rows, width), WIDE)] * 5
        + [pltpu.SemaphoreType.DMA((10,))],
        input_output_aliases=aliases,
        compiler_params=params(),
        name="up",
    )(*ins)


def mean_down_kernel(local, other, out):
    out[...] = 0.5 * (local[...] + other[...].astype(WIDE))


def mean_down(local, other):
    rows, cols = local.shape
    block = pl.BlockSpec((rows // 8, cols), lambda i: (i, 0))
    return pl.pallas_call(
        mean_down_kernel,
        grid=(8,),
        out_shape=shape(rows, cols, dtype=WIDE),
        in_specs=[block] * 2,
        out_specs=block,
        compiler_params=params(),
        name="mean_down",
    )(local, other)


def mean_up_kernel(base, place, local, other, *rest):
    out, kept, sems = rest[-3:]
    rows, width = kept.shape[1:]
    copies = []
    for i in range(2):
        kept[i] = 0.5 * (
            local[i * rows : (i + 1) * rows, :] + other[i * rows : (i + 1) * rows, :].astype(WIDE)
        )
        cols = pl.ds(pl.multiple_of((place[0] ^ (base + i)) * width, width), width)
        copies.append(pltpu.make_async_copy(kept.at[i], out.at[:, cols], sems.at[i]))
        copies[i].start()
    for copy in copies:
        copy.wait()


def mean_up(base, place, local, other, whole):
    rows, width = local.shape[0] // 2, local.shape[1]
    ins, in_specs, aliases = [place, local, other], [SMEM, VMEM, VMEM], {}
    if whole is not None:
        aliases = {3: 0}
        ins.append(whole)
        in_specs.append(HBM)
    return pl.pallas_call(
        partial(mean_up_kernel, base),
        in_specs=in_specs,
        out_specs=HBM,
        out_shape=shape(rows, 4 * width, dtype=WIDE),
        scratch_shapes=[pltpu.VMEM((2, rows, width), WIDE), pltpu.SemaphoreType.DMA((2,))],
        input_output_aliases=aliases,
        compiler_params=params(),
        name="mean_up",
    )(*ins)


def prepare(place, fixes, tokens, grads, up_p, down_p, up_m, down_m, up_v, down_v):
    first = cut(place, up_p)
    ups = [first[0]]
    for k in range(1, 4):
        ups.append(swap(first[k], k))
    n0, *own = norm(tokens, grads, first[0])
    n2 = swap(n0, 2)
    n1 = swap(n0, 1)
    side = swap(grads, 1)
    far, last = [], []
    for c in range(CHUNKS):
        far.append(swap(own[c], 2))
    near_act, near_slope = hidden(place, ups, n0, n1)
    n3 = swap(n2, 1)
    far_act, far_slope = hidden(place, ups, n2, n3)
    for c in range(CHUNKS):
        last.append(swap(far[c], 1))
    acts, slopes = (near_act, far_act), (near_slope, far_slope)
    news = None
    for c in range(CHUNKS - 1):
        ogs = (own[c], side, far[c], last[c])
        news = down(c, fixes, *acts, ogs, down_p, down_m, down_v, news, n0)
    g0, g1, g2, g3 = back(place, down_p, slopes, own, side, far, last, (n0, n1, n2, n3))
    g2 = swap(g2, 2)
    g3 = swap(g3, 3)
    g1 = swap(g1, 1)
    c = CHUNKS - 1
    ogs = (own[c], side, far[c], last[c])
    news = down(c, fixes, *acts, ogs, down_p, down_m, down_v, news, g0)
    near = up(0, place, fixes, g0, g1, up_p, up_m, up_v, None)
    return news, near, g2, g3


def finish(level, place, fixes, made, up_p, up_m, up_v):
    by = 2**level
    (down_local, send, *down_new), (near_local, near_send, *up_new), g2, g3 = made
    other = from_partner(send, by)
    near_other = from_partner(near_send, by)
    far_local, send, *up_new = up(2, place, fixes, g2, g3, up_p, up_m, up_v, up_new)
    far_other = from_partner(send, by)
    new_down = mean_down(down_local, other)
    new_up = mean_up(0, place, near_local, near_other, None)
    new_up = mean_up(2, place, far_local, far_other, new_up)
    return new_up, new_down, up_new[0], down_new[0], up_new[1], down_new[1]


def body(tokens, out_grad, step, *state):
    levels = lax.axis_size("peer").bit_length() - 1
    place = lax.axis_index("zero").astype(jnp.int32)[None]
    state = [a[0] for a in state]
    count = (step[0] + 1).astype(WIDE)
    fixes = jnp.stack(
        [1.0 - jnp.power(WIDE(0.9), count), 1.0 - jnp.power(WIDE(0.999), count)]
    )
    made = prepare(place, fixes, tokens[0], out_grad[0], *state)

    def branch(k, *args):
        return finish(k, *args)

    outs = lax.switch(
        step[0] % levels,
        [partial(branch, k) for k in range(levels)],
        place,
        fixes,
        made,
        *state[::2],
    )
    return tuple(a[None] for a in outs)


def solution(mesh):
    in_specs = (P("peer", "zero", None), P("peer", "zero", None), P()) + (
        P("peer", "zero", None),
    ) * 6
    out_specs = (P("peer", "zero", None),) * 6
    return jax.shard_map(body, mesh=mesh, in_specs=in_specs, out_specs=out_specs, check_vma=False)
```

time: 290 us -> 164 us (0.57)
  waiting for transfers between devices: 214 us -> 89.9 us
  Pallas kernels: 0 us -> 35.4 us
  other arithmetic: 32.6 us -> 0.08 us
  matrix products: 24.7 us -> 0 us
  starting transfers between devices: 3.47 us -> 20.7 us
  local copies, waits for them, and re-layouts: 0.03 us -> 15.5 us
  between operations: 14.6 us -> 1.75 us
    all_gather x2 -> x0, waiting for transfers between devices: 90.3 us -> none  [the longest x1 47.1 us: body(): lax.all_gather(up_low, 'zero', axis=0, tiled=True)]
    reduce_scatter x2 -> x0, waiting for transfers between devices: 80 us -> none  [the longest x1 41.9 us: body(): lax.psum_scatter(across_rows(columns, grad_rows).astype(jnp.bfloat16), 'z...]
    ppermute x2 -> x17, waiting for transfers between devices: 43.5 us -> 89.9 us  [the longest x14 50.8 us: swap(): return lax.ppermute(array, 'zero', [(i, i ^ mask) for i in range(size)])]
    pallas_call x0 -> x12, Pallas kernels: none -> 35.4 us  [the longest x2 10.3 us: down(): pl.pallas_call(partial(down_kernel, c), out_shape=[shape(rows, cols, dtyp...]
    dot_general x3 -> x0, matrix products: 24.7 us -> none  [the longest x2 18.1 us: across_rows(): lax.dot_general(left, right, (((0,), (0,)), ((), ())), preferred_element_...]
    broadcast_in_dim x4 -> x0, other arithmetic: 21.6 us -> none  [the longest x1 7.47 us: body(): down_second_new[None]]
    ppermute x2 -> x17, starting transfers between devices: 3.13 us -> 20.7 us  [the longest x14 14.1 us: swap(): return lax.ppermute(array, 'zero', [(i, i ^ mask) for i in range(size)])]
    unnamed x8 -> x62, local copies, waits for them, and re-layouts: 0.03 us -> 15.5 us
  transfers between devices with their start and end apart: 6 -> 17, of which waited for: 6 -> 6; matrix products, arithmetic and copies ran while one was open for 9% -> 0% of each run, Pallas kernels for 0% -> 15%
where the time goes in v1:
time: 164 us; the launch traced here: 163 us
  waiting for transfers between devices  89.9 us (55%)
  Pallas kernels  35.4 us (22%)
  starting transfers between devices  20.7 us (13%)
  local copies, waits for them, and re-layouts  15.5 us (9%)
  between operations  1.75 us (1%)
    ppermute x14, waiting for transfers between devices, swap(): return lax.ppermute(array, 'zero', [(i, i ^ mask) for i in range(size)])  50.8 us
    ppermute x3, waiting for transfers between devices, from_partner(): lax.ppermute(array, 'peer', [(i, (i - by) % size) for i in range(size)])  39.1 us
    unnamed x62, local copies, waits for them, and re-layouts  15.5 us
    ppermute x14, starting transfers between devices, swap(): return lax.ppermute(array, 'zero', [(i, i ^ mask) for i in range(size)])  14.1 us
    pallas_call x2, Pallas kernels, down(): pl.pallas_call(partial(down_kernel, c), out_shape=[shape(rows, cols, dtyp...  10.3 us
    ppermute x3, starting transfers between devices, from_partner(): lax.ppermute(array, 'peer', [(i, (i - by) % size) for i in range(size)])  6.55 us
    pallas_call x2, Pallas kernels, hidden(): pl.pallas_call(hidden_kernel, out_shape=[shape(width, 2 * rows), shape(2...  6.4 us
    pallas_call x1, Pallas kernels, back(): pl.pallas_call(back_kernel, out_shape=[shape(full // 4, hidden_size)] * 4...  5.87 us
  transfers between devices with their start and end apart: 17, of which 6 were waited for; matrix products, arithmetic and copies ran while one was open for 0% of the time, Pallas kernels for 15%

profile of v1, /device:TPU:1, one launch (start us, length us, event | category | flops | bytes accessed | tf_op | source)
XLA Modules:
  0.0 163.3 jit_solution(14893369304127203305)
XLA Ops:
  0.6 1.8 %cut.1 = (bf16[256,512]{1,0:T(8,128)(2,1)S(1)}, bf16[256,512]{1,0:T(8,128)(2,1)S(1)}, bf16[256,512]{1,0:T(8,128)(2,1)S(1)}, bf16[256,512]{1,0:T(8,128)(2,1)S(1)}) custom-call(s32[1]{0:T(128)} %bitcast.11.place, f32[256,2048]{1,0:T(8,128)} %bitcast.32), custom_call_target="tpu_custom_call" | custom-call | tf_op jit(solution)/shard_map/cut/pallas_call | solution.py:68
  2.5 2.9 %norm.1 = (bf16[512,1024]{1,0:T(8,128)(2,1)S(1)}, bf16[512,640]{1,0:T(8,128)(2,1)S(1)}, bf16[512,384]{1,0:T(8,128)(2,1)S(1)}) custom-call(bf16[512,1024]{1,0:T(8,128)(2,1)S(1)} %bitcast.31, bf16[512,1024]{1,0:T(8,128)(2,1)} %bitcast.15.grads, bf16[256,512]{1,0:T(8,128)(2,1)S(1)} %get-tuple-element.254._.u0), custom_call_target="tpu_custom_call" | custom-call | tf_op jit(solution)/shard_map/norm/pallas_call | solution.py:96
  5.5 2.5 %collective-permute-start.19 = (bf16[512,1024]{1,0:T(8,128)(2,1)S(1)}, bf16[512,1024]{1,0:T(8,128)(2,1)S(1)}, u32[]{:S(2)}, u32[]{:S(2)}) collective-permute-start(bf16[512,1024]{1,0:T(8,128)(2,1)S(1)} %get-tuple-element.258.left.refs_7_.rest_0_), channel_id=1, source_target_pairs={{0,2},{1,3},{2,0},{3,1},{4,6},{5,7},{6,4},{7,5},{8,10},{9,11},{10,... | collective-permute-start | bytes 3145736 | tf_op jit(solution)/shard_map/ppermute | solution.py:33
  11.0 19.9 %collective-permute-done.19.left.refs_9_ = bf16[512,1024]{1,0:T(8,128)(2,1)S(1)} collective-permute-done((bf16[512,1024]{1,0:T(8,128)(2,1)S(1)}, bf16[512,1024]{1,0:T(8,128)(2,1)S(1)}, u32[]{:S(2)}, u32[]{:S(2)}) %collective-permute-start.19) | collective-permute-done | bytes 1048608 | tf_op jit(solution)/shard_map/ppermute | solution.py:33
  30.9 2.1 %collective-permute-start.20 = (bf16[512,1024]{1,0:T(8,128)(2,1)S(1)}, bf16[512,1024]{1,0:T(8,128)(2,1)S(1)}, u32[]{:S(2)}, u32[]{:S(2)}) collective-permute-start(bf16[512,1024]{1,0:T(8,128)(2,1)S(1)} %collective-permute-done.19.left.refs_9_), channel_id=1, source_target_pairs={{0,1},{1,0},{2,3},{3,2},{4,5},{5,4},{6,7},{7,6},{8,9},{9,8},{10,11... | collective-permute-start | bytes 3145736 | tf_op jit(solution)/shard_map/ppermute | solution.py:33
  33.0 3.5 %collective-permute-done.16.u2 = bf16[256,512]{1,0:T(8,128)(2,1)S(1)} collective-permute-done((bf16[256,512]{1,0:T(8,128)(2,1)S(1)}, bf16[256,512]{1,0:T(8,128)(2,1)S(1)}, u32[]{:S(2)}, u32[]{:S(2)}) %collective-permute-start.16) | collective-permute-done | bytes 262176 | tf_op jit(solution)/shard_map/ppermute | solution.py:33
  36.5 2.1 %collective-permute-start.25 = (bf16[512,1024]{1,0:T(8,128)(2,1)}, bf16[512,1024]{1,0:T(8,128)(2,1)S(1)}, u32[]{:S(2)}, u32[]{:S(2)}) collective-permute-start(bf16[512,1024]{1,0:T(8,128)(2,1)} %bitcast.15.grads), channel_id=1, source_target_pairs={{0,1},{1,0},{2,3},{3,2},{4,5},{5,4},{6,7},{7,6},{8,9},{9,8},{10,11... | collective-permute-start | bytes 3145736 | tf_op jit(solution)/shard_map/ppermute | solution.py:33
  38.6 18.1 %collective-permute-done.17.u3 = bf16[256,512]{1,0:T(8,128)(2,1)S(1)} collective-permute-done((bf16[256,512]{1,0:T(8,128)(2,1)S(1)}, bf16[256,512]{1,0:T(8,128)(2,1)S(1)}, u32[]{:S(2)}, u32[]{:S(2)}) %collective-permute-start.17) | collective-permute-done | bytes 262176 | tf_op jit(solution)/shard_map/ppermute | solution.py:33
  58.2 9.3 %collective-permute-done.22.refs_3_.o2 = bf16[512,384]{1,0:T(8,128)(2,1)S(1)} collective-permute-done((bf16[512,384]{1,0:T(8,128)(2,1)S(1)}, bf16[512,384]{1,0:T(8,128)(2,1)S(1)}, u32[]{:S(2)}, u32[]{:S(2)}) %collective-permute-start.22) | collective-permute-done | bytes 393248 | tf_op jit(solution)/shard_map/ppermute | solution.py:33
  68.2 3.2 %hidden.2 = (bf16[512,1024]{1,0:T(8,128)(2,1)S(1)}, f32[1024,512]{1,0:T(8,128)S(1)}) custom-call(s32[1]{0:T(128)} %bitcast.11.place, bf16[256,512]{1,0:T(8,128)(2,1)S(1)} %get-tuple-element.254._.u0, bf16[256,512]{1,0:T(8,128)(2,1)S(1)} %collective-permute-done.15.u1, bf16[256,512]{1,0:T(8,128)(2,1)S(1)} %collective-permute-done.16.u2, ...), custom_call_target="tpu_custom_call" | custom-call | tf_op jit(solution)/shard_map/hidden/pallas_call | solution.py:133
  72.4 3.2 %hidden.3 = (bf16[512,1024]{1,0:T(8,128)(2,1)S(1)}, f32[1024,512]{1,0:T(8,128)S(1)}) custom-call(s32[1]{0:T(128)} %bitcast.11.place, bf16[256,512]{1,0:T(8,128)(2,1)S(1)} %get-tuple-element.254._.u0, bf16[256,512]{1,0:T(8,128)(2,1)S(1)} %collective-permute-done.15.u1, bf16[256,512]{1,0:T(8,128)(2,1)S(1)} %collective-permute-done.16.u2, ...), custom_call_target="tpu_custom_call" | custom-call | tf_op jit(solution)/shard_map/hidden/pallas_call | solution.py:133
  76.7 5.9 %back.1 = (bf16[256,512]{1,0:T(8,128)(2,1)S(1)}, bf16[256,512]{1,0:T(8,128)(2,1)}, bf16[256,512]{1,0:T(8,128)(2,1)}, bf16[256,512]{1,0:T(8,128)(2,1)}) custom-call(s32[1]{0:T(128)} %bitcast.11.place, f32[512,1024]{1,0:T(8,128)S(1)} %bitcast.24, f32[1024,512]{1,0:T(8,128)S(1)} %get-tuple-element.259.sa, f32[1024,512]{1,0:T(8,128)S(1)} %get-tuple-element.260.sb, ...), custom_call_target="tpu_custom_call" | custom-call | tf_op jit(solution)/shard_map/back/pallas_call | solution.py:233
  83.3 1.6 collective-permute-start.26
  87.5 1.6 copy-done.4
  89.1 1.6 copy-done.6
  96.4 6.1 %down.2 = (f32[512,1024]{1,0:T(8,128)S(1)}, bf16[512,1024]{1,0:T(8,128)(2,1)S(1)}, f32[512,1024]{1,0:T(8,128)}, f32[512,1024]{1,0:T(8,128)}) custom-call(f32[2]{0:T(128)S(1)} %pad_maximum_fusion.fixes, bf16[512,1024]{1,0:T(8,128)(2,1)S(1)} %copy-done.8, bf16[512,1024]{1,0:T(8,128)(2,1)S(1)} %copy-done.11, bf16[512,640]{1,0:T(8,128)(2,1)S(1)} %copy-done.13, ...), custom_call_target="tpu_custom_call" | custom-call | tf_op jit(solution)/shard_map/down/pallas_call | solution.py:192
  102.6 4.2 %down.3 = (f32[512,1024]{1,0:T(8,128)S(1)}, bf16[512,1024]{1,0:T(8,128)(2,1)S(1)}, f32[512,1024]{1,0:T(8,128)}, f32[512,1024]{1,0:T(8,128)}) custom-call(f32[2]{0:T(128)S(1)} %pad_maximum_fusion.fixes, bf16[512,1024]{1,0:T(8,128)(2,1)S(1)} %copy-done.9, ...), custom_call_target="tpu_custom_call", output_to_operand_aliasing={{0}: (11, {}), {1}: (12, {}), {2}: (13, {}), {3}: (14, {})} | custom-call | tf_op jit(solution)/shard_map/down/pallas_call | solution.py:192
  106.9 2.8 %up.11 = (f32[512,512]{1,0:T(8,128)S(1)}, bf16[512,512]{1,0:T(8,128)(2,1)S(1)}, f32[256,2048]{1,0:T(8,128)S(1)}, f32[256,2048]{1,0:T(8,128)S(1)}) custom-call(s32[1]{0:T(128)} %bitcast.11.place, f32[2]{0:T(128)S(1)} %pad_maximum_fusion.fixes, bf16[256,512]{1,0:T(8,128)(2,1)S(1)} %copy-done.23, bf16[256,512]{1,0:T(8,128)(2,1)} %collective-permute-done.28.right, ...), custom_call_target="tpu_custom_call" | custom-call | tf_op jit(solution)/shard_map/up/pallas_call | solution.py:295
  109.6 51.0 %conditional.1 = (f32[256,2048]{1,0:T(8,128)S(1)}, f32[256,2048]{1,0:T(8,128)S(1)}, f32[1,256,2048]{2,1,0:T(8,128)}, f32[1,512,1024]{2,1,0:T(8,128)S(1)}) conditional(s32[]{:T(128)} %clamp.3, (s32[1]{0:T(128)}, f32[2]{0:T(128)S(1)}, bf16[256,512]{1,0:T(8,128)(2,1)}, bf16[256,512]{1,0:T(8,128)(2,1)}, ...), branch_computations={%region_0.1_spmd, %region_1.2_spmd, %region_2.3_spmd, %region_3.4_... | conditional | bytes 8388760 | solution.py:424
  109.7 3.5 %collective-permute-start.14 = (bf16[512,1024]{1,0:T(8,128)(2,1)S(1)}, bf16[512,1024]{1,0:T(8,128)(2,1)S(1)}, u32[]{:S(2)}, u32[]{:S(2)}) collective-permute-start(bf16[512,1024]{1,0:T(8,128)(2,1)S(1)} %get-tuple-element.216), channel_id=1, source_target_pairs={{0,64},{4,68},{8,72},{12,76},{16,80},{20,84},{24,88},{28,92},{32,9... | collective-permute-start | bytes 3145736 | tf_op jit(solution)/shard_map/cond/branch_4_fun/ppermute | solution.py:38
  113.3 2.8 %up.10 = (f32[512,512]{1,0:T(8,128)S(1)}, bf16[512,512]{1,0:T(8,128)(2,1)S(1)}, f32[256,2048]{1,0:T(8,128)S(1)}, f32[256,2048]{1,0:T(8,128)S(1)}) custom-call(s32[1]{0:T(128)} %get-tuple-element.200.place, f32[2]{0:T(128)S(1)} %get-tuple-element.201.fixes, bf16[256,512]{1,0:T(8,128)(2,1)} %get-tuple-element.202.left, ...), custom_call_target="tpu_custom_call", output_to_operand_aliasing={{2}: (7, {}), {3}: (8, {})} | custom-call | tf_op jit(solution)/shard_map/cond/branch_4_fun/up/pallas_call | solution.py:295
  116.1 3.0 %collective-permute-start.12 = (bf16[512,512]{1,0:T(8,128)(2,1)S(1)}, bf16[512,512]{1,0:T(8,128)(2,1)S(1)}, u32[]{:S(2)}, u32[]{:S(2)}) collective-permute-start(bf16[512,512]{1,0:T(8,128)(2,1)S(1)} %get-tuple-element.212), channel_id=1, source_target_pairs={{0,64},{4,68},{8,72},{12,76},{16,80},{20,84},{24,88},{28,92},{32,9... | collective-permute-start | bytes 1572872 | tf_op jit(solution)/shard_map/cond/branch_4_fun/ppermute | solution.py:38
  119.1 28.9 %collective-permute-done.13.other = bf16[512,512]{1,0:T(8,128)(2,1)S(1)} collective-permute-done((bf16[512,512]{1,0:T(8,128)(2,1)S(1)}, bf16[512,512]{1,0:T(8,128)(2,1)S(1)}, u32[]{:S(2)}, u32[]{:S(2)}) %collective-permute-start.13) | collective-permute-done | bytes 524320 | tf_op jit(solution)/shard_map/cond/branch_4_fun/ppermute | solution.py:38
  149.0 10.2 %collective-permute-done.12.other = bf16[512,512]{1,0:T(8,128)(2,1)S(1)} collective-permute-done((bf16[512,512]{1,0:T(8,128)(2,1)S(1)}, bf16[512,512]{1,0:T(8,128)(2,1)S(1)}, u32[]{:S(2)}, u32[]{:S(2)}) %collective-permute-start.12) | collective-permute-done | bytes 524320 | tf_op jit(solution)/shard_map/cond/branch_4_fun/ppermute | solution.py:38
  (86 shorter events, 20.8 us)
Async XLA Ops:
  5.4 71.2 %copy-start.12 = (bf16[512,640]{1,0:T(8,128)(2,1)}, bf16[512,640]{1,0:T(8,128)(2,1)S(1)}, u32[]{:S(2)}) copy-start(bf16[512,640]{1,0:T(8,128)(2,1)S(1)} %get-tuple-element.261.refs_0_.o0) | copy-start | bytes 1966084
  5.5 25.4 %collective-permute-start.19 = (bf16[512,1024]{1,0:T(8,128)(2,1)S(1)}, bf16[512,1024]{1,0:T(8,128)(2,1)S(1)}, u32[]{:S(2)}, u32[]{:S(2)}) collective-permute-start(bf16[512,1024]{1,0:T(8,128)(2,1)S(1)} %get-tuple-element.258.left.refs_7_.rest_0_), channel_id=1, source_target_pairs={{0,2},{1,3},{2,0},{3,1},{4,6},{5,7},{6,4},{7,5},{8,10},{9,11},{10,... | collective-permute-start | bytes 3145736 | tf_op jit(solution)/shard_map/ppermute | solution.py:33
  8.0 3.0 %collective-permute-start.15 = (bf16[256,512]{1,0:T(8,128)(2,1)S(1)}, bf16[256,512]{1,0:T(8,128)(2,1)S(1)}, u32[]{:S(2)}, u32[]{:S(2)}) collective-permute-start(bf16[256,512]{1,0:T(8,128)(2,1)S(1)} %get-tuple-element.255), channel_id=1, source_target_pairs={{0,1},{1,0},{2,3},{3,2},{4,5},{5,4},{6,7},{7,6},{8,9},{9,8},{10,11... | collective-permute-start | bytes 786440 | tf_op jit(solution)/shard_map/ppermute | solution.py:33
  8.9 27.5 %collective-permute-start.16 = (bf16[256,512]{1,0:T(8,128)(2,1)S(1)}, bf16[256,512]{1,0:T(8,128)(2,1)S(1)}, u32[]{:S(2)}, u32[]{:S(2)}) collective-permute-start(bf16[256,512]{1,0:T(8,128)(2,1)S(1)} %get-tuple-element.256), channel_id=1, source_target_pairs={{0,2},{1,3},{2,0},{3,1},{4,6},{5,7},{6,4},{7,5},{8,10},{9,11},{10,... | collective-permute-start | bytes 786440 | tf_op jit(solution)/shard_map/ppermute | solution.py:33
  8.9 49.2 %collective-permute-start.21 = (bf16[512,640]{1,0:T(8,128)(2,1)S(1)}, bf16[512,640]{1,0:T(8,128)(2,1)S(1)}, u32[]{:S(2)}, u32[]{:S(2)}) collective-permute-start(bf16[512,640]{1,0:T(8,128)(2,1)S(1)} %get-tuple-element.261.refs_0_.o0), channel_id=1, source_target_pairs={{0,2},{1,3},{2,0},{3,1},{4,6},{5,7},{6,4},{7,5},{8,10},{9,11},{10,... | collective-permute-start | bytes 1966088 | tf_op jit(solution)/shard_map/ppermute | solution.py:33
  10.4 57.8 %collective-permute-start.18 = (bf16[512,1024]{1,0:T(8,128)(2,1)S(1)}, bf16[512,1024]{1,0:T(8,128)(2,1)S(1)}, u32[]{:S(2)}, u32[]{:S(2)}) collective-permute-start(bf16[512,1024]{1,0:T(8,128)(2,1)S(1)} %get-tuple-element.258.left.refs_7_.rest_0_), channel_id=1, source_target_pairs={{0,1},{1,0},{2,3},{3,2},{4,5},{5,4},{6,7},{7,6},{8,9},{9,8},{10,11... | collective-permute-start | bytes 3145736 | tf_op jit(solution)/shard_map/ppermute | solution.py:33
  11.0 45.7 %collective-permute-start.17 = (bf16[256,512]{1,0:T(8,128)(2,1)S(1)}, bf16[256,512]{1,0:T(8,128)(2,1)S(1)}, u32[]{:S(2)}, u32[]{:S(2)}) collective-permute-start(bf16[256,512]{1,0:T(8,128)(2,1)S(1)} %get-tuple-element.257), channel_id=1, source_target_pairs={{0,3},{1,2},{2,1},{3,0},{4,7},{5,6},{6,5},{7,4},{8,11},{9,10},{10,... | collective-permute-start | bytes 786440 | tf_op jit(solution)/shard_map/ppermute | solution.py:33
  30.9 41.6 %collective-permute-start.20 = (bf16[512,1024]{1,0:T(8,128)(2,1)S(1)}, bf16[512,1024]{1,0:T(8,128)(2,1)S(1)}, u32[]{:S(2)}, u32[]{:S(2)}) collective-permute-start(bf16[512,1024]{1,0:T(8,128)(2,1)S(1)} %collective-permute-done.19.left.refs_9_), channel_id=1, source_target_pairs={{0,1},{1,0},{2,3},{3,2},{4,5},{5,4},{6,7},{7,6},{8,9},{9,8},{10,11... | collective-permute-start | bytes 3145736 | tf_op jit(solution)/shard_map/ppermute | solution.py:33
  36.5 40.1 %collective-permute-start.25 = (bf16[512,1024]{1,0:T(8,128)(2,1)}, bf16[512,1024]{1,0:T(8,128)(2,1)S(1)}, u32[]{:S(2)}, u32[]{:S(2)}) collective-permute-start(bf16[512,1024]{1,0:T(8,128)(2,1)} %bitcast.15.grads), channel_id=1, source_target_pairs={{0,1},{1,0},{2,3},{3,2},{4,5},{5,4},{6,7},{7,6},{8,9},{9,8},{10,11... | collective-permute-start | bytes 3145736 | tf_op jit(solution)/shard_map/ppermute | solution.py:33
  56.7 10.7 %collective-permute-start.22 = (bf16[512,384]{1,0:T(8,128)(2,1)S(1)}, bf16[512,384]{1,0:T(8,128)(2,1)S(1)}, u32[]{:S(2)}, u32[]{:S(2)}) collective-permute-start(bf16[512,384]{1,0:T(8,128)(2,1)S(1)} %get-tuple-element.262.refs_1_.o0), channel_id=1, source_target_pairs={{0,2},{1,3},{2,0},{3,1},{4,6},{5,7},{6,4},{7,5},{8,10},{9,11},{10,... | collective-permute-start | bytes 1179656 | tf_op jit(solution)/shard_map/ppermute | solution.py:33
  58.2 18.5 %copy-start.14 = (bf16[512,640]{1,0:T(8,128)(2,1)}, bf16[512,640]{1,0:T(8,128)(2,1)S(1)}, u32[]{:S(2)}) copy-start(bf16[512,640]{1,0:T(8,128)(2,1)S(1)} %collective-permute-done.21.refs_2_.o2) | copy-start | bytes 1966084
  58.2 18.5 %collective-permute-start.23 = (bf16[512,640]{1,0:T(8,128)(2,1)S(1)}, bf16[512,640]{1,0:T(8,128)(2,1)S(1)}, u32[]{:S(2)}, u32[]{:S(2)}) collective-permute-start(bf16[512,640]{1,0:T(8,128)(2,1)S(1)} %collective-permute-done.21.refs_2_.o2), channel_id=1, source_target_pairs={{0,1},{1,0},{2,3},{3,2},{4,5},{5,4},{6,7},{7,6},{8,9},{9,8},{10,11... | collective-permute-start | bytes 1966088 | tf_op jit(solution)/shard_map/ppermute | solution.py:33
  67.4 9.2 %copy-start.18 = (bf16[512,384]{1,0:T(8,128)(2,1)}, bf16[512,384]{1,0:T(8,128)(2,1)S(1)}, u32[]{:S(2)}) copy-start(bf16[512,384]{1,0:T(8,128)(2,1)S(1)} %collective-permute-done.22.refs_3_.o2) | copy-start | bytes 1179652
  67.4 9.2 %collective-permute-start.24 = (bf16[512,384]{1,0:T(8,128)(2,1)S(1)}, bf16[512,384]{1,0:T(8,128)(2,1)S(1)}, u32[]{:S(2)}, u32[]{:S(2)}) collective-permute-start(bf16[512,384]{1,0:T(8,128)(2,1)S(1)} %collective-permute-done.22.refs_3_.o2), channel_id=1, source_target_pairs={{0,1},{1,0},{2,3},{3,2},{4,5},{5,4},{6,7},{7,6},{8,9},{9,8},{10,11... | collective-permute-start | bytes 1179656 | tf_op jit(solution)/shard_map/ppermute | solution.py:33
  83.3 23.5 %collective-permute-start.28 = (bf16[256,512]{1,0:T(8,128)(2,1)}, bf16[256,512]{1,0:T(8,128)(2,1)}, u32[]{:S(2)}, u32[]{:S(2)}) collective-permute-start(bf16[256,512]{1,0:T(8,128)(2,1)} %get-tuple-element.266), channel_id=1, source_target_pairs={{0,1},{1,0},{2,3},{3,2},{4,5},{5,4},{6,7},{7,6},{8,9},{9,8},{10,11... | collective-permute-start | bytes 786440 | tf_op jit(solution)/shard_map/ppermute | solution.py:33
  83.3 26.4 %collective-permute-start.26 = (bf16[256,512]{1,0:T(8,128)(2,1)}, bf16[256,512]{1,0:T(8,128)(2,1)}, u32[]{:S(2)}, u32[]{:S(2)}) collective-permute-start(bf16[256,512]{1,0:T(8,128)(2,1)} %get-tuple-element.263), channel_id=1, source_target_pairs={{0,2},{1,3},{2,0},{3,1},{4,6},{5,7},{6,4},{7,5},{8,10},{9,11},{10,... | collective-permute-start | bytes 786440 | tf_op jit(solution)/shard_map/ppermute | solution.py:33
  84.8 24.8 %collective-permute-start.27 = (bf16[256,512]{1,0:T(8,128)(2,1)}, bf16[256,512]{1,0:T(8,128)(2,1)}, u32[]{:S(2)}, u32[]{:S(2)}) collective-permute-start(bf16[256,512]{1,0:T(8,128)(2,1)} %get-tuple-element.264), channel_id=1, source_target_pairs={{0,3},{1,2},{2,1},{3,0},{4,7},{5,6},{6,5},{7,4},{8,11},{9,10},{10,... | collective-permute-start | bytes 786440 | tf_op jit(solution)/shard_map/ppermute | solution.py:33
  96.4 6.1 %copy-start.9 = (bf16[512,1024]{1,0:T(8,128)(2,1)S(1)}, bf16[512,1024]{1,0:T(8,128)(2,1)}, u32[]{:S(2)}) copy-start(bf16[512,1024]{1,0:T(8,128)(2,1)} %copy-done.7) | copy-start | bytes 3145732
  96.4 6.1 %copy-start.19 = (bf16[512,384]{1,0:T(8,128)(2,1)S(1)}, bf16[512,384]{1,0:T(8,128)(2,1)}, u32[]{:S(2)}) copy-start(bf16[512,384]{1,0:T(8,128)(2,1)} %copy-done.18) | copy-start | bytes 1179652
  96.4 6.1 %copy-start.21 = (bf16[512,384]{1,0:T(8,128)(2,1)S(1)}, bf16[512,384]{1,0:T(8,128)(2,1)}, u32[]{:S(2)}) copy-start(bf16[512,384]{1,0:T(8,128)(2,1)} %copy-done.20) | copy-start | bytes 1179652
  96.4 6.1 %copy-start.23 = (bf16[256,512]{1,0:T(8,128)(2,1)S(1)}, bf16[256,512]{1,0:T(8,128)(2,1)}, u32[]{:S(2)}) copy-start(bf16[256,512]{1,0:T(8,128)(2,1)} %copy-done.22) | copy-start | bytes 786436
  109.7 50.6 %collective-permute-start.14 = (bf16[512,1024]{1,0:T(8,128)(2,1)S(1)}, bf16[512,1024]{1,0:T(8,128)(2,1)S(1)}, u32[]{:S(2)}, u32[]{:S(2)}) collective-permute-start(bf16[512,1024]{1,0:T(8,128)(2,1)S(1)} %get-tuple-element.216), channel_id=1, source_target_pairs={{0,64},{4,68},{8,72},{12,76},{16,80},{20,84},{24,88},{28,92},{32,9... | collective-permute-start | bytes 3145736 | tf_op jit(solution)/shard_map/cond/branch_4_fun/ppermute | solution.py:38
  113.2 34.8 %collective-permute-start.13 = (bf16[512,512]{1,0:T(8,128)(2,1)S(1)}, bf16[512,512]{1,0:T(8,128)(2,1)S(1)}, u32[]{:S(2)}, u32[]{:S(2)}) collective-permute-start(bf16[512,512]{1,0:T(8,128)(2,1)S(1)} %get-tuple-element.214), channel_id=1, source_target_pairs={{0,64},{4,68},{8,72},{12,76},{16,80},{20,84},{24,88},{28,92},{32,9... | collective-permute-start | bytes 1572872 | tf_op jit(solution)/shard_map/cond/branch_4_fun/ppermute | solution.py:38
  116.1 43.1 %collective-permute-start.12 = (bf16[512,512]{1,0:T(8,128)(2,1)S(1)}, bf16[512,512]{1,0:T(8,128)(2,1)S(1)}, u32[]{:S(2)}, u32[]{:S(2)}) collective-permute-start(bf16[512,512]{1,0:T(8,128)(2,1)S(1)} %get-tuple-element.212), channel_id=1, source_target_pairs={{0,64},{4,68},{8,72},{12,76},{16,80},{20,84},{24,88},{28,92},{32,9... | collective-permute-start | bytes 1572872 | tf_op jit(solution)/shard_map/cond/branch_4_fun/ppermute | solution.py:38
  (24 other events, 67.8 us)

commit v2 on v1

--- a/solution.py
+++ b/solution.py
@@ -8,7 +8,7 @@
 from jax.sharding import PartitionSpec as P
 
 
-WIDTHS = (640, 384)
+WIDTHS = (512, 512)
 STARTS = tuple(sum(WIDTHS[:c]) for c in range(len(WIDTHS)))
 CHUNKS = len(WIDTHS)
 LOW = jnp.bfloat16
@@ -50,7 +50,8 @@
     return local, first_new, second_new
 
 
-def cut_kernel(place, up, *outs):
+def cut_kernel(place, up, *refs):
+    outs = refs[-4:]
     step = 32
     width = outs[0].shape[1]
 
@@ -64,15 +65,15 @@
     lax.fori_loop(0, up.shape[0] // step, rows, 0)
 
 
-def cut(place, up):
+def cut(place, up, *after):
     return pl.pallas_call(
         cut_kernel,
         out_shape=[shape(up.shape[0], up.shape[1] // 4)] * 4,
-        in_specs=[SMEM, VMEM],
+        in_specs=[SMEM, VMEM] + [ANY] * len(after),
         out_specs=[VMEM] * 4,
         compiler_params=params(),
         name="cut",
-    )(place, up)
+    )(place, up, *after)
 
 
 def norm_kernel(tokens, grads, _, normed, *pieces):
@@ -323,7 +324,7 @@
         out_shape=shape(rows, cols, dtype=WIDE),
         in_specs=[block] * 2,
         out_specs=block,
-        compiler_params=params(),
+        compiler_params=params(60 * 2**20),
         name="mean_down",
     )(local, other)
 
@@ -362,8 +363,8 @@
     )(*ins)
 
 
-def prepare(place, fixes, tokens, grads, up_p, down_p, up_m, down_m, up_v, down_v):
-    first = cut(place, up_p)
+def prepare(place, fixes, level, tokens, grads, up_p, down_p, up_m, down_m, up_v, down_v):
+    first = cut(place, up_p, fixes, level)
     ups = [first[0]]
     for k in range(1, 4):
         ups.append(swap(first[k], k))
@@ -416,13 +417,14 @@
     fixes = jnp.stack(
         [1.0 - jnp.power(WIDE(0.9), count), 1.0 - jnp.power(WIDE(0.999), count)]
     )
-    made = prepare(place, fixes, tokens[0], out_grad[0], *state)
+    level = step % levels
+    made = prepare(place, fixes, level, tokens[0], out_grad[0], *state)
 
     def branch(k, *args):
         return finish(k, *args)
 
     outs = lax.switch(
-        step[0] % levels,
+        level[0],
         [partial(branch, k) for k in range(levels)],
         place,
         fixes,

time: 164 us -> 150 us (0.915)
  local copies, waits for them, and re-layouts: 15.5 us -> 1.02 us
  waiting for transfers between devices: 89.9 us -> 84.4 us
  starting transfers between devices: 20.7 us -> 23.6 us
  Pallas kernels: 35.4 us -> 38.2 us
    unnamed x62 -> x16, local copies, waits for them, and re-layouts: 15.5 us -> 0.05 us
    ppermute x14, waiting for transfers between devices: 50.8 us -> 45.5 us  [swap(): return lax.ppermute(array, 'zero', [(i, i ^ mask) for i in range(size)])]
    pallas_call x1, Pallas kernels: 0.34 us -> 5.43 us  [mean_down(): pl.pallas_call(mean_down_kernel, grid=(8,), out_shape=shape(rows, cols, d...]
    ppermute x14, starting transfers between devices: 14.1 us -> 17.1 us  [swap(): return lax.ppermute(array, 'zero', [(i, i ^ mask) for i in range(size)])]
  transfers between devices with their start and end apart: 17 -> 17, of which waited for: 6 -> 6; matrix products, arithmetic and copies ran while one was open for 0% -> 0% of each run, Pallas kernels for 15% -> 17%
where the time goes in v2:
time: 150 us; the launch traced here: 149 us
  waiting for transfers between devices  84.4 us (56%)
  Pallas kernels  38.2 us (25%)
  starting transfers between devices  23.6 us (16%)
  between operations  1.77 us (1%)
    ppermute x14, waiting for transfers between devices, swap(): return lax.ppermute(array, 'zero', [(i, i ^ mask) for i in range(size)])  45.5 us
    ppermute x3, waiting for transfers between devices, from_partner(): lax.ppermute(array, 'peer', [(i, (i - by) % size) for i in range(size)])  38.9 us
    ppermute x14, starting transfers between devices, swap(): return lax.ppermute(array, 'zero', [(i, i ^ mask) for i in range(size)])  17.1 us
    pallas_call x2, Pallas kernels, down(): pl.pallas_call(partial(down_kernel, c), out_shape=[shape(rows, cols, dtyp...  10.2 us
    ppermute x3, starting transfers between devices, from_partner(): lax.ppermute(array, 'peer', [(i, (i - by) % size) for i in range(size)])  6.55 us
    pallas_call x2, Pallas kernels, hidden(): pl.pallas_call(hidden_kernel, out_shape=[shape(width, 2 * rows), shape(2...  6.4 us
    pallas_call x2, Pallas kernels, up(): pl.pallas_call(partial(up_kernel, base), in_specs=in_specs, out_specs=[VM...  6.12 us
    pallas_call x1, Pallas kernels, mean_down(): pl.pallas_call(mean_down_kernel, grid=(8,), out_shape=shape(rows, cols, d...  5.43 us
  transfers between devices with their start and end apart: 17, of which 6 were waited for; matrix products, arithmetic and copies ran while one was open for 0% of the time, Pallas kernels for 17%

profile of v2, /device:TPU:1, one launch (start us, length us, event | category | flops | bytes accessed | tf_op | source)
XLA Modules:
  0.0 149.4 jit_solution(10019530382473114189)
XLA Ops:
  1.6 1.7 %cut.1 = (bf16[256,512]{1,0:T(8,128)(2,1)S(1)}, bf16[256,512]{1,0:T(8,128)(2,1)S(1)}, bf16[256,512]{1,0:T(8,128)(2,1)S(1)}, bf16[256,512]{1,0:T(8,128)(2,1)S(1)}) custom-call(s32[1]{0:T(128)} %bitcast.11.place, f32[256,2048]{1,0:T(8,128)} %bitcast.34, f32[2]{0:T(128)S(1)} %pad_maximum_fusion.refs_0_.fixes, s32[1]{0:T(128)S(6)} %select_n.7.refs_1_), custom_call_target="tpu_custom_call" | custom-call | tf_op jit(solution)/shard_map/cut/pallas_call | solution.py:69
  3.4 1.7 %norm.1 = (bf16[512,1024]{1,0:T(8,128)(2,1)S(1)}, bf16[512,512]{1,0:T(8,128)(2,1)S(1)}, bf16[512,512]{1,0:T(8,128)(2,1)S(1)}) custom-call(bf16[512,1024]{1,0:T(8,128)(2,1)S(1)} %bitcast.31, bf16[512,1024]{1,0:T(8,128)(2,1)S(1)} %bitcast.32, bf16[256,512]{1,0:T(8,128)(2,1)S(1)} %get-tuple-element.254._.u0), custom_call_target="tpu_custom_call" | custom-call | tf_op jit(solution)/shard_map/norm/pallas_call | solution.py:97
  5.1 2.5 %collective-permute-start.19 = (bf16[512,1024]{1,0:T(8,128)(2,1)S(1)}, bf16[512,1024]{1,0:T(8,128)(2,1)S(1)}, u32[]{:S(2)}, u32[]{:S(2)}) collective-permute-start(bf16[512,1024]{1,0:T(8,128)(2,1)S(1)} %get-tuple-element.258.left.refs_7_.rest_0_), channel_id=1, source_target_pairs={{0,2},{1,3},{2,0},{3,1},{4,6},{5,7},{6,4},{7,5},{8,10},{9,11},{10,... | collective-permute-start | bytes 3145736 | tf_op jit(solution)/shard_map/ppermute | solution.py:33
  8.6 1.6 %collective-permute-start.17 = (bf16[256,512]{1,0:T(8,128)(2,1)S(1)}, bf16[256,512]{1,0:T(8,128)(2,1)S(1)}, u32[]{:S(2)}, u32[]{:S(2)}) collective-permute-start(bf16[256,512]{1,0:T(8,128)(2,1)S(1)} %get-tuple-element.257), channel_id=1, source_target_pairs={{0,3},{1,2},{2,1},{3,0},{4,7},{5,6},{6,5},{7,4},{8,11},{9,10},{10,... | collective-permute-start | bytes 786440 | tf_op jit(solution)/shard_map/ppermute | solution.py:33
  10.7 25.4 %collective-permute-done.16.u2 = bf16[256,512]{1,0:T(8,128)(2,1)S(1)} collective-permute-done((bf16[256,512]{1,0:T(8,128)(2,1)S(1)}, bf16[256,512]{1,0:T(8,128)(2,1)S(1)}, u32[]{:S(2)}, u32[]{:S(2)}) %collective-permute-start.16) | collective-permute-done | bytes 262176 | tf_op jit(solution)/shard_map/ppermute | solution.py:33
  37.3 2.9 %collective-permute-start.20 = (bf16[512,1024]{1,0:T(8,128)(2,1)S(1)}, bf16[512,1024]{1,0:T(8,128)(2,1)S(1)}, u32[]{:S(2)}, u32[]{:S(2)}) collective-permute-start(bf16[512,1024]{1,0:T(8,128)(2,1)S(1)} %collective-permute-done.19.left.refs_9_), channel_id=1, source_target_pairs={{0,1},{1,0},{2,3},{3,2},{4,5},{5,4},{6,7},{7,6},{8,9},{9,8},{10,11... | collective-permute-start | bytes 3145736 | tf_op jit(solution)/shard_map/ppermute | solution.py:33
  40.2 2.9 %collective-permute-done.17.u3 = bf16[256,512]{1,0:T(8,128)(2,1)S(1)} collective-permute-done((bf16[256,512]{1,0:T(8,128)(2,1)S(1)}, bf16[256,512]{1,0:T(8,128)(2,1)S(1)}, u32[]{:S(2)}, u32[]{:S(2)}) %collective-permute-start.17) | collective-permute-done | bytes 262176 | tf_op jit(solution)/shard_map/ppermute | solution.py:33
  43.1 1.7 %collective-permute-start.22 = (bf16[512,512]{1,0:T(8,128)(2,1)S(1)}, bf16[512,512]{1,0:T(8,128)(2,1)S(1)}, u32[]{:S(2)}, u32[]{:S(2)}) collective-permute-start(bf16[512,512]{1,0:T(8,128)(2,1)S(1)} %get-tuple-element.262.refs_1_.o0), channel_id=1, source_target_pairs={{0,2},{1,3},{2,0},{3,1},{4,6},{5,7},{6,4},{7,5},{8,10},{9,11},{10,... | collective-permute-start | bytes 1572872 | tf_op jit(solution)/shard_map/ppermute | solution.py:33
  44.9 8.1 %collective-permute-done.21.refs_2_.o2 = bf16[512,512]{1,0:T(8,128)(2,1)S(1)} collective-permute-done((bf16[512,512]{1,0:T(8,128)(2,1)S(1)}, bf16[512,512]{1,0:T(8,128)(2,1)S(1)}, u32[]{:S(2)}, u32[]{:S(2)}) %collective-permute-start.21) | collective-permute-done | bytes 524320 | tf_op jit(solution)/shard_map/ppermute | solution.py:33
  53.0 2.1 %collective-permute-start.23 = (bf16[512,512]{1,0:T(8,128)(2,1)S(1)}, bf16[512,512]{1,0:T(8,128)(2,1)S(1)}, u32[]{:S(2)}, u32[]{:S(2)}) collective-permute-start(bf16[512,512]{1,0:T(8,128)(2,1)S(1)} %collective-permute-done.21.refs_2_.o2), channel_id=1, source_target_pairs={{0,1},{1,0},{2,3},{3,2},{4,5},{5,4},{6,7},{7,6},{8,9},{9,8},{10,11... | collective-permute-start | bytes 1572872 | tf_op jit(solution)/shard_map/ppermute | solution.py:33
  55.1 9.1 %collective-permute-done.22.refs_3_.o2 = bf16[512,512]{1,0:T(8,128)(2,1)S(1)} collective-permute-done((bf16[512,512]{1,0:T(8,128)(2,1)S(1)}, bf16[512,512]{1,0:T(8,128)(2,1)S(1)}, u32[]{:S(2)}, u32[]{:S(2)}) %collective-permute-start.22) | collective-permute-done | bytes 524320 | tf_op jit(solution)/shard_map/ppermute | solution.py:33
  65.5 3.2 %hidden.2 = (bf16[512,1024]{1,0:T(8,128)(2,1)S(1)}, f32[1024,512]{1,0:T(8,128)S(1)}) custom-call(s32[1]{0:T(128)} %bitcast.11.place, bf16[256,512]{1,0:T(8,128)(2,1)S(1)} %get-tuple-element.254._.u0, bf16[256,512]{1,0:T(8,128)(2,1)S(1)} %collective-permute-done.15.u1, bf16[256,512]{1,0:T(8,128)(2,1)S(1)} %collective-permute-done.16.u2, ...), custom_call_target="tpu_custom_call" | custom-call | tf_op jit(solution)/shard_map/hidden/pallas_call | solution.py:134
  68.7 3.2 %hidden.3 = (bf16[512,1024]{1,0:T(8,128)(2,1)S(1)}, f32[1024,512]{1,0:T(8,128)S(1)}) custom-call(s32[1]{0:T(128)} %bitcast.11.place, bf16[256,512]{1,0:T(8,128)(2,1)S(1)} %get-tuple-element.254._.u0, bf16[256,512]{1,0:T(8,128)(2,1)S(1)} %collective-permute-done.15.u1, bf16[256,512]{1,0:T(8,128)(2,1)S(1)} %collective-permute-done.16.u2, ...), custom_call_target="tpu_custom_call" | custom-call | tf_op jit(solution)/shard_map/hidden/pallas_call | solution.py:134
  72.0 4.6 %back.1 = (bf16[256,512]{1,0:T(8,128)(2,1)S(1)}, bf16[256,512]{1,0:T(8,128)(2,1)S(1)}, bf16[256,512]{1,0:T(8,128)(2,1)S(1)}, bf16[256,512]{1,0:T(8,128)(2,1)S(1)}) custom-call(s32[1]{0:T(128)} %bitcast.11.place, f32[512,1024]{1,0:T(8,128)S(1)} %bitcast.24, f32[1024,512]{1,0:T(8,128)S(1)} %get-tuple-element.259.sa, f32[1024,512]{1,0:T(8,128)S(1)} %get-tuple-element.260.sb, ...), custom_call_target="tpu_custom_call" | custom-call | tf_op jit(solution)/shard_map/back/pallas_call | solution.py:234
  78.8 5.1 %down.2 = (f32[512,1024]{1,0:T(8,128)}, bf16[512,1024]{1,0:T(8,128)(2,1)S(1)}, f32[512,1024]{1,0:T(8,128)}, f32[512,1024]{1,0:T(8,128)}) custom-call(f32[2]{0:T(128)S(1)} %pad_maximum_fusion.refs_0_.fixes, bf16[512,1024]{1,0:T(8,128)(2,1)S(1)} %get-tuple-element.271.near, bf16[512,1024]{1,0:T(8,128)(2,1)S(1)} %get-tuple-element.272.far, ...), custom_call_target="tpu_custom_call" | custom-call | tf_op jit(solution)/shard_map/down/pallas_call | solution.py:193
  83.9 5.1 %down.3 = (f32[512,1024]{1,0:T(8,128)}, bf16[512,1024]{1,0:T(8,128)(2,1)S(1)}, f32[512,1024]{1,0:T(8,128)}, f32[512,1024]{1,0:T(8,128)}) custom-call(f32[2]{0:T(128)S(1)} %pad_maximum_fusion.refs_0_.fixes, bf16[512,1024]{1,0:T(8,128)(2,1)S(1)} %get-tuple-element.271.near, ...), custom_call_target="tpu_custom_call", output_to_operand_aliasing={{0}: (11, {}), {1}: (12, {}), {2}: (13, {}), {3}: (14, {})} | custom-call | tf_op jit(solution)/shard_map/down/pallas_call | solution.py:193
  89.1 3.1 %up.11 = (f32[512,512]{1,0:T(8,128)S(1)}, bf16[512,512]{1,0:T(8,128)(2,1)S(1)}, f32[256,2048]{1,0:T(8,128)}, f32[256,2048]{1,0:T(8,128)}) custom-call(s32[1]{0:T(128)} %bitcast.11.place, f32[2]{0:T(128)S(1)} %pad_maximum_fusion.refs_0_.fixes, bf16[256,512]{1,0:T(8,128)(2,1)S(1)} %get-tuple-element.265.left.rest_0_, ...), custom_call_target="tpu_custom_call" | custom-call | tf_op jit(solution)/shard_map/up/pallas_call | solution.py:296
  92.2 57.2 %conditional.1 = (f32[256,2048]{1,0:T(8,128)}, f32[256,2048]{1,0:T(8,128)}, f32[1,256,2048]{2,1,0:T(8,128)}, f32[1,512,1024]{2,1,0:T(8,128)}) conditional(s32[]{:T(128)} %bitcast.10, (s32[1]{0:T(128)}, f32[2]{0:T(128)S(1)}, bf16[256,512]{1,0:T(8,128)(2,1)S(1)}, bf16[256,512]{1,0:T(8,128)(2,1)S(1)}, ...), branch_computations={%region_0.1_spmd, %region_1.2_spmd, %region_2.3_spmd, %region_3.4_... | conditional | bytes 20971728 | solution.py:426
  92.4 3.5 %collective-permute-start.14 = (bf16[512,1024]{1,0:T(8,128)(2,1)S(1)}, bf16[512,1024]{1,0:T(8,128)(2,1)S(1)}, u32[]{:S(2)}, u32[]{:S(2)}) collective-permute-start(bf16[512,1024]{1,0:T(8,128)(2,1)S(1)} %get-tuple-element.216), channel_id=1, source_target_pairs={{0,64},{4,68},{8,72},{12,76},{16,80},{20,84},{24,88},{28,92},{32,9... | collective-permute-start | bytes 3145736 | tf_op jit(solution)/shard_map/cond/branch_4_fun/ppermute | solution.py:38
  96.0 3.1 %up.10 = (f32[512,512]{1,0:T(8,128)S(1)}, bf16[512,512]{1,0:T(8,128)(2,1)S(1)}, f32[256,2048]{1,0:T(8,128)}, f32[256,2048]{1,0:T(8,128)}) custom-call(s32[1]{0:T(128)} %get-tuple-element.200.place, f32[2]{0:T(128)S(1)} %get-tuple-element.201.fixes, bf16[256,512]{1,0:T(8,128)(2,1)S(1)} %get-tuple-element.202.left, ...), custom_call_target="tpu_custom_call", output_to_operand_aliasing={{2}: (7, {}), {3}: (8, {})} | custom-call | tf_op jit(solution)/shard_map/cond/branch_4_fun/up/pallas_call | solution.py:296
  99.0 3.0 %collective-permute-start.12 = (bf16[512,512]{1,0:T(8,128)(2,1)S(1)}, bf16[512,512]{1,0:T(8,128)(2,1)S(1)}, u32[]{:S(2)}, u32[]{:S(2)}) collective-permute-start(bf16[512,512]{1,0:T(8,128)(2,1)S(1)} %get-tuple-element.212), channel_id=1, source_target_pairs={{0,64},{4,68},{8,72},{12,76},{16,80},{20,84},{24,88},{28,92},{32,9... | collective-permute-start | bytes 1572872 | tf_op jit(solution)/shard_map/cond/branch_4_fun/ppermute | solution.py:38
  102.0 28.7 %collective-permute-done.13.other = bf16[512,512]{1,0:T(8,128)(2,1)S(1)} collective-permute-done((bf16[512,512]{1,0:T(8,128)(2,1)S(1)}, bf16[512,512]{1,0:T(8,128)(2,1)S(1)}, u32[]{:S(2)}, u32[]{:S(2)}) %collective-permute-start.13) | collective-permute-done | bytes 524320 | tf_op jit(solution)/shard_map/cond/branch_4_fun/ppermute | solution.py:38
  131.7 10.2 %collective-permute-done.12.other = bf16[512,512]{1,0:T(8,128)(2,1)S(1)} collective-permute-done((bf16[512,512]{1,0:T(8,128)(2,1)S(1)}, bf16[512,512]{1,0:T(8,128)(2,1)S(1)}, u32[]{:S(2)}, u32[]{:S(2)}) %collective-permute-start.12) | collective-permute-done | bytes 524320 | tf_op jit(solution)/shard_map/cond/branch_4_fun/ppermute | solution.py:38
  143.9 5.4 %mean_down.9 = f32[512,1024]{1,0:T(8,128)} custom-call(f32[512,1024]{1,0:T(8,128)S(1)} %copy-done.10, bf16[512,1024]{1,0:T(8,128)(2,1)} %copy-done.17), custom_call_target="tpu_custom_call" | custom-call | tf_op jit(solution)/shard_map/cond/branch_4_fun/mean_down/pallas_call | solution.py:321
  (44 shorter events, 9.4 us)
Async XLA Ops:
  0.6 2.7 %copy-start.4 = (bf16[1,512,1024]{2,1,0:T(8,128)(2,1)S(1)}, bf16[1,512,1024]{2,1,0:T(8,128)(2,1)}, u32[]{:S(2)}) copy-start(bf16[1,512,1024]{2,1,0:T(8,128)(2,1)} %param.15) | copy-start | bytes 3145732
  5.1 32.2 %collective-permute-start.19 = (bf16[512,1024]{1,0:T(8,128)(2,1)S(1)}, bf16[512,1024]{1,0:T(8,128)(2,1)S(1)}, u32[]{:S(2)}, u32[]{:S(2)}) collective-permute-start(bf16[512,1024]{1,0:T(8,128)(2,1)S(1)} %get-tuple-element.258.left.refs_7_.rest_0_), channel_id=1, source_target_pairs={{0,2},{1,3},{2,0},{3,1},{4,6},{5,7},{6,4},{7,5},{8,10},{9,11},{10,... | collective-permute-start | bytes 3145736 | tf_op jit(solution)/shard_map/ppermute | solution.py:33
  7.6 2.8 %collective-permute-start.15 = (bf16[256,512]{1,0:T(8,128)(2,1)S(1)}, bf16[256,512]{1,0:T(8,128)(2,1)S(1)}, u32[]{:S(2)}, u32[]{:S(2)}) collective-permute-start(bf16[256,512]{1,0:T(8,128)(2,1)S(1)} %get-tuple-element.255), channel_id=1, source_target_pairs={{0,1},{1,0},{2,3},{3,2},{4,5},{5,4},{6,7},{7,6},{8,9},{9,8},{10,11... | collective-permute-start | bytes 786440 | tf_op jit(solution)/shard_map/ppermute | solution.py:33
  8.6 27.5 %collective-permute-start.16 = (bf16[256,512]{1,0:T(8,128)(2,1)S(1)}, bf16[256,512]{1,0:T(8,128)(2,1)S(1)}, u32[]{:S(2)}, u32[]{:S(2)}) collective-permute-start(bf16[256,512]{1,0:T(8,128)(2,1)S(1)} %get-tuple-element.256), channel_id=1, source_target_pairs={{0,2},{1,3},{2,0},{3,1},{4,6},{5,7},{6,4},{7,5},{8,10},{9,11},{10,... | collective-permute-start | bytes 786440 | tf_op jit(solution)/shard_map/ppermute | solution.py:33
  8.6 34.6 %collective-permute-start.17 = (bf16[256,512]{1,0:T(8,128)(2,1)S(1)}, bf16[256,512]{1,0:T(8,128)(2,1)S(1)}, u32[]{:S(2)}, u32[]{:S(2)}) collective-permute-start(bf16[256,512]{1,0:T(8,128)(2,1)S(1)} %get-tuple-element.257), channel_id=1, source_target_pairs={{0,3},{1,2},{2,1},{3,0},{4,7},{5,6},{6,5},{7,4},{8,11},{9,10},{10,... | collective-permute-start | bytes 786440 | tf_op jit(solution)/shard_map/ppermute | solution.py:33
  10.2 61.7 %collective-permute-start.25 = (bf16[512,1024]{1,0:T(8,128)(2,1)S(1)}, bf16[512,1024]{1,0:T(8,128)(2,1)S(1)}, u32[]{:S(2)}, u32[]{:S(2)}) collective-permute-start(bf16[512,1024]{1,0:T(8,128)(2,1)S(1)} %bitcast.33), channel_id=1, source_target_pairs={{0,1},{1,0},{2,3},{3,2},{4,5},{5,4},{6,7},{7,6},{8,9},{9,8},{10,11... | collective-permute-start | bytes 3145736 | tf_op jit(solution)/shard_map/ppermute | solution.py:33
  10.5 55.0 %collective-permute-start.18 = (bf16[512,1024]{1,0:T(8,128)(2,1)S(1)}, bf16[512,1024]{1,0:T(8,128)(2,1)S(1)}, u32[]{:S(2)}, u32[]{:S(2)}) collective-permute-start(bf16[512,1024]{1,0:T(8,128)(2,1)S(1)} %get-tuple-element.258.left.refs_7_.rest_0_), channel_id=1, source_target_pairs={{0,1},{1,0},{2,3},{3,2},{4,5},{5,4},{6,7},{7,6},{8,9},{9,8},{10,11... | collective-permute-start | bytes 3145736 | tf_op jit(solution)/shard_map/ppermute | solution.py:33
  36.1 16.9 %collective-permute-start.21 = (bf16[512,512]{1,0:T(8,128)(2,1)S(1)}, bf16[512,512]{1,0:T(8,128)(2,1)S(1)}, u32[]{:S(2)}, u32[]{:S(2)}) collective-permute-start(bf16[512,512]{1,0:T(8,128)(2,1)S(1)} %get-tuple-element.261.refs_0_.o0), channel_id=1, source_target_pairs={{0,2},{1,3},{2,0},{3,1},{4,6},{5,7},{6,4},{7,5},{8,10},{9,11},{10,... | collective-permute-start | bytes 1572872 | tf_op jit(solution)/shard_map/ppermute | solution.py:33
  37.3 31.4 %collective-permute-start.20 = (bf16[512,1024]{1,0:T(8,128)(2,1)S(1)}, bf16[512,1024]{1,0:T(8,128)(2,1)S(1)}, u32[]{:S(2)}, u32[]{:S(2)}) collective-permute-start(bf16[512,1024]{1,0:T(8,128)(2,1)S(1)} %collective-permute-done.19.left.refs_9_), channel_id=1, source_target_pairs={{0,1},{1,0},{2,3},{3,2},{4,5},{5,4},{6,7},{7,6},{8,9},{9,8},{10,11... | collective-permute-start | bytes 3145736 | tf_op jit(solution)/shard_map/ppermute | solution.py:33
  43.1 21.1 %collective-permute-start.22 = (bf16[512,512]{1,0:T(8,128)(2,1)S(1)}, bf16[512,512]{1,0:T(8,128)(2,1)S(1)}, u32[]{:S(2)}, u32[]{:S(2)}) collective-permute-start(bf16[512,512]{1,0:T(8,128)(2,1)S(1)} %get-tuple-element.262.refs_1_.o0), channel_id=1, source_target_pairs={{0,2},{1,3},{2,0},{3,1},{4,6},{5,7},{6,4},{7,5},{8,10},{9,11},{10,... | collective-permute-start | bytes 1572872 | tf_op jit(solution)/shard_map/ppermute | solution.py:33
  53.0 18.9 %collective-permute-start.23 = (bf16[512,512]{1,0:T(8,128)(2,1)S(1)}, bf16[512,512]{1,0:T(8,128)(2,1)S(1)}, u32[]{:S(2)}, u32[]{:S(2)}) collective-permute-start(bf16[512,512]{1,0:T(8,128)(2,1)S(1)} %collective-permute-done.21.refs_2_.o2), channel_id=1, source_target_pairs={{0,1},{1,0},{2,3},{3,2},{4,5},{5,4},{6,7},{7,6},{8,9},{9,8},{10,11... | collective-permute-start | bytes 1572872 | tf_op jit(solution)/shard_map/ppermute | solution.py:33
  64.2 7.7 %collective-permute-start.24 = (bf16[512,512]{1,0:T(8,128)(2,1)S(1)}, bf16[512,512]{1,0:T(8,128)(2,1)S(1)}, u32[]{:S(2)}, u32[]{:S(2)}) collective-permute-start(bf16[512,512]{1,0:T(8,128)(2,1)S(1)} %collective-permute-done.22.refs_3_.o2), channel_id=1, source_target_pairs={{0,1},{1,0},{2,3},{3,2},{4,5},{5,4},{6,7},{7,6},{8,9},{9,8},{10,11... | collective-permute-start | bytes 1572872 | tf_op jit(solution)/shard_map/ppermute | solution.py:33
  68.7 3.3 %copy-start = (f32[1,512,1024]{2,1,0:T(8,128)S(1)}, f32[1,512,1024]{2,1,0:T(8,128)}, u32[]{:S(2)}) copy-start(f32[1,512,1024]{2,1,0:T(8,128)} %param.18) | copy-start | bytes 6291460
  71.9 6.8 %copy-start.1 = (f32[1,512,1024]{2,1,0:T(8,128)S(1)}, f32[1,512,1024]{2,1,0:T(8,128)}, u32[]{:S(2)}) copy-start(f32[1,512,1024]{2,1,0:T(8,128)} %param.20) | copy-start | bytes 6291460
  72.0 6.8 %copy-start.2 = (f32[1,512,1024]{2,1,0:T(8,128)S(1)}, f32[1,512,1024]{2,1,0:T(8,128)}, u32[]{:S(2)}) copy-start(f32[1,512,1024]{2,1,0:T(8,128)} %param.22) | copy-start | bytes 6291460
  76.6 12.5 %collective-permute-start.28 = (bf16[256,512]{1,0:T(8,128)(2,1)S(1)}, bf16[256,512]{1,0:T(8,128)(2,1)S(1)}, u32[]{:S(2)}, u32[]{:S(2)}) collective-permute-start(bf16[256,512]{1,0:T(8,128)(2,1)S(1)} %get-tuple-element.266), channel_id=1, source_target_pairs={{0,1},{1,0},{2,3},{3,2},{4,5},{5,4},{6,7},{7,6},{8,9},{9,8},{10,11... | collective-permute-start | bytes 786440 | tf_op jit(solution)/shard_map/ppermute | solution.py:33
  76.7 15.5 %collective-permute-start.26 = (bf16[256,512]{1,0:T(8,128)(2,1)S(1)}, bf16[256,512]{1,0:T(8,128)(2,1)S(1)}, u32[]{:S(2)}, u32[]{:S(2)}) collective-permute-start(bf16[256,512]{1,0:T(8,128)(2,1)S(1)} %get-tuple-element.263), channel_id=1, source_target_pairs={{0,2},{1,3},{2,0},{3,1},{4,6},{5,7},{6,4},{7,5},{8,10},{9,11},{10,... | collective-permute-start | bytes 786440 | tf_op jit(solution)/shard_map/ppermute | solution.py:33
  78.2 13.9 %collective-permute-start.27 = (bf16[256,512]{1,0:T(8,128)(2,1)S(1)}, bf16[256,512]{1,0:T(8,128)(2,1)S(1)}, u32[]{:S(2)}, u32[]{:S(2)}) collective-permute-start(bf16[256,512]{1,0:T(8,128)(2,1)S(1)} %get-tuple-element.264), channel_id=1, source_target_pairs={{0,3},{1,2},{2,1},{3,0},{4,7},{5,6},{6,5},{7,4},{8,11},{9,10},{10,... | collective-permute-start | bytes 786440 | tf_op jit(solution)/shard_map/ppermute | solution.py:33
  83.9 5.2 %copy-start.5 = (f32[1,256,2048]{2,1,0:T(8,128)S(1)}, f32[1,256,2048]{2,1,0:T(8,128)}, u32[]{:S(2)}) copy-start(f32[1,256,2048]{2,1,0:T(8,128)} %param.17) | copy-start | bytes 6291460
  83.9 5.2 %copy-start.11 = (f32[1,256,2048]{2,1,0:T(8,128)S(1)}, f32[1,256,2048]{2,1,0:T(8,128)}, u32[]{:S(2)}) copy-start(f32[1,256,2048]{2,1,0:T(8,128)} %param.19) | copy-start | bytes 6291460
  83.9 5.1 %copy-start.12 = (f32[1,256,2048]{2,1,0:T(8,128)S(1)}, f32[1,256,2048]{2,1,0:T(8,128)}, u32[]{:S(2)}) copy-start(f32[1,256,2048]{2,1,0:T(8,128)} %param.21) | copy-start | bytes 6291460
  92.4 50.6 %collective-permute-start.14 = (bf16[512,1024]{1,0:T(8,128)(2,1)S(1)}, bf16[512,1024]{1,0:T(8,128)(2,1)S(1)}, u32[]{:S(2)}, u32[]{:S(2)}) collective-permute-start(bf16[512,1024]{1,0:T(8,128)(2,1)S(1)} %get-tuple-element.216), channel_id=1, source_target_pairs={{0,64},{4,68},{8,72},{12,76},{16,80},{20,84},{24,88},{28,92},{32,9... | collective-permute-start | bytes 3145736 | tf_op jit(solution)/shard_map/cond/branch_4_fun/ppermute | solution.py:38
  95.9 34.8 %collective-permute-start.13 = (bf16[512,512]{1,0:T(8,128)(2,1)S(1)}, bf16[512,512]{1,0:T(8,128)(2,1)S(1)}, u32[]{:S(2)}, u32[]{:S(2)}) collective-permute-start(bf16[512,512]{1,0:T(8,128)(2,1)S(1)} %get-tuple-element.214), channel_id=1, source_target_pairs={{0,64},{4,68},{8,72},{12,76},{16,80},{20,84},{24,88},{28,92},{32,9... | collective-permute-start | bytes 1572872 | tf_op jit(solution)/shard_map/cond/branch_4_fun/ppermute | solution.py:38
  99.0 42.9 %collective-permute-start.12 = (bf16[512,512]{1,0:T(8,128)(2,1)S(1)}, bf16[512,512]{1,0:T(8,128)(2,1)S(1)}, u32[]{:S(2)}, u32[]{:S(2)}) collective-permute-start(bf16[512,512]{1,0:T(8,128)(2,1)S(1)} %get-tuple-element.212), channel_id=1, source_target_pairs={{0,64},{4,68},{8,72},{12,76},{16,80},{20,84},{24,88},{28,92},{32,9... | collective-permute-start | bytes 1572872 | tf_op jit(solution)/shard_map/cond/branch_4_fun/ppermute | solution.py:38
  (3 other events, 5.8 us)

commit v3 on v2

--- a/solution.py
+++ b/solution.py
@@ -8,7 +8,7 @@
 from jax.sharding import PartitionSpec as P
 
 
-WIDTHS = (512, 512)
+WIDTHS = (640, 384)
 STARTS = tuple(sum(WIDTHS[:c]) for c in range(len(WIDTHS)))
 CHUNKS = len(WIDTHS)
 LOW = jnp.bfloat16
@@ -143,8 +143,8 @@
 
 
 def down_kernel(c, fixes, near, far, o0, o1, o2, o3, param, first, second, *rest):
-    wholes, kept, (p, m, v, sems) = rest[-12:-8], rest[-8:-4], rest[-4:]
-    local, send, mn, vn = kept
+    wholes, send, kept, (p, m, v, sems) = rest[-11:-8], rest[-8], rest[-7:-4], rest[-4:]
+    local, mn, vn = kept
     cols = pl.ds(STARTS[c], WIDTHS[c])
     loads = [
         pltpu.make_async_copy(whole.at[:, cols], part, sems.at[i])
@@ -186,27 +186,25 @@
     in_specs = [SMEM] + [VMEM] * 6 + [HBM] * 3 + [ANY]
     aliases = {}
     if news is not None:
-        aliases = {len(ins) + i: i for i in range(4)}
+        aliases = {len(ins) + i: i for i in range(3)}
         ins += news
-        in_specs += [HBM] * 4
-    kinds = (WIDE, LOW, WIDE, WIDE)
+        in_specs += [HBM] * 3
     return pl.pallas_call(
         partial(down_kernel, c),
-        out_shape=[shape(rows, cols, dtype=kind) for kind in kinds],
+        out_shape=[shape(rows, cols, dtype=WIDE)] * 3 + [shape(*part)],
         in_specs=in_specs,
-        out_specs=[HBM] * 4,
+        out_specs=[HBM] * 3 + [VMEM],
         input_output_aliases=aliases,
-        scratch_shapes=[pltpu.VMEM(part, kind) for kind in kinds + (WIDE,) * 3]
-        + [pltpu.SemaphoreType.DMA((4,))],
+        scratch_shapes=[pltpu.VMEM(part, WIDE)] * 6 + [pltpu.SemaphoreType.DMA((3,))],
         compiler_params=params(),
         name="down",
     )(*ins)
 
 
 def back_kernel(place, param, sa, sb, *refs):
-    ogs, side, outs = refs[: 3 * CHUNKS], refs[3 * CHUNKS], refs[-6:-2]
+    ogs, side, outs = refs[: 3 * CHUNKS], refs[3 * CHUNKS], refs[-7:-3]
     normed = refs[3 * CHUNKS + 1 : 3 * CHUNKS + 5]
-    low, pre_grad = refs[-2:]
+    low, pre_grad, grads = refs[-3:]
     rows = normed[0].shape[0]
     low[...] = param[...].astype(LOW)
     for k in range(4):
@@ -219,13 +217,19 @@
         slope = (sa, sb)[k // 2][(k % 2) * rows : (k % 2 + 1) * rows, :]
         pre_grad[k * rows : (k + 1) * rows, :] = (got * slope).astype(LOW)
     size = outs[0].shape[0]
-    for k in range(4):
+
+    def block(k, _):
         at = pl.ds(pl.multiple_of((place[0] ^ k) * size, size), size)
         total = None
         for j in range(4):
             part = dot(normed[j][:, at], pre_grad[j * rows : (j + 1) * rows, :], ((0,), (0,)))
             total = part if total is None else total + part
-        outs[k][...] = total.astype(LOW)
+        grads[k] = total.astype(LOW)
+        return 0
+
+    lax.fori_loop(0, 4, block, 0)
+    for k in range(4):
+        outs[k][...] = grads[k]
 
 
 def back(place, param, slopes, own, side, far, last, normed):
@@ -236,7 +240,7 @@
         out_shape=[shape(full // 4, hidden_size)] * 4,
         in_specs=[SMEM] + [VMEM] * (3 + 3 * CHUNKS + 5),
         out_specs=[VMEM] * 4,
-        scratch_shapes=[pltpu.VMEM(param.shape, LOW), pltpu.VMEM((4 * rows, hidden_size), LOW)],
+        scratch_shapes=[pltpu.VMEM(param.shape, LOW), pltpu.VMEM((4 * rows, hidden_size), LOW), pltpu.VMEM((4, full // 4, hidden_size), LOW)],
         compiler_params=params(),
         name="back",
     )(place, param, *slopes, *own, *far, *last, side, *normed)
@@ -311,22 +315,25 @@
     )(*ins)
 
 
-def mean_down_kernel(local, other, out):
-    out[...] = 0.5 * (local[...] + other[...].astype(WIDE))
-
-
-def mean_down(local, other):
+def mean_down_kernel(local, *refs):
+    out = refs[-1]
+    for c in range(CHUNKS):
+        cols = slice(STARTS[c], STARTS[c] + WIDTHS[c])
+        out[:, cols] = 0.5 * (local[:, cols] + refs[c][...].astype(WIDE))
+
+
+def mean_down(local, others):
     rows, cols = local.shape
     block = pl.BlockSpec((rows // 8, cols), lambda i: (i, 0))
     return pl.pallas_call(
         mean_down_kernel,
         grid=(8,),
         out_shape=shape(rows, cols, dtype=WIDE),
-        in_specs=[block] * 2,
+        in_specs=[block] + [pl.BlockSpec((rows // 8, w), lambda i: (i, 0)) for w in WIDTHS],
         out_specs=block,
         compiler_params=params(60 * 2**20),
         name="mean_down",
-    )(local, other)
+    )(local, *others)
 
 
 def mean_up_kernel(base, place, local, other, *rest):
@@ -363,7 +370,7 @@
     )(*ins)
 
 
-def prepare(place, fixes, level, tokens, grads, up_p, down_p, up_m, down_m, up_v, down_v):
+def prepare(place, fixes, level, tokens, grads, up_p, down_p, down_m, down_v):
     first = cut(place, up_p, fixes, level)
     ups = [first[0]]
     for k in range(1, 4):
@@ -381,32 +388,36 @@
     for c in range(CHUNKS):
         last.append(swap(far[c], 1))
     acts, slopes = (near_act, far_act), (near_slope, far_slope)
-    news = None
+    news, sends = None, []
     for c in range(CHUNKS - 1):
         ogs = (own[c], side, far[c], last[c])
-        news = down(c, fixes, *acts, ogs, down_p, down_m, down_v, news, n0)
-    g0, g1, g2, g3 = back(place, down_p, slopes, own, side, far, last, (n0, n1, n2, n3))
+        *news, send = down(c, fixes, *acts, ogs, down_p, down_m, down_v, news, n0)
+        sends.append(send)
+    return news, sends, acts, slopes, own, side, far, last, (n0, n1, n2, n3)
+
+
+def finish(level, place, fixes, made, up_p, down_p, up_m, down_m, up_v, down_v):
+    by = 2**level
+    news, sends, acts, slopes, own, side, far, last, normed = made
+    others = []
+    for c, send in enumerate(sends):
+        others.append(from_partner(send, by))
+    g0, g1, g2, g3 = back(place, down_p, slopes, own, side, far, last, normed)
     g2 = swap(g2, 2)
     g3 = swap(g3, 3)
     g1 = swap(g1, 1)
     c = CHUNKS - 1
     ogs = (own[c], side, far[c], last[c])
-    news = down(c, fixes, *acts, ogs, down_p, down_m, down_v, news, g0)
-    near = up(0, place, fixes, g0, g1, up_p, up_m, up_v, None)
-    return news, near, g2, g3
-
-
-def finish(level, place, fixes, made, up_p, up_m, up_v):
-    by = 2**level
-    (down_local, send, *down_new), (near_local, near_send, *up_new), g2, g3 = made
-    other = from_partner(send, by)
-    near_other = from_partner(near_send, by)
+    *news, send = down(c, fixes, *acts, ogs, down_p, down_m, down_v, news, g0)
+    others.append(from_partner(send, by))
+    near_local, send, *up_new = up(0, place, fixes, g0, g1, up_p, up_m, up_v, None)
+    near_other = from_partner(send, by)
     far_local, send, *up_new = up(2, place, fixes, g2, g3, up_p, up_m, up_v, up_new)
     far_other = from_partner(send, by)
-    new_down = mean_down(down_local, other)
+    new_down = mean_down(news[0], others)
     new_up = mean_up(0, place, near_local, near_other, None)
     new_up = mean_up(2, place, far_local, far_other, new_up)
-    return new_up, new_down, up_new[0], down_new[0], up_new[1], down_new[1]
+    return new_up, new_down, up_new[0], news[1], up_new[1], news[2]
 
 
 def body(tokens, out_grad, step, *state):
@@ -418,7 +429,9 @@
         [1.0 - jnp.power(WIDE(0.9), count), 1.0 - jnp.power(WIDE(0.999), count)]
     )
     level = step % levels
-    made = prepare(place, fixes, level, tokens[0], out_grad[0], *state)
+    made = prepare(
+        place, fixes, level, tokens[0], out_grad[0], state[0], *state[1::2]
+    )
 
     def branch(k, *args):
         return finish(k, *args)
@@ -429,7 +442,7 @@
         place,
         fixes,
         made,
-        *state[::2],
+        *state,
     )
     return tuple(a[None] for a in outs)
 

time: 150 us -> 166 us (1.11)
  waiting for transfers between devices: 84.4 us -> 93.6 us
  loops' own time: 0.27 us -> 6.13 us
    ppermute x14, waiting for transfers between devices: 45.5 us -> 59.2 us  [swap(): return lax.ppermute(array, 'zero', [(i, i ^ mask) for i in range(size)])]
    another operation x1, loops' own time: 0.27 us -> 6.13 us  [body(): lax.switch(level[0], [partial(branch, k) for k in range(levels)], place,...]
    ppermute x3 -> x4, waiting for transfers between devices: 38.9 us -> 34.5 us  [from_partner(): lax.ppermute(array, 'peer', [(i, (i - by) % size) for i in range(size)])]
    ppermute x14, starting transfers between devices: 17.1 us -> 15.3 us  [swap(): return lax.ppermute(array, 'zero', [(i, i ^ mask) for i in range(size)])]
    ppermute x3 -> x4, starting transfers between devices: 6.55 us -> 7.66 us  [from_partner(): lax.ppermute(array, 'peer', [(i, (i - by) % size) for i in range(size)])]
  transfers between devices with their start and end apart: 17 -> 18, of which waited for: 6 -> 6; matrix products, arithmetic and copies ran while one was open for 0% -> 0% of each run, Pallas kernels for 17% -> 18%
where the time goes in v3:
time: 166 us; the launch traced here: 165 us
  waiting for transfers between devices  93.6 us (56%)
  Pallas kernels  39.5 us (24%)
  starting transfers between devices  22.9 us (14%)
  loops' own time  6.13 us (4%)
  between operations  1.93 us (1%)
    ppermute x14, waiting for transfers between devices, swap(): return lax.ppermute(array, 'zero', [(i, i ^ mask) for i in range(size)])  59.2 us
    ppermute x4, waiting for transfers between devices, from_partner(): lax.ppermute(array, 'peer', [(i, (i - by) % size) for i in range(size)])  34.5 us
    ppermute x14, starting transfers between devices, swap(): return lax.ppermute(array, 'zero', [(i, i ^ mask) for i in range(size)])  15.3 us
    pallas_call x2, Pallas kernels, down(): pl.pallas_call(partial(down_kernel, c), out_shape=[shape(rows, cols, dtyp...  10.1 us
    ppermute x4, starting transfers between devices, from_partner(): lax.ppermute(array, 'peer', [(i, (i - by) % size) for i in range(size)])  7.66 us
    pallas_call x2, Pallas kernels, hidden(): pl.pallas_call(hidden_kernel, out_shape=[shape(width, 2 * rows), shape(2...  6.4 us
    another operation x1, loops' own time, body(): lax.switch(level[0], [partial(branch, k) for k in range(levels)], place,...  6.13 us
    pallas_call x1, Pallas kernels, back(): pl.pallas_call(back_kernel, out_shape=[shape(full // 4, hidden_size)] * 4...  6.05 us
  transfers between devices with their start and end apart: 18, of which 6 were waited for; matrix products, arithmetic and copies ran while one was open for 0% of the time, Pallas kernels for 18%

profile of v3, /device:TPU:1, one launch (start us, length us, event | category | flops | bytes accessed | tf_op | source)
XLA Modules:
  0.0 165.3 jit_solution(5988581118502048700)
XLA Ops:
  1.6 1.7 %cut.1 = (bf16[256,512]{1,0:T(8,128)(2,1)S(1)}, bf16[256,512]{1,0:T(8,128)(2,1)S(1)}, bf16[256,512]{1,0:T(8,128)(2,1)S(1)}, bf16[256,512]{1,0:T(8,128)(2,1)S(1)}) custom-call(s32[1]{0:T(128)} %bitcast.11.place, f32[256,2048]{1,0:T(8,128)} %bitcast.33, f32[2]{0:T(128)S(1)} %pad_maximum_fusion.refs_0_.fixes, s32[1]{0:T(128)S(6)} %select_n.7.refs_1_), custom_call_target="tpu_custom_call" | custom-call | tf_op jit(solution)/shard_map/cut/pallas_call | solution.py:69
  3.4 1.7 %norm.1 = (bf16[512,1024]{1,0:T(8,128)(2,1)S(1)}, bf16[512,640]{1,0:T(8,128)(2,1)S(1)}, bf16[512,384]{1,0:T(8,128)(2,1)S(1)}) custom-call(bf16[512,1024]{1,0:T(8,128)(2,1)S(1)} %bitcast.24, bf16[512,1024]{1,0:T(8,128)(2,1)S(1)} %bitcast.25, bf16[256,512]{1,0:T(8,128)(2,1)S(1)} %get-tuple-element.514._.u0), custom_call_target="tpu_custom_call" | custom-call | tf_op jit(solution)/shard_map/norm/pallas_call | solution.py:97
  5.1 2.5 %collective-permute-start.39 = (bf16[512,1024]{1,0:T(8,128)(2,1)S(1)}, bf16[512,1024]{1,0:T(8,128)(2,1)S(1)}, u32[]{:S(2)}, u32[]{:S(2)}) collective-permute-start(bf16[512,1024]{1,0:T(8,128)(2,1)S(1)} %get-tuple-element.518.left.rest_0_), channel_id=1, source_target_pairs={{0,2},{1,3},{2,0},{3,1},{4,6},{5,7},{6,4},{7,5},{8,10},{9,11},{10,... | collective-permute-start | bytes 3145736 | tf_op jit(solution)/shard_map/ppermute | solution.py:33
  10.6 19.9 %collective-permute-done.39.left = bf16[512,1024]{1,0:T(8,128)(2,1)S(1)} collective-permute-done((bf16[512,1024]{1,0:T(8,128)(2,1)S(1)}, bf16[512,1024]{1,0:T(8,128)(2,1)S(1)}, u32[]{:S(2)}, u32[]{:S(2)}) %collective-permute-start.39) | collective-permute-done | bytes 1048608 | tf_op jit(solution)/shard_map/ppermute | solution.py:33
  30.5 2.1 %collective-permute-start.40 = (bf16[512,1024]{1,0:T(8,128)(2,1)S(1)}, bf16[512,1024]{1,0:T(8,128)(2,1)S(1)}, u32[]{:S(2)}, u32[]{:S(2)}) collective-permute-start(bf16[512,1024]{1,0:T(8,128)(2,1)S(1)} %collective-permute-done.39.left), channel_id=1, source_target_pairs={{0,1},{1,0},{2,3},{3,2},{4,5},{5,4},{6,7},{7,6},{8,9},{9,8},{10,11... | collective-permute-start | bytes 3145736 | tf_op jit(solution)/shard_map/ppermute | solution.py:33
  32.6 17.6 %collective-permute-done.36.u2 = bf16[256,512]{1,0:T(8,128)(2,1)S(1)} collective-permute-done((bf16[256,512]{1,0:T(8,128)(2,1)S(1)}, bf16[256,512]{1,0:T(8,128)(2,1)S(1)}, u32[]{:S(2)}, u32[]{:S(2)}) %collective-permute-start.36) | collective-permute-done | bytes 262176 | tf_op jit(solution)/shard_map/ppermute | solution.py:33
  50.2 2.6 %collective-permute-start.37 = (bf16[256,512]{1,0:T(8,128)(2,1)S(1)}, bf16[256,512]{1,0:T(8,128)(2,1)S(1)}, u32[]{:S(2)}, u32[]{:S(2)}) collective-permute-start(bf16[256,512]{1,0:T(8,128)(2,1)S(1)} %get-tuple-element.517), channel_id=1, source_target_pairs={{0,3},{1,2},{2,1},{3,0},{4,7},{5,6},{6,5},{7,4},{8,11},{9,10},{10,... | collective-permute-start | bytes 786440 | tf_op jit(solution)/shard_map/ppermute | solution.py:33
  52.8 6.6 %collective-permute-done.37.u3 = bf16[256,512]{1,0:T(8,128)(2,1)S(1)} collective-permute-done((bf16[256,512]{1,0:T(8,128)(2,1)S(1)}, bf16[256,512]{1,0:T(8,128)(2,1)S(1)}, u32[]{:S(2)}, u32[]{:S(2)}) %collective-permute-start.37) | collective-permute-done | bytes 262176 | tf_op jit(solution)/shard_map/ppermute | solution.py:33
  59.4 1.5 collective-permute-start.43
  60.9 8.7 %collective-permute-done.42 = bf16[512,384]{1,0:T(8,128)(2,1)S(1)} collective-permute-done((bf16[512,384]{1,0:T(8,128)(2,1)S(1)}, bf16[512,384]{1,0:T(8,128)(2,1)S(1)}, u32[]{:S(2)}, u32[]{:S(2)}) %collective-permute-start.42) | collective-permute-done | bytes 393248 | tf_op jit(solution)/shard_map/ppermute | solution.py:33
  70.9 3.2 %hidden.2 = (bf16[512,1024]{1,0:T(8,128)(2,1)S(1)}, f32[1024,512]{1,0:T(8,128)S(1)}) custom-call(s32[1]{0:T(128)} %bitcast.11.place, bf16[256,512]{1,0:T(8,128)(2,1)S(1)} %get-tuple-element.514._.u0, bf16[256,512]{1,0:T(8,128)(2,1)S(1)} %collective-permute-done.35.u1, bf16[256,512]{1,0:T(8,128)(2,1)S(1)} %collective-permute-done.36.u2, ...), custom_call_target="tpu_custom_call" | custom-call | tf_op jit(solution)/shard_map/hidden/pallas_call | solution.py:134
  74.1 3.2 %hidden.3 = (bf16[512,1024]{1,0:T(8,128)(2,1)S(1)}, f32[1024,512]{1,0:T(8,128)S(1)}) custom-call(s32[1]{0:T(128)} %bitcast.11.place, bf16[256,512]{1,0:T(8,128)(2,1)S(1)} %get-tuple-element.514._.u0, bf16[256,512]{1,0:T(8,128)(2,1)S(1)} %collective-permute-done.35.u1, bf16[256,512]{1,0:T(8,128)(2,1)S(1)} %collective-permute-done.36.u2, ...), custom_call_target="tpu_custom_call" | custom-call | tf_op jit(solution)/shard_map/hidden/pallas_call | solution.py:134
  77.4 6.3 %down.11 = (f32[512,1024]{1,0:T(8,128)}, f32[512,1024]{1,0:T(8,128)}, f32[512,1024]{1,0:T(8,128)}, bf16[512,640]{1,0:T(8,128)(2,1)S(1)}) custom-call(f32[2]{0:T(128)S(1)} %pad_maximum_fusion.refs_0_.fixes, bf16[512,1024]{1,0:T(8,128)(2,1)S(1)} %get-tuple-element.523.near, bf16[512,1024]{1,0:T(8,128)(2,1)S(1)} %get-tuple-element.524.far, ...), custom_call_target="tpu_custom_call" | custom-call | tf_op jit(solution)/shard_map/down/pallas_call | solution.py:192
  83.7 81.3 %conditional.1 = (f32[256,2048]{1,0:T(8,128)}, f32[512,1024]{1,0:T(8,128)}, f32[256,2048]{1,0:T(8,128)}, f32[512,1024]{1,0:T(8,128)}, f32[1,256,2048]{2,1,0:T(8,128)}, /*index=5*/f32[1,512,1024]{2,1,0:T(8,128)}) conditional(s32[]{:T(128)} %bitcast.10, (s32[1]{0:T(128)}, f32[512,1024]{1,0:T(8,128)S(1)}, ...), branch_computations={%region_0.1_spmd, %region_1.2_spmd, %region_2.3_spmd, %region_3.4_... | conditional | bytes 66060840 | solution.py:439
  89.4 6.0 %back.9 = (bf16[256,512]{1,0:T(8,128)(2,1)S(1)}, bf16[256,512]{1,0:T(8,128)(2,1)S(1)}, bf16[256,512]{1,0:T(8,128)(2,1)S(1)}, bf16[256,512]{1,0:T(8,128)(2,1)S(1)}) custom-call(s32[1]{0:T(128)} %get-tuple-element.444.place, f32[512,1024]{1,0:T(8,128)S(1)} %get-tuple-element.446.param, f32[1024,512]{1,0:T(8,128)S(1)} %get-tuple-element.447.sa, ...), custom_call_target="tpu_custom_call" | custom-call | tf_op jit(solution)/shard_map/cond/branch_4_fun/back/pallas_call | solution.py:238
  95.7 2.0 %collective-permute-start.29 = (bf16[256,512]{1,0:T(8,128)(2,1)S(1)}, bf16[256,512]{1,0:T(8,128)(2,1)S(1)}, u32[]{:S(2)}, u32[]{:S(2)}) collective-permute-start(bf16[256,512]{1,0:T(8,128)(2,1)S(1)} %get-tuple-element.461), channel_id=1, source_target_pairs={{0,3},{1,2},{2,1},{3,0},{4,7},{5,6},{6,5},{7,4},{8,11},{9,10},{10,... | collective-permute-start | bytes 786440 | tf_op jit(solution)/shard_map/cond/branch_4_fun/ppermute | solution.py:33
  97.7 3.5 %collective-permute-start.33 = (bf16[512,640]{1,0:T(8,128)(2,1)S(1)}, bf16[512,640]{1,0:T(8,128)(2,1)S(1)}, u32[]{:S(2)}, u32[]{:S(2)}) collective-permute-start(bf16[512,640]{1,0:T(8,128)(2,1)S(1)} %get-tuple-element.485), channel_id=1, source_target_pairs={{0,64},{4,68},{8,72},{12,76},{16,80},{20,84},{24,88},{28,92},{32,9... | collective-permute-start | bytes 1966088 | tf_op jit(solution)/shard_map/cond/branch_4_fun/ppermute | solution.py:38
  101.3 2.3 %up.18 = (f32[512,512]{1,0:T(8,128)S(1)}, bf16[512,512]{1,0:T(8,128)(2,1)S(1)}, f32[256,2048]{1,0:T(8,128)S(1)}, f32[256,2048]{1,0:T(8,128)S(1)}) custom-call(s32[1]{0:T(128)} %get-tuple-element.444.place, f32[2]{0:T(128)S(1)} %get-tuple-element.445.fixes, bf16[256,512]{1,0:T(8,128)(2,1)S(1)} %get-tuple-element.465.left.rest_0_, ...), custom_call_target="tpu_custom_call" | custom-call | tf_op jit(solution)/shard_map/cond/branch_4_fun/up/pallas_call | solution.py:300
  103.7 6.5 %collective-permute-done.29.right = bf16[256,512]{1,0:T(8,128)(2,1)S(1)} collective-permute-done((bf16[256,512]{1,0:T(8,128)(2,1)S(1)}, bf16[256,512]{1,0:T(8,128)(2,1)S(1)}, u32[]{:S(2)}, u32[]{:S(2)}) %collective-permute-start.29) | collective-permute-done | bytes 262176 | tf_op jit(solution)/shard_map/cond/branch_4_fun/ppermute | solution.py:33
  110.2 3.2 %up.19 = (f32[512,512]{1,0:T(8,128)S(1)}, bf16[512,512]{1,0:T(8,128)(2,1)}, f32[256,2048]{1,0:T(8,128)S(1)}, f32[256,2048]{1,0:T(8,128)S(1)}) custom-call(s32[1]{0:T(128)} %get-tuple-element.444.place, f32[2]{0:T(128)S(1)} %get-tuple-element.445.fixes, ...), custom_call_target="tpu_custom_call", output_to_operand_aliasing={{2}: (7, {}), {3}: (8, {})} | custom-call | tf_op jit(solution)/shard_map/cond/branch_4_fun/up/pallas_call | solution.py:300
  113.4 3.9 %collective-permute-start.31 = (bf16[512,512]{1,0:T(8,128)(2,1)}, bf16[512,512]{1,0:T(8,128)(2,1)S(1)}, u32[]{:S(2)}, u32[]{:S(2)}) collective-permute-start(bf16[512,512]{1,0:T(8,128)(2,1)} %get-tuple-element.481), channel_id=1, source_target_pairs={{0,64},{4,68},{8,72},{12,76},{16,80},{20,84},{24,88},{28,92},{32,9... | collective-permute-start | bytes 1572872 | tf_op jit(solution)/shard_map/cond/branch_4_fun/ppermute | solution.py:38
  117.3 3.8 %down.10 = (f32[512,1024]{1,0:T(8,128)}, f32[512,1024]{1,0:T(8,128)S(1)}, f32[512,1024]{1,0:T(8,128)S(1)}, bf16[512,384]{1,0:T(8,128)(2,1)S(1)}) custom-call(f32[2]{0:T(128)S(1)} %get-tuple-element.445.fixes, bf16[512,1024]{1,0:T(8,128)(2,1)S(1)} %get-tuple-element.470.near, ...), custom_call_target="tpu_custom_call", output_to_operand_aliasing={{0}: (11, {}), {1}: (12, {}), {2}: (13, {})} | custom-call | tf_op jit(solution)/shard_map/cond/branch_4_fun/down/pallas_call | solution.py:192
  121.3 34.5 %collective-permute-done.34.refs_1_ = bf16[512,384]{1,0:T(8,128)(2,1)S(1)} collective-permute-done((bf16[512,384]{1,0:T(8,128)(2,1)S(1)}, bf16[512,384]{1,0:T(8,128)(2,1)S(1)}, u32[]{:S(2)}, u32[]{:S(2)}) %collective-permute-start.34) | collective-permute-done | bytes 393248 | tf_op jit(solution)/shard_map/cond/branch_4_fun/ppermute | solution.py:38
  156.8 5.9 %mean_down.9 = f32[512,1024]{1,0:T(8,128)} custom-call(f32[512,1024]{1,0:T(8,128)} %get-tuple-element.484.local, bf16[512,640]{1,0:T(8,128)(2,1)} %copy-done.42, bf16[512,384]{1,0:T(8,128)(2,1)} %copy-done.47), custom_call_target="tpu_custom_call" | custom-call | tf_op jit(solution)/shard_map/cond/branch_4_fun/mean_down/pallas_call | solution.py:328
  (58 shorter events, 8.0 us)
Async XLA Ops:
  5.1 25.4 %collective-permute-start.39 = (bf16[512,1024]{1,0:T(8,128)(2,1)S(1)}, bf16[512,1024]{1,0:T(8,128)(2,1)S(1)}, u32[]{:S(2)}, u32[]{:S(2)}) collective-permute-start(bf16[512,1024]{1,0:T(8,128)(2,1)S(1)} %get-tuple-element.518.left.rest_0_), channel_id=1, source_target_pairs={{0,2},{1,3},{2,0},{3,1},{4,6},{5,7},{6,4},{7,5},{8,10},{9,11},{10,... | collective-permute-start | bytes 3145736 | tf_op jit(solution)/shard_map/ppermute | solution.py:33
  7.7 25.0 %collective-permute-start.35 = (bf16[256,512]{1,0:T(8,128)(2,1)S(1)}, bf16[256,512]{1,0:T(8,128)(2,1)S(1)}, u32[]{:S(2)}, u32[]{:S(2)}) collective-permute-start(bf16[256,512]{1,0:T(8,128)(2,1)S(1)} %get-tuple-element.515), channel_id=1, source_target_pairs={{0,1},{1,0},{2,3},{3,2},{4,5},{5,4},{6,7},{7,6},{8,9},{9,8},{10,11... | collective-permute-start | bytes 786440 | tf_op jit(solution)/shard_map/ppermute | solution.py:33
  8.6 50.8 %collective-permute-start.41 = (bf16[512,640]{1,0:T(8,128)(2,1)S(1)}, bf16[512,640]{1,0:T(8,128)(2,1)S(1)}, u32[]{:S(2)}, u32[]{:S(2)}) collective-permute-start(bf16[512,640]{1,0:T(8,128)(2,1)S(1)} %get-tuple-element.521.o0), channel_id=1, source_target_pairs={{0,2},{1,3},{2,0},{3,1},{4,6},{5,7},{6,4},{7,5},{8,10},{9,11},{10,... | collective-permute-start | bytes 1966088 | tf_op jit(solution)/shard_map/ppermute | solution.py:33
  8.6 41.6 %collective-permute-start.36 = (bf16[256,512]{1,0:T(8,128)(2,1)S(1)}, bf16[256,512]{1,0:T(8,128)(2,1)S(1)}, u32[]{:S(2)}, u32[]{:S(2)}) collective-permute-start(bf16[256,512]{1,0:T(8,128)(2,1)S(1)} %get-tuple-element.516), channel_id=1, source_target_pairs={{0,2},{1,3},{2,0},{3,1},{4,6},{5,7},{6,4},{7,5},{8,10},{9,11},{10,... | collective-permute-start | bytes 786440 | tf_op jit(solution)/shard_map/ppermute | solution.py:33
  10.1 60.8 %collective-permute-start.38 = (bf16[512,1024]{1,0:T(8,128)(2,1)S(1)}, bf16[512,1024]{1,0:T(8,128)(2,1)S(1)}, u32[]{:S(2)}, u32[]{:S(2)}) collective-permute-start(bf16[512,1024]{1,0:T(8,128)(2,1)S(1)} %get-tuple-element.518.left.rest_0_), channel_id=1, source_target_pairs={{0,1},{1,0},{2,3},{3,2},{4,5},{5,4},{6,7},{7,6},{8,9},{9,8},{10,11... | collective-permute-start | bytes 3145736 | tf_op jit(solution)/shard_map/ppermute | solution.py:33
  30.5 43.6 %collective-permute-start.40 = (bf16[512,1024]{1,0:T(8,128)(2,1)S(1)}, bf16[512,1024]{1,0:T(8,128)(2,1)S(1)}, u32[]{:S(2)}, u32[]{:S(2)}) collective-permute-start(bf16[512,1024]{1,0:T(8,128)(2,1)S(1)} %collective-permute-done.39.left), channel_id=1, source_target_pairs={{0,1},{1,0},{2,3},{3,2},{4,5},{5,4},{6,7},{7,6},{8,9},{9,8},{10,11... | collective-permute-start | bytes 3145736 | tf_op jit(solution)/shard_map/ppermute | solution.py:33
  32.6 44.7 %collective-permute-start.45 = (bf16[512,1024]{1,0:T(8,128)(2,1)S(1)}, bf16[512,1024]{1,0:T(8,128)(2,1)S(1)}, u32[]{:S(2)}, u32[]{:S(2)}) collective-permute-start(bf16[512,1024]{1,0:T(8,128)(2,1)S(1)} %bitcast.26), channel_id=1, source_target_pairs={{0,1},{1,0},{2,3},{3,2},{4,5},{5,4},{6,7},{7,6},{8,9},{9,8},{10,11... | collective-permute-start | bytes 3145736 | tf_op jit(solution)/shard_map/ppermute | solution.py:33
  50.2 9.2 %collective-permute-start.37 = (bf16[256,512]{1,0:T(8,128)(2,1)S(1)}, bf16[256,512]{1,0:T(8,128)(2,1)S(1)}, u32[]{:S(2)}, u32[]{:S(2)}) collective-permute-start(bf16[256,512]{1,0:T(8,128)(2,1)S(1)} %get-tuple-element.517), channel_id=1, source_target_pairs={{0,3},{1,2},{2,1},{3,0},{4,7},{5,6},{6,5},{7,4},{8,11},{9,10},{10,... | collective-permute-start | bytes 786440 | tf_op jit(solution)/shard_map/ppermute | solution.py:33
  59.3 10.3 %collective-permute-start.42 = (bf16[512,384]{1,0:T(8,128)(2,1)S(1)}, bf16[512,384]{1,0:T(8,128)(2,1)S(1)}, u32[]{:S(2)}, u32[]{:S(2)}) collective-permute-start(bf16[512,384]{1,0:T(8,128)(2,1)S(1)} %get-tuple-element.522), channel_id=1, source_target_pairs={{0,2},{1,3},{2,0},{3,1},{4,6},{5,7},{6,4},{7,5},{8,10},{9,11},{10,... | collective-permute-start | bytes 1179656 | tf_op jit(solution)/shard_map/ppermute | solution.py:33
  59.4 17.9 %collective-permute-start.43 = (bf16[512,640]{1,0:T(8,128)(2,1)S(1)}, bf16[512,640]{1,0:T(8,128)(2,1)S(1)}, u32[]{:S(2)}, u32[]{:S(2)}) collective-permute-start(bf16[512,640]{1,0:T(8,128)(2,1)S(1)} %collective-permute-done.41.o2), channel_id=1, source_target_pairs={{0,1},{1,0},{2,3},{3,2},{4,5},{5,4},{6,7},{7,6},{8,9},{9,8},{10,11... | collective-permute-start | bytes 1966088 | tf_op jit(solution)/shard_map/ppermute | solution.py:33
  69.6 14.1 %collective-permute-start.44 = (bf16[512,384]{1,0:T(8,128)(2,1)S(1)}, bf16[512,384]{1,0:T(8,128)(2,1)S(1)}, u32[]{:S(2)}, u32[]{:S(2)}) collective-permute-start(bf16[512,384]{1,0:T(8,128)(2,1)S(1)} %collective-permute-done.42), channel_id=1, source_target_pairs={{0,1},{1,0},{2,3},{3,2},{4,5},{5,4},{6,7},{7,6},{8,9},{9,8},{10,11... | collective-permute-start | bytes 1179656 | tf_op jit(solution)/shard_map/ppermute | solution.py:33
  95.5 5.8 %collective-permute-start.30 = (bf16[256,512]{1,0:T(8,128)(2,1)S(1)}, bf16[256,512]{1,0:T(8,128)(2,1)S(1)}, u32[]{:S(2)}, u32[]{:S(2)}) collective-permute-start(bf16[256,512]{1,0:T(8,128)(2,1)S(1)} %get-tuple-element.466), channel_id=1, source_target_pairs={{0,1},{1,0},{2,3},{3,2},{4,5},{5,4},{6,7},{7,6},{8,9},{9,8},{10,11... | collective-permute-start | bytes 786440 | tf_op jit(solution)/shard_map/cond/branch_4_fun/ppermute | solution.py:33
  95.6 8.1 %collective-permute-start.28 = (bf16[256,512]{1,0:T(8,128)(2,1)S(1)}, bf16[256,512]{1,0:T(8,128)(2,1)S(1)}, u32[]{:S(2)}, u32[]{:S(2)}) collective-permute-start(bf16[256,512]{1,0:T(8,128)(2,1)S(1)} %get-tuple-element.460), channel_id=1, source_target_pairs={{0,2},{1,3},{2,0},{3,1},{4,6},{5,7},{6,4},{7,5},{8,10},{9,11},{10,... | collective-permute-start | bytes 786440 | tf_op jit(solution)/shard_map/cond/branch_4_fun/ppermute | solution.py:33
  95.7 14.5 %collective-permute-start.29 = (bf16[256,512]{1,0:T(8,128)(2,1)S(1)}, bf16[256,512]{1,0:T(8,128)(2,1)S(1)}, u32[]{:S(2)}, u32[]{:S(2)}) collective-permute-start(bf16[256,512]{1,0:T(8,128)(2,1)S(1)} %get-tuple-element.461), channel_id=1, source_target_pairs={{0,3},{1,2},{2,1},{3,0},{4,7},{5,6},{6,5},{7,4},{8,11},{9,10},{10,... | collective-permute-start | bytes 786440 | tf_op jit(solution)/shard_map/cond/branch_4_fun/ppermute | solution.py:33
  97.7 58.1 %collective-permute-start.33 = (bf16[512,640]{1,0:T(8,128)(2,1)S(1)}, bf16[512,640]{1,0:T(8,128)(2,1)S(1)}, u32[]{:S(2)}, u32[]{:S(2)}) collective-permute-start(bf16[512,640]{1,0:T(8,128)(2,1)S(1)} %get-tuple-element.485), channel_id=1, source_target_pairs={{0,64},{4,68},{8,72},{12,76},{16,80},{20,84},{24,88},{28,92},{32,9... | collective-permute-start | bytes 1966088 | tf_op jit(solution)/shard_map/cond/branch_4_fun/ppermute | solution.py:38
  103.6 59.1 %collective-permute-start.32 = (bf16[512,512]{1,0:T(8,128)(2,1)S(1)}, bf16[512,512]{1,0:T(8,128)(2,1)S(1)}, u32[]{:S(2)}, u32[]{:S(2)}) collective-permute-start(bf16[512,512]{1,0:T(8,128)(2,1)S(1)} %get-tuple-element.483), channel_id=1, source_target_pairs={{0,64},{4,68},{8,72},{12,76},{16,80},{20,84},{24,88},{28,92},{32,9... | collective-permute-start | bytes 1572872 | tf_op jit(solution)/shard_map/cond/branch_4_fun/ppermute | solution.py:38
  110.2 7.2 %copy-start.12 = (f32[512,1024]{1,0:T(8,128)S(1)}, f32[512,1024]{1,0:T(8,128)}, u32[]{:S(2)}) copy-start(f32[512,1024]{1,0:T(8,128)} %get-tuple-element.475.rest_2_) | copy-start | bytes 6291460 | tf_op jit(solution)/shard_map/cond
  110.2 7.2 %copy-start.22 = (f32[512,1024]{1,0:T(8,128)S(1)}, f32[512,1024]{1,0:T(8,128)}, u32[]{:S(2)}) copy-start(f32[512,1024]{1,0:T(8,128)} %get-tuple-element.476.rest_3_) | copy-start | bytes 6291460 | tf_op jit(solution)/shard_map/cond
  113.4 7.8 %copy-start.32 = (f32[256,2048]{1,0:T(8,128)}, f32[256,2048]{1,0:T(8,128)S(1)}, u32[]{:S(2)}) copy-start(f32[256,2048]{1,0:T(8,128)S(1)} %get-tuple-element.559) | copy-start | bytes 6291460 | tf_op jit(solution)/shard_map/cond
  113.4 7.8 %copy-start.37 = (f32[256,2048]{1,0:T(8,128)}, f32[256,2048]{1,0:T(8,128)S(1)}, u32[]{:S(2)}) copy-start(f32[256,2048]{1,0:T(8,128)S(1)} %get-tuple-element.561) | copy-start | bytes 6291460 | tf_op jit(solution)/shard_map/cond
  113.4 50.3 %collective-permute-start.31 = (bf16[512,512]{1,0:T(8,128)(2,1)}, bf16[512,512]{1,0:T(8,128)(2,1)S(1)}, u32[]{:S(2)}, u32[]{:S(2)}) collective-permute-start(bf16[512,512]{1,0:T(8,128)(2,1)} %get-tuple-element.481), channel_id=1, source_target_pairs={{0,64},{4,68},{8,72},{12,76},{16,80},{20,84},{24,88},{28,92},{32,9... | collective-permute-start | bytes 1572872 | tf_op jit(solution)/shard_map/cond/branch_4_fun/ppermute | solution.py:38
  121.2 34.6 %copy-start.17 = (f32[512,1024]{1,0:T(8,128)}, f32[512,1024]{1,0:T(8,128)S(1)}, u32[]{:S(2)}) copy-start(f32[512,1024]{1,0:T(8,128)S(1)} %get-tuple-element.560) | copy-start | bytes 6291460 | tf_op jit(solution)/shard_map/cond
  121.2 34.6 %copy-start.27 = (f32[512,1024]{1,0:T(8,128)}, f32[512,1024]{1,0:T(8,128)S(1)}, u32[]{:S(2)}) copy-start(f32[512,1024]{1,0:T(8,128)S(1)} %get-tuple-element.562) | copy-start | bytes 6291460 | tf_op jit(solution)/shard_map/cond
  121.2 34.6 %collective-permute-start.34 = (bf16[512,384]{1,0:T(8,128)(2,1)S(1)}, bf16[512,384]{1,0:T(8,128)(2,1)S(1)}, u32[]{:S(2)}, u32[]{:S(2)}) collective-permute-start(bf16[512,384]{1,0:T(8,128)(2,1)S(1)} %get-tuple-element.486), channel_id=1, source_target_pairs={{0,64},{4,68},{8,72},{12,76},{16,80},{20,84},{24,88},{28,92},{32,9... | collective-permute-start | bytes 1179656 | tf_op jit(solution)/shard_map/cond/branch_4_fun/ppermute | solution.py:38
  (10 other events, 42.6 us)

commit v4 on v3

--- a/solution.py
+++ b/solution.py
@@ -8,7 +8,7 @@
 from jax.sharding import PartitionSpec as P
 
 
-WIDTHS = (640, 384)
+WIDTHS = (384, 640)
 STARTS = tuple(sum(WIDTHS[:c]) for c in range(len(WIDTHS)))
 CHUNKS = len(WIDTHS)
 LOW = jnp.bfloat16
@@ -396,22 +396,32 @@
     return news, sends, acts, slopes, own, side, far, last, (n0, n1, n2, n3)
 
 
-def finish(level, place, fixes, made, up_p, down_p, up_m, down_m, up_v, down_v):
-    by = 2**level
-    news, sends, acts, slopes, own, side, far, last, normed = made
+def first_part(level, place, made, param):
+    sends, slopes, own, side, far, last, normed = made
     others = []
-    for c, send in enumerate(sends):
-        others.append(from_partner(send, by))
-    g0, g1, g2, g3 = back(place, down_p, slopes, own, side, far, last, normed)
+    for send in sends:
+        others.append(from_partner(send, 2**level))
+    return others, back(place, param, slopes, own, side, far, last, normed)
+
+
+def between(place, fixes, made, gs, up_p, down_p, up_m, down_m, up_v, down_v):
+    news, acts, own, side, far, last = made
+    g0, g1, g2, g3 = gs
     g2 = swap(g2, 2)
     g3 = swap(g3, 3)
     g1 = swap(g1, 1)
     c = CHUNKS - 1
     ogs = (own[c], side, far[c], last[c])
     *news, send = down(c, fixes, *acts, ogs, down_p, down_m, down_v, news, g0)
-    others.append(from_partner(send, by))
-    near_local, send, *up_new = up(0, place, fixes, g0, g1, up_p, up_m, up_v, None)
-    near_other = from_partner(send, by)
+    near = up(0, place, fixes, g0, g1, up_p, up_m, up_v, None)
+    return news, send, near, g2, g3
+
+
+def finish(level, place, fixes, others, made, up_p, up_m, up_v):
+    by = 2**level
+    news, send, (near_local, near_send, *up_new), g2, g3 = made
+    others = [*others, from_partner(send, by)]
+    near_other = from_partner(near_send, by)
     far_local, send, *up_new = up(2, place, fixes, g2, g3, up_p, up_m, up_v, up_new)
     far_other = from_partner(send, by)
     new_down = mean_down(news[0], others)
@@ -429,21 +439,19 @@
         [1.0 - jnp.power(WIDE(0.9), count), 1.0 - jnp.power(WIDE(0.999), count)]
     )
     level = step % levels
-    made = prepare(
+    news, sends, acts, slopes, own, side, far, last, normed = prepare(
         place, fixes, level, tokens[0], out_grad[0], state[0], *state[1::2]
     )
 
-    def branch(k, *args):
-        return finish(k, *args)
-
-    outs = lax.switch(
-        level[0],
-        [partial(branch, k) for k in range(levels)],
-        place,
-        fixes,
-        made,
-        *state,
-    )
+    def branch(part, k, *args):
+        return part(k, *args)
+
+    def switch(part, *args):
+        return lax.switch(level[0], [partial(branch, part, k) for k in range(levels)], *args)
+
+    others, gs = switch(first_part, place, (sends, slopes, own, side, far, last, normed), state[1])
+    made = between(place, fixes, (news, acts, own, side, far, last), gs, *state)
+    outs = switch(finish, place, fixes, others, made, *state[::2])
     return tuple(a[None] for a in outs)
 
 

time: 166 us -> 157 us (0.946)
  waiting for transfers between devices: 93.6 us -> 83.1 us
  loops' own time: 6.13 us -> 0.37 us
  Pallas kernels: 39.5 us -> 43.6 us
  local copies, waits for them, and re-layouts: 1.08 us -> 3.74 us
    ppermute x14, waiting for transfers between devices: 59.2 us -> 50.8 us  [swap(): return lax.ppermute(array, 'zero', [(i, i ^ mask) for i in range(size)])]
    another operation x1 -> x2, loops' own time: 6.13 us -> 0.37 us  [switch(): lax.switch(level[0], [partial(branch, part, k) for k in range(levels)], *...]
    unnamed x16 -> x28, local copies, waits for them, and re-layouts: 0.04 us -> 2.87 us
    ppermute x4, waiting for transfers between devices: 34.5 us -> 32.4 us  [from_partner(): lax.ppermute(array, 'peer', [(i, (i - by) % size) for i in range(size)])]
    ppermute x4, starting transfers between devices: 7.66 us -> 9.6 us  [from_partner(): lax.ppermute(array, 'peer', [(i, (i - by) % size) for i in range(size)])]
  transfers between devices with their start and end apart: 18 -> 18, of which waited for: 6 -> 7; matrix products, arithmetic and copies ran while one was open for 0% -> 0% of each run, Pallas kernels for 18% -> 21%
where the time goes in v4:
time: 157 us; the launch traced here: 156 us
  waiting for transfers between devices  83.1 us (53%)
  Pallas kernels  43.6 us (28%)
  starting transfers between devices  23.8 us (15%)
  local copies, waits for them, and re-layouts  3.74 us (2%)
  between operations  1.73 us (1%)
    ppermute x14, waiting for transfers between devices, swap(): return lax.ppermute(array, 'zero', [(i, i ^ mask) for i in range(size)])  50.8 us
    ppermute x4, waiting for transfers between devices, from_partner(): lax.ppermute(array, 'peer', [(i, (i - by) % size) for i in range(size)])  32.4 us
    ppermute x14, starting transfers between devices, swap(): return lax.ppermute(array, 'zero', [(i, i ^ mask) for i in range(size)])  14.2 us
    pallas_call x2, Pallas kernels, down(): pl.pallas_call(partial(down_kernel, c), out_shape=[shape(rows, cols, dtyp...  11.7 us
    ppermute x4, starting transfers between devices, from_partner(): lax.ppermute(array, 'peer', [(i, (i - by) % size) for i in range(size)])  9.6 us
    pallas_call x1, Pallas kernels, back(): pl.pallas_call(back_kernel, out_shape=[shape(full // 4, hidden_size)] * 4...  7.13 us
    pallas_call x2, Pallas kernels, hidden(): pl.pallas_call(hidden_kernel, out_shape=[shape(width, 2 * rows), shape(2...  6.4 us
    pallas_call x2, Pallas kernels, up(): pl.pallas_call(partial(up_kernel, base), in_specs=in_specs, out_specs=[VM...  6.12 us
  transfers between devices with their start and end apart: 18, of which 7 were waited for; matrix products, arithmetic and copies ran while one was open for 0% of the time, Pallas kernels for 21%

profile of v4, /device:TPU:1, one launch (start us, length us, event | category | flops | bytes accessed | tf_op | source)
XLA Modules:
  0.0 156.5 jit_solution(4006278043661278078)
XLA Ops:
  3.3 2.9 %norm.1 = (bf16[512,1024]{1,0:T(8,128)(2,1)S(1)}, bf16[512,384]{1,0:T(8,128)(2,1)S(1)}, bf16[512,640]{1,0:T(8,128)(2,1)S(1)}) custom-call(bf16[512,1024]{1,0:T(8,128)(2,1)S(1)} %bitcast.28, bf16[512,1024]{1,0:T(8,128)(2,1)} %bitcast.14.grads, bf16[256,512]{1,0:T(8,128)(2,1)S(1)} %get-tuple-element.530._.u0), custom_call_target="tpu_custom_call" | custom-call | tf_op jit(solution)/shard_map/norm/pallas_call | solution.py:97
  6.3 2.5 %collective-permute-start.24 = (bf16[512,1024]{1,0:T(8,128)(2,1)S(1)}, bf16[512,1024]{1,0:T(8,128)(2,1)S(1)}, u32[]{:S(2)}, u32[]{:S(2)}) collective-permute-start(bf16[512,1024]{1,0:T(8,128)(2,1)S(1)} %get-tuple-element.534.left.rest_0_), channel_id=1, source_target_pairs={{0,2},{1,3},{2,0},{3,1},{4,6},{5,7},{6,4},{7,5},{8,10},{9,11},{10,... | collective-permute-start | bytes 3145736 | tf_op jit(solution)/shard_map/ppermute | solution.py:33
  11.8 19.9 %collective-permute-done.24.left = bf16[512,1024]{1,0:T(8,128)(2,1)S(1)} collective-permute-done((bf16[512,1024]{1,0:T(8,128)(2,1)S(1)}, bf16[512,1024]{1,0:T(8,128)(2,1)S(1)}, u32[]{:S(2)}, u32[]{:S(2)}) %collective-permute-start.24) | collective-permute-done | bytes 1048608 | tf_op jit(solution)/shard_map/ppermute | solution.py:33
  31.7 2.1 %collective-permute-start.25 = (bf16[512,1024]{1,0:T(8,128)(2,1)S(1)}, bf16[512,1024]{1,0:T(8,128)(2,1)S(1)}, u32[]{:S(2)}, u32[]{:S(2)}) collective-permute-start(bf16[512,1024]{1,0:T(8,128)(2,1)S(1)} %collective-permute-done.24.left), channel_id=1, source_target_pairs={{0,1},{1,0},{2,3},{3,2},{4,5},{5,4},{6,7},{7,6},{8,9},{9,8},{10,11... | collective-permute-start | bytes 3145736 | tf_op jit(solution)/shard_map/ppermute | solution.py:33
  33.8 3.5 %collective-permute-done.21.u2 = bf16[256,512]{1,0:T(8,128)(2,1)S(1)} collective-permute-done((bf16[256,512]{1,0:T(8,128)(2,1)S(1)}, bf16[256,512]{1,0:T(8,128)(2,1)S(1)}, u32[]{:S(2)}, u32[]{:S(2)}) %collective-permute-start.21) | collective-permute-done | bytes 262176 | tf_op jit(solution)/shard_map/ppermute | solution.py:33
  37.3 2.1 %collective-permute-start.26 = (bf16[512,1024]{1,0:T(8,128)(2,1)}, bf16[512,1024]{1,0:T(8,128)(2,1)S(1)}, u32[]{:S(2)}, u32[]{:S(2)}) collective-permute-start(bf16[512,1024]{1,0:T(8,128)(2,1)} %bitcast.14.grads), channel_id=1, source_target_pairs={{0,1},{1,0},{2,3},{3,2},{4,5},{5,4},{6,7},{7,6},{8,9},{9,8},{10,11... | collective-permute-start | bytes 3145736 | tf_op jit(solution)/shard_map/ppermute | solution.py:33
  39.4 18.1 %collective-permute-done.22.u3 = bf16[256,512]{1,0:T(8,128)(2,1)S(1)} collective-permute-done((bf16[256,512]{1,0:T(8,128)(2,1)S(1)}, bf16[256,512]{1,0:T(8,128)(2,1)S(1)}, u32[]{:S(2)}, u32[]{:S(2)}) %collective-permute-start.22) | collective-permute-done | bytes 262176 | tf_op jit(solution)/shard_map/ppermute | solution.py:33
  59.0 9.3 %collective-permute-done.27.o2 = bf16[512,384]{1,0:T(8,128)(2,1)S(1)} collective-permute-done((bf16[512,384]{1,0:T(8,128)(2,1)S(1)}, bf16[512,384]{1,0:T(8,128)(2,1)S(1)}, u32[]{:S(2)}, u32[]{:S(2)}) %collective-permute-start.27) | collective-permute-done | bytes 393248 | tf_op jit(solution)/shard_map/ppermute | solution.py:33
  69.1 3.2 %hidden.2 = (bf16[512,1024]{1,0:T(8,128)(2,1)S(1)}, f32[1024,512]{1,0:T(8,128)S(1)}) custom-call(s32[1]{0:T(128)} %bitcast.11.place, bf16[256,512]{1,0:T(8,128)(2,1)S(1)} %get-tuple-element.530._.u0, bf16[256,512]{1,0:T(8,128)(2,1)S(1)} %collective-permute-done.20.u1, bf16[256,512]{1,0:T(8,128)(2,1)S(1)} %collective-permute-done.21.u2, ...), custom_call_target="tpu_custom_call" | custom-call | tf_op jit(solution)/shard_map/hidden/pallas_call | solution.py:134
  72.3 3.2 %hidden.3 = (bf16[512,1024]{1,0:T(8,128)(2,1)S(1)}, f32[1024,512]{1,0:T(8,128)S(1)}) custom-call(s32[1]{0:T(128)} %bitcast.11.place, bf16[256,512]{1,0:T(8,128)(2,1)S(1)} %get-tuple-element.530._.u0, bf16[256,512]{1,0:T(8,128)(2,1)S(1)} %collective-permute-done.20.u1, bf16[256,512]{1,0:T(8,128)(2,1)S(1)} %collective-permute-done.21.u2, ...), custom_call_target="tpu_custom_call" | custom-call | tf_op jit(solution)/shard_map/hidden/pallas_call | solution.py:134
  75.6 4.3 %down.2 = (f32[512,1024]{1,0:T(8,128)}, f32[512,1024]{1,0:T(8,128)}, f32[512,1024]{1,0:T(8,128)}, bf16[512,384]{1,0:T(8,128)(2,1)S(1)}) custom-call(f32[2]{0:T(128)S(1)} %pad_maximum_fusion.refs_0_.fixes, bf16[512,1024]{1,0:T(8,128)(2,1)S(1)} %get-tuple-element.535.near, bf16[512,1024]{1,0:T(8,128)(2,1)S(1)} %get-tuple-element.536.far, ...), custom_call_target="tpu_custom_call" | custom-call | tf_op jit(solution)/shard_map/down/pallas_call | solution.py:192
  79.9 13.4 %conditional.2 = (bf16[512,384]{1,0:T(8,128)(2,1)}, bf16[256,512]{1,0:T(8,128)(2,1)S(1)}, bf16[256,512]{1,0:T(8,128)(2,1)S(1)}, bf16[256,512]{1,0:T(8,128)(2,1)S(1)}, bf16[256,512]{1,0:T(8,128)(2,1)S(1)}) conditional(s32[]{:T(128)} %bitcast.10, (bf16[512,384]{1,0:T(8,128)(2,1)S(1)}, s32[1]{0:T(128)}, ...), branch_computations={%region_0.1_spmd, %region_1.2_spmd, %region_2.3_spmd, %region_3.4_... | conditional | bytes 1572944 | solution.py:450
  80.2 3.5 %collective-permute-start.4 = (bf16[512,384]{1,0:T(8,128)(2,1)S(1)}, bf16[512,384]{1,0:T(8,128)(2,1)}, u32[]{:S(2)}, u32[]{:S(2)}) collective-permute-start(bf16[512,384]{1,0:T(8,128)(2,1)S(1)} %get-tuple-element.382), channel_id=1, source_target_pairs={{0,64},{4,68},{8,72},{12,76},{16,80},{20,84},{24,88},{28,92},{32,9... | collective-permute-start | bytes 1179656 | tf_op jit(solution)/shard_map/cond/branch_4_fun/ppermute | solution.py:38
  83.7 7.1 %back.9 = (bf16[256,512]{1,0:T(8,128)(2,1)S(1)}, bf16[256,512]{1,0:T(8,128)(2,1)S(1)}, bf16[256,512]{1,0:T(8,128)(2,1)S(1)}, bf16[256,512]{1,0:T(8,128)(2,1)S(1)}) custom-call(s32[1]{0:T(128)} %get-tuple-element.383.place, f32[512,1024]{1,0:T(8,128)S(1)} %get-tuple-element.384.param, f32[1024,512]{1,0:T(8,128)S(1)} %get-tuple-element.385.sa, ...), custom_call_target="tpu_custom_call" | custom-call | tf_op jit(solution)/shard_map/cond/branch_4_fun/back/pallas_call | solution.py:238
  90.8 2.4 %collective-permute-done.4 = bf16[512,384]{1,0:T(8,128)(2,1)} collective-permute-done((bf16[512,384]{1,0:T(8,128)(2,1)S(1)}, bf16[512,384]{1,0:T(8,128)(2,1)}, u32[]{:S(2)}, u32[]{:S(2)}) %collective-permute-start.4) | collective-permute-done | bytes 393248 | tf_op jit(solution)/shard_map/cond/branch_4_fun/ppermute | solution.py:38
  98.3 7.4 %down.3 = (f32[512,1024]{1,0:T(8,128)}, f32[512,1024]{1,0:T(8,128)}, f32[512,1024]{1,0:T(8,128)}, bf16[512,640]{1,0:T(8,128)(2,1)S(1)}) custom-call(f32[2]{0:T(128)S(1)} %pad_maximum_fusion.refs_0_.fixes, bf16[512,1024]{1,0:T(8,128)(2,1)S(1)} %get-tuple-element.535.near, ...), custom_call_target="tpu_custom_call", output_to_operand_aliasing={{0}: (11, {}), {1}: (12, {}), {2}: (13, {})} | custom-call | tf_op jit(solution)/shard_map/down/pallas_call | solution.py:192
  105.8 3.1 %up.11 = (f32[512,512]{1,0:T(8,128)S(1)}, bf16[512,512]{1,0:T(8,128)(2,1)S(1)}, f32[256,2048]{1,0:T(8,128)}, f32[256,2048]{1,0:T(8,128)}) custom-call(s32[1]{0:T(128)} %bitcast.11.place, f32[2]{0:T(128)S(1)} %pad_maximum_fusion.refs_0_.fixes, bf16[256,512]{1,0:T(8,128)(2,1)S(1)} %get-tuple-element.544.left.rest_0_, ...), custom_call_target="tpu_custom_call" | custom-call | tf_op jit(solution)/shard_map/up/pallas_call | solution.py:300
  108.9 47.6 %conditional.3 = (f32[256,2048]{1,0:T(8,128)}, f32[256,2048]{1,0:T(8,128)}, f32[1,256,2048]{2,1,0:T(8,128)}, f32[1,512,1024]{2,1,0:T(8,128)}) conditional(s32[]{:T(128)} %bitcast.10, (s32[1]{0:T(128)}, f32[2]{0:T(128)S(1)}, bf16[256,512]{1,0:T(8,128)(2,1)S(1)}, bf16[256,512]{1,0:T(8,128)(2,1)S(1)}, ...), branch_computations={%region_5.6_spmd, %region_6.7_spmd, %region_7.8_spmd, %region_8.9_... | conditional | bytes 9437364 | solution.py:450
  109.0 3.0 %collective-permute-start.19 = (bf16[512,640]{1,0:T(8,128)(2,1)S(1)}, bf16[512,640]{1,0:T(8,128)(2,1)S(1)}, u32[]{:S(2)}, u32[]{:S(2)}) collective-permute-start(bf16[512,640]{1,0:T(8,128)(2,1)S(1)} %get-tuple-element.491), channel_id=1, source_target_pairs={{0,64},{4,68},{8,72},{12,76},{16,80},{20,84},{24,88},{28,92},{32,9... | collective-permute-start | bytes 1966088 | tf_op jit(solution)/shard_map/cond/branch_4_fun/ppermute | solution.py:38
  112.1 3.1 %up.10 = (f32[512,512]{1,0:T(8,128)S(1)}, bf16[512,512]{1,0:T(8,128)(2,1)S(1)}, f32[256,2048]{1,0:T(8,128)}, f32[256,2048]{1,0:T(8,128)}) custom-call(s32[1]{0:T(128)} %get-tuple-element.474.place, f32[2]{0:T(128)S(1)} %get-tuple-element.475.fixes, bf16[256,512]{1,0:T(8,128)(2,1)S(1)} %get-tuple-element.476.left, ...), custom_call_target="tpu_custom_call", output_to_operand_aliasing={{2}: (7, {}), {3}: (8, {})} | custom-call | tf_op jit(solution)/shard_map/cond/branch_4_fun/up/pallas_call | solution.py:300
  115.2 3.0 %collective-permute-start.17 = (bf16[512,512]{1,0:T(8,128)(2,1)S(1)}, bf16[512,512]{1,0:T(8,128)(2,1)S(1)}, u32[]{:S(2)}, u32[]{:S(2)}) collective-permute-start(bf16[512,512]{1,0:T(8,128)(2,1)S(1)} %get-tuple-element.486), channel_id=1, source_target_pairs={{0,64},{4,68},{8,72},{12,76},{16,80},{20,84},{24,88},{28,92},{32,9... | collective-permute-start | bytes 1572872 | tf_op jit(solution)/shard_map/cond/branch_4_fun/ppermute | solution.py:38
  118.1 19.7 %collective-permute-done.18.other = bf16[512,512]{1,0:T(8,128)(2,1)S(1)} collective-permute-done((bf16[512,512]{1,0:T(8,128)(2,1)S(1)}, bf16[512,512]{1,0:T(8,128)(2,1)S(1)}, u32[]{:S(2)}, u32[]{:S(2)}) %collective-permute-start.18) | collective-permute-done | bytes 524320 | tf_op jit(solution)/shard_map/cond/branch_4_fun/ppermute | solution.py:38
  138.9 10.2 %collective-permute-done.17.other = bf16[512,512]{1,0:T(8,128)(2,1)S(1)} collective-permute-done((bf16[512,512]{1,0:T(8,128)(2,1)S(1)}, bf16[512,512]{1,0:T(8,128)(2,1)S(1)}, u32[]{:S(2)}, u32[]{:S(2)}) %collective-permute-start.17) | collective-permute-done | bytes 524320 | tf_op jit(solution)/shard_map/cond/branch_4_fun/ppermute | solution.py:38
  151.0 5.5 %mean_down.9 = f32[512,1024]{1,0:T(8,128)} custom-call(f32[512,1024]{1,0:T(8,128)S(1)} %get-tuple-element.489.local, bf16[512,384]{1,0:T(8,128)(2,1)} %get-tuple-element.490.refs_0_, bf16[512,640]{1,0:T(8,128)(2,1)} %copy-done.18), custom_call_target="tpu_custom_call" | custom-call | tf_op jit(solution)/shard_map/cond/branch_4_fun/mean_down/pallas_call | solution.py:328
  (57 shorter events, 15.2 us)
Async XLA Ops:
  6.3 73.6 %copy-start.12 = (bf16[512,640]{1,0:T(8,128)(2,1)}, bf16[512,640]{1,0:T(8,128)(2,1)S(1)}, u32[]{:S(2)}) copy-start(bf16[512,640]{1,0:T(8,128)(2,1)S(1)} %get-tuple-element.541.o0) | copy-start | bytes 1966084
  6.3 25.4 %collective-permute-start.24 = (bf16[512,1024]{1,0:T(8,128)(2,1)S(1)}, bf16[512,1024]{1,0:T(8,128)(2,1)S(1)}, u32[]{:S(2)}, u32[]{:S(2)}) collective-permute-start(bf16[512,1024]{1,0:T(8,128)(2,1)S(1)} %get-tuple-element.534.left.rest_0_), channel_id=1, source_target_pairs={{0,2},{1,3},{2,0},{3,1},{4,6},{5,7},{6,4},{7,5},{8,10},{9,11},{10,... | collective-permute-start | bytes 3145736 | tf_op jit(solution)/shard_map/ppermute | solution.py:33
  8.8 3.0 %collective-permute-start.20 = (bf16[256,512]{1,0:T(8,128)(2,1)S(1)}, bf16[256,512]{1,0:T(8,128)(2,1)S(1)}, u32[]{:S(2)}, u32[]{:S(2)}) collective-permute-start(bf16[256,512]{1,0:T(8,128)(2,1)S(1)} %get-tuple-element.531), channel_id=1, source_target_pairs={{0,1},{1,0},{2,3},{3,2},{4,5},{5,4},{6,7},{7,6},{8,9},{9,8},{10,11... | collective-permute-start | bytes 786440 | tf_op jit(solution)/shard_map/ppermute | solution.py:33
  9.8 27.5 %collective-permute-start.21 = (bf16[256,512]{1,0:T(8,128)(2,1)S(1)}, bf16[256,512]{1,0:T(8,128)(2,1)S(1)}, u32[]{:S(2)}, u32[]{:S(2)}) collective-permute-start(bf16[256,512]{1,0:T(8,128)(2,1)S(1)} %get-tuple-element.532), channel_id=1, source_target_pairs={{0,2},{1,3},{2,0},{3,1},{4,6},{5,7},{6,4},{7,5},{8,10},{9,11},{10,... | collective-permute-start | bytes 786440 | tf_op jit(solution)/shard_map/ppermute | solution.py:33
  9.8 49.2 %collective-permute-start.29 = (bf16[512,640]{1,0:T(8,128)(2,1)S(1)}, bf16[512,640]{1,0:T(8,128)(2,1)S(1)}, u32[]{:S(2)}, u32[]{:S(2)}) collective-permute-start(bf16[512,640]{1,0:T(8,128)(2,1)S(1)} %get-tuple-element.541.o0), channel_id=1, source_target_pairs={{0,2},{1,3},{2,0},{3,1},{4,6},{5,7},{6,4},{7,5},{8,10},{9,11},{10,... | collective-permute-start | bytes 1966088 | tf_op jit(solution)/shard_map/ppermute | solution.py:33
  11.2 57.8 %collective-permute-start.23 = (bf16[512,1024]{1,0:T(8,128)(2,1)S(1)}, bf16[512,1024]{1,0:T(8,128)(2,1)S(1)}, u32[]{:S(2)}, u32[]{:S(2)}) collective-permute-start(bf16[512,1024]{1,0:T(8,128)(2,1)S(1)} %get-tuple-element.534.left.rest_0_), channel_id=1, source_target_pairs={{0,1},{1,0},{2,3},{3,2},{4,5},{5,4},{6,7},{7,6},{8,9},{9,8},{10,11... | collective-permute-start | bytes 3145736 | tf_op jit(solution)/shard_map/ppermute | solution.py:33
  11.8 45.7 %collective-permute-start.22 = (bf16[256,512]{1,0:T(8,128)(2,1)S(1)}, bf16[256,512]{1,0:T(8,128)(2,1)S(1)}, u32[]{:S(2)}, u32[]{:S(2)}) collective-permute-start(bf16[256,512]{1,0:T(8,128)(2,1)S(1)} %get-tuple-element.533), channel_id=1, source_target_pairs={{0,3},{1,2},{2,1},{3,0},{4,7},{5,6},{6,5},{7,4},{8,11},{9,10},{10,... | collective-permute-start | bytes 786440 | tf_op jit(solution)/shard_map/ppermute | solution.py:33
  31.7 40.6 %collective-permute-start.25 = (bf16[512,1024]{1,0:T(8,128)(2,1)S(1)}, bf16[512,1024]{1,0:T(8,128)(2,1)S(1)}, u32[]{:S(2)}, u32[]{:S(2)}) collective-permute-start(bf16[512,1024]{1,0:T(8,128)(2,1)S(1)} %collective-permute-done.24.left), channel_id=1, source_target_pairs={{0,1},{1,0},{2,3},{3,2},{4,5},{5,4},{6,7},{7,6},{8,9},{9,8},{10,11... | collective-permute-start | bytes 3145736 | tf_op jit(solution)/shard_map/ppermute | solution.py:33
  37.3 38.2 %collective-permute-start.26 = (bf16[512,1024]{1,0:T(8,128)(2,1)}, bf16[512,1024]{1,0:T(8,128)(2,1)S(1)}, u32[]{:S(2)}, u32[]{:S(2)}) collective-permute-start(bf16[512,1024]{1,0:T(8,128)(2,1)} %bitcast.14.grads), channel_id=1, source_target_pairs={{0,1},{1,0},{2,3},{3,2},{4,5},{5,4},{6,7},{7,6},{8,9},{9,8},{10,11... | collective-permute-start | bytes 3145736 | tf_op jit(solution)/shard_map/ppermute | solution.py:33
  57.5 10.7 %collective-permute-start.27 = (bf16[512,384]{1,0:T(8,128)(2,1)S(1)}, bf16[512,384]{1,0:T(8,128)(2,1)S(1)}, u32[]{:S(2)}, u32[]{:S(2)}) collective-permute-start(bf16[512,384]{1,0:T(8,128)(2,1)S(1)} %get-tuple-element.537.o0), channel_id=1, source_target_pairs={{0,2},{1,3},{2,0},{3,1},{4,6},{5,7},{6,4},{7,5},{8,10},{9,11},{10,... | collective-permute-start | bytes 1179656 | tf_op jit(solution)/shard_map/ppermute | solution.py:33
  59.0 20.9 %copy-start.13 = (bf16[512,640]{1,0:T(8,128)(2,1)}, bf16[512,640]{1,0:T(8,128)(2,1)S(1)}, u32[]{:S(2)}) copy-start(bf16[512,640]{1,0:T(8,128)(2,1)S(1)} %collective-permute-done.29.o2) | copy-start | bytes 1966084
  59.0 20.9 %collective-permute-start.30 = (bf16[512,640]{1,0:T(8,128)(2,1)S(1)}, bf16[512,640]{1,0:T(8,128)(2,1)}, u32[]{:S(2)}, u32[]{:S(2)}) collective-permute-start(bf16[512,640]{1,0:T(8,128)(2,1)S(1)} %collective-permute-done.29.o2), channel_id=1, source_target_pairs={{0,1},{1,0},{2,3},{3,2},{4,5},{5,4},{6,7},{7,6},{8,9},{9,8},{10,11... | collective-permute-start | bytes 1966088 | tf_op jit(solution)/shard_map/ppermute | solution.py:33
  68.2 7.3 %collective-permute-start.28 = (bf16[512,384]{1,0:T(8,128)(2,1)S(1)}, bf16[512,384]{1,0:T(8,128)(2,1)S(1)}, u32[]{:S(2)}, u32[]{:S(2)}) collective-permute-start(bf16[512,384]{1,0:T(8,128)(2,1)S(1)} %collective-permute-done.27.o2), channel_id=1, source_target_pairs={{0,1},{1,0},{2,3},{3,2},{4,5},{5,4},{6,7},{7,6},{8,9},{9,8},{10,11... | collective-permute-start | bytes 1179656 | tf_op jit(solution)/shard_map/ppermute | solution.py:33
  69.0 6.5 %copy-start.7 = (f32[1,512,1024]{2,1,0:T(8,128)S(1)}, f32[1,512,1024]{2,1,0:T(8,128)}, u32[]{:S(2)}) copy-start(f32[1,512,1024]{2,1,0:T(8,128)} %param.23) | copy-start | bytes 6291460
  80.2 13.1 %collective-permute-start.4 = (bf16[512,384]{1,0:T(8,128)(2,1)S(1)}, bf16[512,384]{1,0:T(8,128)(2,1)}, u32[]{:S(2)}, u32[]{:S(2)}) collective-permute-start(bf16[512,384]{1,0:T(8,128)(2,1)S(1)} %get-tuple-element.382), channel_id=1, source_target_pairs={{0,64},{4,68},{8,72},{12,76},{16,80},{20,84},{24,88},{28,92},{32,9... | collective-permute-start | bytes 1179656 | tf_op jit(solution)/shard_map/cond/branch_4_fun/ppermute | solution.py:38
  93.3 12.5 %collective-permute-start.33 = (bf16[256,512]{1,0:T(8,128)(2,1)S(1)}, bf16[256,512]{1,0:T(8,128)(2,1)S(1)}, u32[]{:S(2)}, u32[]{:S(2)}) collective-permute-start(bf16[256,512]{1,0:T(8,128)(2,1)S(1)} %get-tuple-element.545), channel_id=1, source_target_pairs={{0,1},{1,0},{2,3},{3,2},{4,5},{5,4},{6,7},{7,6},{8,9},{9,8},{10,11... | collective-permute-start | bytes 786440 | tf_op jit(solution)/shard_map/ppermute | solution.py:33
  93.9 15.0 %collective-permute-start.31 = (bf16[256,512]{1,0:T(8,128)(2,1)S(1)}, bf16[256,512]{1,0:T(8,128)(2,1)S(1)}, u32[]{:S(2)}, u32[]{:S(2)}) collective-permute-start(bf16[256,512]{1,0:T(8,128)(2,1)S(1)} %get-tuple-element.542), channel_id=1, source_target_pairs={{0,2},{1,3},{2,0},{3,1},{4,6},{5,7},{6,4},{7,5},{8,10},{9,11},{10,... | collective-permute-start | bytes 786440 | tf_op jit(solution)/shard_map/ppermute | solution.py:33
  94.9 14.0 %collective-permute-start.32 = (bf16[256,512]{1,0:T(8,128)(2,1)S(1)}, bf16[256,512]{1,0:T(8,128)(2,1)S(1)}, u32[]{:S(2)}, u32[]{:S(2)}) collective-permute-start(bf16[256,512]{1,0:T(8,128)(2,1)S(1)} %get-tuple-element.543), channel_id=1, source_target_pairs={{0,3},{1,2},{2,1},{3,0},{4,7},{5,6},{6,5},{7,4},{8,11},{9,10},{10,... | collective-permute-start | bytes 786440 | tf_op jit(solution)/shard_map/ppermute | solution.py:33
  98.3 7.5 %copy-start.6 = (f32[1,256,2048]{2,1,0:T(8,128)S(1)}, f32[1,256,2048]{2,1,0:T(8,128)}, u32[]{:S(2)}) copy-start(f32[1,256,2048]{2,1,0:T(8,128)} %param.22) | copy-start | bytes 6291460
  98.3 7.5 %copy-start.9 = (f32[1,256,2048]{2,1,0:T(8,128)S(1)}, f32[1,256,2048]{2,1,0:T(8,128)}, u32[]{:S(2)}) copy-start(f32[1,256,2048]{2,1,0:T(8,128)} %param.24) | copy-start | bytes 6291460
  98.3 7.5 %copy-start.10 = (f32[1,256,2048]{2,1,0:T(8,128)S(1)}, f32[1,256,2048]{2,1,0:T(8,128)}, u32[]{:S(2)}) copy-start(f32[1,256,2048]{2,1,0:T(8,128)} %param.26) | copy-start | bytes 6291460
  109.0 41.2 %collective-permute-start.19 = (bf16[512,640]{1,0:T(8,128)(2,1)S(1)}, bf16[512,640]{1,0:T(8,128)(2,1)S(1)}, u32[]{:S(2)}, u32[]{:S(2)}) collective-permute-start(bf16[512,640]{1,0:T(8,128)(2,1)S(1)} %get-tuple-element.491), channel_id=1, source_target_pairs={{0,64},{4,68},{8,72},{12,76},{16,80},{20,84},{24,88},{28,92},{32,9... | collective-permute-start | bytes 1966088 | tf_op jit(solution)/shard_map/cond/branch_4_fun/ppermute | solution.py:38
  112.0 25.8 %collective-permute-start.18 = (bf16[512,512]{1,0:T(8,128)(2,1)S(1)}, bf16[512,512]{1,0:T(8,128)(2,1)S(1)}, u32[]{:S(2)}, u32[]{:S(2)}) collective-permute-start(bf16[512,512]{1,0:T(8,128)(2,1)S(1)} %get-tuple-element.488), channel_id=1, source_target_pairs={{0,64},{4,68},{8,72},{12,76},{16,80},{20,84},{24,88},{28,92},{32,9... | collective-permute-start | bytes 1572872 | tf_op jit(solution)/shard_map/cond/branch_4_fun/ppermute | solution.py:38
  115.2 33.9 %collective-permute-start.17 = (bf16[512,512]{1,0:T(8,128)(2,1)S(1)}, bf16[512,512]{1,0:T(8,128)(2,1)S(1)}, u32[]{:S(2)}, u32[]{:S(2)}) collective-permute-start(bf16[512,512]{1,0:T(8,128)(2,1)S(1)} %get-tuple-element.486), channel_id=1, source_target_pairs={{0,64},{4,68},{8,72},{12,76},{16,80},{20,84},{24,88},{28,92},{32,9... | collective-permute-start | bytes 1572872 | tf_op jit(solution)/shard_map/cond/branch_4_fun/ppermute | solution.py:38
  (9 other events, 28.0 us)

commit v5 on v2

--- a/solution.py
+++ b/solution.py
@@ -8,7 +8,7 @@
 from jax.sharding import PartitionSpec as P
 
 
-WIDTHS = (512, 512)
+WIDTHS = (384, 640)
 STARTS = tuple(sum(WIDTHS[:c]) for c in range(len(WIDTHS)))
 CHUNKS = len(WIDTHS)
 LOW = jnp.bfloat16
@@ -76,7 +76,23 @@
     )(place, up, *after)
 
 
-def norm_kernel(tokens, grads, _, normed, *pieces):
+def pieces_kernel(grads, *refs):
+    for c, piece in enumerate(refs[-CHUNKS:]):
+        piece[...] = grads[:, STARTS[c] : STARTS[c] + WIDTHS[c]]
+
+
+def pieces(grads, *after):
+    return pl.pallas_call(
+        pieces_kernel,
+        out_shape=[shape(grads.shape[0], width) for width in WIDTHS],
+        in_specs=[VMEM] + [ANY] * len(after),
+        out_specs=[VMEM] * CHUNKS,
+        compiler_params=params(),
+        name="pieces",
+    )(grads, *after)
+
+
+def norm_kernel(tokens, _, normed):
     step = 64
 
     def rows(i, _):
@@ -85,23 +101,20 @@
         centered = wide - jnp.mean(wide, axis=1, keepdims=True)
         spread = jnp.mean(centered * centered, axis=1, keepdims=True)
         normed[at, :] = (centered * lax.rsqrt(spread + 1e-05)).astype(LOW)
-        for c, piece in enumerate(pieces):
-            piece[at, :] = grads[at, STARTS[c] : STARTS[c] + WIDTHS[c]]
         return 0
 
     lax.fori_loop(0, tokens.shape[0] // step, rows, 0)
 
 
-def norm(tokens, grads, after):
-    rows, cols = tokens.shape
+def norm(tokens, after):
     return pl.pallas_call(
         norm_kernel,
-        out_shape=[shape(rows, cols)] + [shape(rows, width) for width in WIDTHS],
-        in_specs=[VMEM] * 2 + [ANY],
-        out_specs=[VMEM] * (1 + CHUNKS),
+        out_shape=shape(*tokens.shape),
+        in_specs=[VMEM, ANY],
+        out_specs=VMEM,
         compiler_params=params(),
         name="norm",
-    )(tokens, grads, after)
+    )(tokens, after)
 
 
 def hidden_kernel(place, u0, u1, u2, u3, left, right, act, slope, up, both):
@@ -204,9 +217,9 @@
 
 
 def back_kernel(place, param, sa, sb, *refs):
-    ogs, side, outs = refs[: 3 * CHUNKS], refs[3 * CHUNKS], refs[-6:-2]
+    ogs, side, outs = refs[: 3 * CHUNKS], refs[3 * CHUNKS], refs[-4:-2]
     normed = refs[3 * CHUNKS + 1 : 3 * CHUNKS + 5]
-    low, pre_grad = refs[-2:]
+    pre_grad, low = refs[-2:]
     rows = normed[0].shape[0]
     low[...] = param[...].astype(LOW)
     for k in range(4):
@@ -218,14 +231,35 @@
             got = part if got is None else got + part
         slope = (sa, sb)[k // 2][(k % 2) * rows : (k % 2 + 1) * rows, :]
         pre_grad[k * rows : (k + 1) * rows, :] = (got * slope).astype(LOW)
+    blocks(place, (2, 3), normed, pre_grad, outs)
+
+
+def blocks(place, masks, normed, pre_grad, outs):
+    rows = normed[0].shape[0]
     size = outs[0].shape[0]
-    for k in range(4):
+    for k, out in zip(masks, outs):
         at = pl.ds(pl.multiple_of((place[0] ^ k) * size, size), size)
         total = None
         for j in range(4):
             part = dot(normed[j][:, at], pre_grad[j * rows : (j + 1) * rows, :], ((0,), (0,)))
             total = part if total is None else total + part
-        outs[k][...] = total.astype(LOW)
+        out[...] = total.astype(LOW)
+
+
+def rest_kernel(place, *refs):
+    blocks(place, (0, 1), refs[:4], refs[4], refs[5:])
+
+
+def rest_of_back(place, normed, pre_grad):
+    size, hidden_size = normed[0].shape[1] // 4, pre_grad.shape[1]
+    return pl.pallas_call(
+        rest_kernel,
+        out_shape=[shape(size, hidden_size)] * 2,
+        in_specs=[SMEM] + [VMEM] * 5,
+        out_specs=[VMEM] * 2,
+        compiler_params=params(),
+        name="rest",
+    )(place, *normed, pre_grad)
 
 
 def back(place, param, slopes, own, side, far, last, normed):
@@ -233,10 +267,10 @@
     rows, full = normed[0].shape
     return pl.pallas_call(
         back_kernel,
-        out_shape=[shape(full // 4, hidden_size)] * 4,
+        out_shape=[shape(full // 4, hidden_size)] * 2 + [shape(4 * rows, hidden_size)],
         in_specs=[SMEM] + [VMEM] * (3 + 3 * CHUNKS + 5),
-        out_specs=[VMEM] * 4,
-        scratch_shapes=[pltpu.VMEM(param.shape, LOW), pltpu.VMEM((4 * rows, hidden_size), LOW)],
+        out_specs=[VMEM] * 3,
+        scratch_shapes=[pltpu.VMEM(param.shape, LOW)],
         compiler_params=params(),
         name="back",
     )(place, param, *slopes, *own, *far, *last, side, *normed)
@@ -364,11 +398,12 @@
 
 
 def prepare(place, fixes, level, tokens, grads, up_p, down_p, up_m, down_m, up_v, down_v):
-    first = cut(place, up_p, fixes, level)
+    own = pieces(grads, fixes, level)
+    first = cut(place, up_p, own[0])
     ups = [first[0]]
     for k in range(1, 4):
         ups.append(swap(first[k], k))
-    n0, *own = norm(tokens, grads, first[0])
+    n0 = norm(tokens, first[0])
     n2 = swap(n0, 2)
     n1 = swap(n0, 1)
     side = swap(grads, 1)
@@ -385,9 +420,11 @@
     for c in range(CHUNKS - 1):
         ogs = (own[c], side, far[c], last[c])
         news = down(c, fixes, *acts, ogs, down_p, down_m, down_v, news, n0)
-    g0, g1, g2, g3 = back(place, down_p, slopes, own, side, far, last, (n0, n1, n2, n3))
+    normed = (n0, n1, n2, n3)
+    g2, g3, pre_grad = back(place, down_p, slopes, own, side, far, last, normed)
     g2 = swap(g2, 2)
     g3 = swap(g3, 3)
+    g0, g1 = rest_of_back(place, normed, pre_grad)
     g1 = swap(g1, 1)
     c = CHUNKS - 1
     ogs = (own[c], side, far[c], last[c])

time: 150 us -> 154 us (1.027)
  waiting for transfers between devices: 84.4 us -> 89.6 us
  starting transfers between devices: 23.6 us -> 20.8 us
    ppermute x14, waiting for transfers between devices: 45.5 us -> 50.8 us  [swap(): return lax.ppermute(array, 'zero', [(i, i ^ mask) for i in range(size)])]
    ppermute x14, starting transfers between devices: 17.1 us -> 14.2 us  [swap(): return lax.ppermute(array, 'zero', [(i, i ^ mask) for i in range(size)])]
    pallas_call x2 -> x4, Pallas kernels: 6.29 us -> 7.12 us  [the longest x1 4.06 us: back(): pl.pallas_call(back_kernel, out_shape=[shape(full // 4, hidden_size)] * 2...]
  transfers between devices with their start and end apart: 17 -> 17, of which waited for: 6 -> 6; matrix products, arithmetic and copies ran while one was open for 0% -> 0% of each run, Pallas kernels for 17% -> 16%
where the time goes in v5:
time: 154 us
  waiting for transfers between devices  89.6 us (58%)
  Pallas kernels  39.5 us (26%)
  starting transfers between devices  20.8 us (14%)
  local copies, waits for them, and re-layouts  2.26 us (1%)
  between operations  1.62 us (1%)
    ppermute x14, waiting for transfers between devices, swap(): return lax.ppermute(array, 'zero', [(i, i ^ mask) for i in range(size)])  50.8 us
    ppermute x3, waiting for transfers between devices, from_partner(): lax.ppermute(array, 'peer', [(i, (i - by) % size) for i in range(size)])  38.8 us
    ppermute x14, starting transfers between devices, swap(): return lax.ppermute(array, 'zero', [(i, i ^ mask) for i in range(size)])  14.2 us
    pallas_call x2, Pallas kernels, down(): pl.pallas_call(partial(down_kernel, c), out_shape=[shape(rows, cols, dtyp...  10.5 us
    ppermute x3, starting transfers between devices, from_partner(): lax.ppermute(array, 'peer', [(i, (i - by) % size) for i in range(size)])  6.55 us
    pallas_call x2, Pallas kernels, hidden(): pl.pallas_call(hidden_kernel, out_shape=[shape(width, 2 * rows), shape(2...  6.4 us
    pallas_call x2, Pallas kernels, up(): pl.pallas_call(partial(up_kernel, base), in_specs=in_specs, out_specs=[VM...  6.12 us
    pallas_call x1, Pallas kernels, mean_down(): pl.pallas_call(mean_down_kernel, grid=(8,), out_shape=shape(rows, cols, d...  5.43 us
  transfers between devices with their start and end apart: 17, of which 6 were waited for; matrix products, arithmetic and copies ran while one was open for 0% of the time, Pallas kernels for 16%

profile of v5, /device:TPU:1, one launch (start us, length us, event | category | flops | bytes accessed | tf_op | source)
XLA Modules:
  0.0 154.0 jit_solution(10147580362581169766)
XLA Ops:
  2.8 1.9 %cut.1 = (bf16[256,512]{1,0:T(8,128)(2,1)S(1)}, bf16[256,512]{1,0:T(8,128)(2,1)S(1)}, bf16[256,512]{1,0:T(8,128)(2,1)S(1)}, bf16[256,512]{1,0:T(8,128)(2,1)S(1)}) custom-call(s32[1]{0:T(128)} %bitcast.11.place, f32[256,2048]{1,0:T(8,128)} %bitcast.34, bf16[512,384]{1,0:T(8,128)(2,1)S(1)} %get-tuple-element.254.refs_0_.o0), custom_call_target="tpu_custom_call" | custom-call | tf_op jit(solution)/shard_map/cut/pallas_call | solution.py:69
  4.7 1.7 %norm.1.left.refs_7_.refs_0_.rest_0_ = bf16[512,1024]{1,0:T(8,128)(2,1)S(1)} custom-call(bf16[512,1024]{1,0:T(8,128)(2,1)S(1)} %bitcast.33, bf16[256,512]{1,0:T(8,128)(2,1)S(1)} %get-tuple-element.255._.u0), custom_call_target="tpu_custom_call" | custom-call | tf_op jit(solution)/shard_map/norm/pallas_call | solution.py:110
  6.4 2.5 %collective-permute-start.19 = (bf16[512,1024]{1,0:T(8,128)(2,1)S(1)}, bf16[512,1024]{1,0:T(8,128)(2,1)S(1)}, u32[]{:S(2)}, u32[]{:S(2)}) collective-permute-start(bf16[512,1024]{1,0:T(8,128)(2,1)S(1)} %norm.1.left.refs_7_.refs_0_.rest_0_), channel_id=1, source_target_pairs={{0,2},{1,3},{2,0},{3,1},{4,6},{5,7},{6,4},{7,5},{8,10},{9,11},{10,... | collective-permute-start | bytes 3145736 | tf_op jit(solution)/shard_map/ppermute | solution.py:33
  9.8 1.5 collective-permute-start.22
  11.9 19.9 %collective-permute-done.19.left.refs_9_.refs_2_ = bf16[512,1024]{1,0:T(8,128)(2,1)S(1)} collective-permute-done((bf16[512,1024]{1,0:T(8,128)(2,1)S(1)}, bf16[512,1024]{1,0:T(8,128)(2,1)S(1)}, u32[]{:S(2)}, u32[]{:S(2)}) %collective-permute-start.19) | collective-permute-done | bytes 1048608 | tf_op jit(solution)/shard_map/ppermute | solution.py:33
  31.8 2.1 %collective-permute-start.20 = (bf16[512,1024]{1,0:T(8,128)(2,1)S(1)}, bf16[512,1024]{1,0:T(8,128)(2,1)S(1)}, u32[]{:S(2)}, u32[]{:S(2)}) collective-permute-start(bf16[512,1024]{1,0:T(8,128)(2,1)S(1)} %collective-permute-done.19.left.refs_9_.refs_2_), channel_id=1, source_target_pairs={{0,1},{1,0},{2,3},{3,2},{4,5},{5,4},{6,7},{7,6},{8,9},{9,8},{10,11... | collective-permute-start | bytes 3145736 | tf_op jit(solution)/shard_map/ppermute | solution.py:33
  33.9 3.5 %collective-permute-done.16.u2 = bf16[256,512]{1,0:T(8,128)(2,1)S(1)} collective-permute-done((bf16[256,512]{1,0:T(8,128)(2,1)S(1)}, bf16[256,512]{1,0:T(8,128)(2,1)S(1)}, u32[]{:S(2)}, u32[]{:S(2)}) %collective-permute-start.16) | collective-permute-done | bytes 262176 | tf_op jit(solution)/shard_map/ppermute | solution.py:33
  37.4 2.1 %collective-permute-start.25 = (bf16[512,1024]{1,0:T(8,128)(2,1)S(1)}, bf16[512,1024]{1,0:T(8,128)(2,1)S(1)}, u32[]{:S(2)}, u32[]{:S(2)}) collective-permute-start(bf16[512,1024]{1,0:T(8,128)(2,1)S(1)} %bitcast.32), channel_id=1, source_target_pairs={{0,1},{1,0},{2,3},{3,2},{4,5},{5,4},{6,7},{7,6},{8,9},{9,8},{10,11... | collective-permute-start | bytes 3145736 | tf_op jit(solution)/shard_map/ppermute | solution.py:33
  39.5 18.1 %collective-permute-done.17.u3 = bf16[256,512]{1,0:T(8,128)(2,1)S(1)} collective-permute-done((bf16[256,512]{1,0:T(8,128)(2,1)S(1)}, bf16[256,512]{1,0:T(8,128)(2,1)S(1)}, u32[]{:S(2)}, u32[]{:S(2)}) %collective-permute-start.17) | collective-permute-done | bytes 262176 | tf_op jit(solution)/shard_map/ppermute | solution.py:33
  59.1 9.3 %collective-permute-done.21.refs_2_.o2 = bf16[512,384]{1,0:T(8,128)(2,1)S(1)} collective-permute-done((bf16[512,384]{1,0:T(8,128)(2,1)S(1)}, bf16[512,384]{1,0:T(8,128)(2,1)S(1)}, u32[]{:S(2)}, u32[]{:S(2)}) %collective-permute-start.21) | collective-permute-done | bytes 393248 | tf_op jit(solution)/shard_map/ppermute | solution.py:33
  69.1 3.2 %hidden.2 = (bf16[512,1024]{1,0:T(8,128)(2,1)S(1)}, f32[1024,512]{1,0:T(8,128)S(1)}) custom-call(s32[1]{0:T(128)} %bitcast.11.place, bf16[256,512]{1,0:T(8,128)(2,1)S(1)} %get-tuple-element.255._.u0, bf16[256,512]{1,0:T(8,128)(2,1)S(1)} %collective-permute-done.15.u1, bf16[256,512]{1,0:T(8,128)(2,1)S(1)} %collective-permute-done.16.u2, ...), custom_call_target="tpu_custom_call" | custom-call | tf_op jit(solution)/shard_map/hidden/pallas_call | solution.py:147
  72.4 3.2 %hidden.3 = (bf16[512,1024]{1,0:T(8,128)(2,1)S(1)}, f32[1024,512]{1,0:T(8,128)S(1)}) custom-call(s32[1]{0:T(128)} %bitcast.11.place, bf16[256,512]{1,0:T(8,128)(2,1)S(1)} %get-tuple-element.255._.u0, bf16[256,512]{1,0:T(8,128)(2,1)S(1)} %collective-permute-done.15.u1, bf16[256,512]{1,0:T(8,128)(2,1)S(1)} %collective-permute-done.16.u2, ...), custom_call_target="tpu_custom_call" | custom-call | tf_op jit(solution)/shard_map/hidden/pallas_call | solution.py:147
  75.6 4.1 %back.1 = (bf16[256,512]{1,0:T(8,128)(2,1)S(1)}, bf16[256,512]{1,0:T(8,128)(2,1)S(1)}, bf16[2048,512]{1,0:T(8,128)(2,1)S(1)}) custom-call(s32[1]{0:T(128)} %bitcast.11.place, f32[512,1024]{1,0:T(8,128)S(1)} %bitcast.24, f32[1024,512]{1,0:T(8,128)S(1)} %get-tuple-element.259.sa, f32[1024,512]{1,0:T(8,128)S(1)} %get-tuple-element.260.sb, ...), custom_call_target="tpu_custom_call" | custom-call | tf_op jit(solution)/shard_map/back/pallas_call | solution.py:268
  81.1 1.5 collective-permute-start.26
  83.2 4.3 %down.2 = (f32[512,1024]{1,0:T(8,128)}, bf16[512,1024]{1,0:T(8,128)(2,1)S(1)}, f32[512,1024]{1,0:T(8,128)}, f32[512,1024]{1,0:T(8,128)}) custom-call(f32[2]{0:T(128)S(1)} %pad_maximum_fusion.refs_0_.fixes, bf16[512,1024]{1,0:T(8,128)(2,1)S(1)} %get-tuple-element.271.near, bf16[512,1024]{1,0:T(8,128)(2,1)S(1)} %get-tuple-element.272.far, ...), custom_call_target="tpu_custom_call" | custom-call | tf_op jit(solution)/shard_map/down/pallas_call | solution.py:206
  87.6 6.2 %down.3 = (f32[512,1024]{1,0:T(8,128)}, bf16[512,1024]{1,0:T(8,128)(2,1)S(1)}, f32[512,1024]{1,0:T(8,128)}, f32[512,1024]{1,0:T(8,128)}) custom-call(f32[2]{0:T(128)S(1)} %pad_maximum_fusion.refs_0_.fixes, bf16[512,1024]{1,0:T(8,128)(2,1)S(1)} %get-tuple-element.271.near, ...), custom_call_target="tpu_custom_call", output_to_operand_aliasing={{0}: (11, {}), {1}: (12, {}), {2}: (13, {}), {3}: (14, {})} | custom-call | tf_op jit(solution)/shard_map/down/pallas_call | solution.py:206
  93.9 3.1 %up.11 = (f32[512,512]{1,0:T(8,128)S(1)}, bf16[512,512]{1,0:T(8,128)(2,1)S(1)}, f32[256,2048]{1,0:T(8,128)}, f32[256,2048]{1,0:T(8,128)}) custom-call(s32[1]{0:T(128)} %bitcast.11.place, f32[2]{0:T(128)S(1)} %pad_maximum_fusion.refs_0_.fixes, bf16[256,512]{1,0:T(8,128)(2,1)S(1)} %get-tuple-element.265.left.rest_0_, ...), custom_call_target="tpu_custom_call" | custom-call | tf_op jit(solution)/shard_map/up/pallas_call | solution.py:330
  96.9 57.0 %conditional.1 = (f32[256,2048]{1,0:T(8,128)}, f32[256,2048]{1,0:T(8,128)}, f32[1,256,2048]{2,1,0:T(8,128)}, f32[1,512,1024]{2,1,0:T(8,128)}) conditional(s32[]{:T(128)} %bitcast.10, (s32[1]{0:T(128)}, f32[2]{0:T(128)S(1)}, bf16[256,512]{1,0:T(8,128)(2,1)S(1)}, bf16[256,512]{1,0:T(8,128)(2,1)S(1)}, ...), branch_computations={%region_0.1_spmd, %region_1.2_spmd, %region_2.3_spmd, %region_3.4_... | conditional | bytes 20971728 | solution.py:463
  97.0 3.5 %collective-permute-start.14 = (bf16[512,1024]{1,0:T(8,128)(2,1)S(1)}, bf16[512,1024]{1,0:T(8,128)(2,1)S(1)}, u32[]{:S(2)}, u32[]{:S(2)}) collective-permute-start(bf16[512,1024]{1,0:T(8,128)(2,1)S(1)} %get-tuple-element.216), channel_id=1, source_target_pairs={{0,64},{4,68},{8,72},{12,76},{16,80},{20,84},{24,88},{28,92},{32,9... | collective-permute-start | bytes 3145736 | tf_op jit(solution)/shard_map/cond/branch_4_fun/ppermute | solution.py:38
  100.6 3.1 %up.10 = (f32[512,512]{1,0:T(8,128)S(1)}, bf16[512,512]{1,0:T(8,128)(2,1)S(1)}, f32[256,2048]{1,0:T(8,128)}, f32[256,2048]{1,0:T(8,128)}) custom-call(s32[1]{0:T(128)} %get-tuple-element.200.place, f32[2]{0:T(128)S(1)} %get-tuple-element.201.fixes, bf16[256,512]{1,0:T(8,128)(2,1)S(1)} %get-tuple-element.202.left, ...), custom_call_target="tpu_custom_call", output_to_operand_aliasing={{2}: (7, {}), {3}: (8, {})} | custom-call | tf_op jit(solution)/shard_map/cond/branch_4_fun/up/pallas_call | solution.py:330
  103.7 3.0 %collective-permute-start.12 = (bf16[512,512]{1,0:T(8,128)(2,1)S(1)}, bf16[512,512]{1,0:T(8,128)(2,1)S(1)}, u32[]{:S(2)}, u32[]{:S(2)}) collective-permute-start(bf16[512,512]{1,0:T(8,128)(2,1)S(1)} %get-tuple-element.212), channel_id=1, source_target_pairs={{0,64},{4,68},{8,72},{12,76},{16,80},{20,84},{24,88},{28,92},{32,9... | collective-permute-start | bytes 1572872 | tf_op jit(solution)/shard_map/cond/branch_4_fun/ppermute | solution.py:38
  106.6 28.6 %collective-permute-done.13.other = bf16[512,512]{1,0:T(8,128)(2,1)S(1)} collective-permute-done((bf16[512,512]{1,0:T(8,128)(2,1)S(1)}, bf16[512,512]{1,0:T(8,128)(2,1)S(1)}, u32[]{:S(2)}, u32[]{:S(2)}) %collective-permute-start.13) | collective-permute-done | bytes 524320 | tf_op jit(solution)/shard_map/cond/branch_4_fun/ppermute | solution.py:38
  136.3 10.2 %collective-permute-done.12.other = bf16[512,512]{1,0:T(8,128)(2,1)S(1)} collective-permute-done((bf16[512,512]{1,0:T(8,128)(2,1)S(1)}, bf16[512,512]{1,0:T(8,128)(2,1)S(1)}, u32[]{:S(2)}, u32[]{:S(2)}) %collective-permute-start.12) | collective-permute-done | bytes 524320 | tf_op jit(solution)/shard_map/cond/branch_4_fun/ppermute | solution.py:38
  148.5 5.4 %mean_down.9 = f32[512,1024]{1,0:T(8,128)} custom-call(f32[512,1024]{1,0:T(8,128)S(1)} %copy-done.11, bf16[512,1024]{1,0:T(8,128)(2,1)} %copy-done.18), custom_call_target="tpu_custom_call" | custom-call | tf_op jit(solution)/shard_map/cond/branch_4_fun/mean_down/pallas_call | solution.py:355
  (48 shorter events, 10.4 us)
Async XLA Ops:
  2.8 34.6 %copy-start.4 = (bf16[1,512,1024]{2,1,0:T(8,128)(2,1)S(1)}, bf16[1,512,1024]{2,1,0:T(8,128)(2,1)}, u32[]{:S(2)}) copy-start(bf16[1,512,1024]{2,1,0:T(8,128)(2,1)} %param.15) | copy-start | bytes 3145732
  6.4 25.4 %collective-permute-start.19 = (bf16[512,1024]{1,0:T(8,128)(2,1)S(1)}, bf16[512,1024]{1,0:T(8,128)(2,1)S(1)}, u32[]{:S(2)}, u32[]{:S(2)}) collective-permute-start(bf16[512,1024]{1,0:T(8,128)(2,1)S(1)} %norm.1.left.refs_7_.refs_0_.rest_0_), channel_id=1, source_target_pairs={{0,2},{1,3},{2,0},{3,1},{4,6},{5,7},{6,4},{7,5},{8,10},{9,11},{10,... | collective-permute-start | bytes 3145736 | tf_op jit(solution)/shard_map/ppermute | solution.py:33
  8.9 3.0 %collective-permute-start.15 = (bf16[256,512]{1,0:T(8,128)(2,1)S(1)}, bf16[256,512]{1,0:T(8,128)(2,1)S(1)}, u32[]{:S(2)}, u32[]{:S(2)}) collective-permute-start(bf16[256,512]{1,0:T(8,128)(2,1)S(1)} %get-tuple-element.256), channel_id=1, source_target_pairs={{0,1},{1,0},{2,3},{3,2},{4,5},{5,4},{6,7},{7,6},{8,9},{9,8},{10,11... | collective-permute-start | bytes 786440 | tf_op jit(solution)/shard_map/ppermute | solution.py:33
  9.8 27.5 %collective-permute-start.16 = (bf16[256,512]{1,0:T(8,128)(2,1)S(1)}, bf16[256,512]{1,0:T(8,128)(2,1)S(1)}, u32[]{:S(2)}, u32[]{:S(2)}) collective-permute-start(bf16[256,512]{1,0:T(8,128)(2,1)S(1)} %get-tuple-element.257), channel_id=1, source_target_pairs={{0,2},{1,3},{2,0},{3,1},{4,6},{5,7},{6,4},{7,5},{8,10},{9,11},{10,... | collective-permute-start | bytes 786440 | tf_op jit(solution)/shard_map/ppermute | solution.py:33
  9.8 49.2 %collective-permute-start.22 = (bf16[512,640]{1,0:T(8,128)(2,1)S(1)}, bf16[512,640]{1,0:T(8,128)(2,1)S(1)}, u32[]{:S(2)}, u32[]{:S(2)}) collective-permute-start(bf16[512,640]{1,0:T(8,128)(2,1)S(1)} %get-tuple-element.261.refs_1_.o0), channel_id=1, source_target_pairs={{0,2},{1,3},{2,0},{3,1},{4,6},{5,7},{6,4},{7,5},{8,10},{9,11},{10,... | collective-permute-start | bytes 1966088 | tf_op jit(solution)/shard_map/ppermute | solution.py:33
  11.3 57.8 %collective-permute-start.18 = (bf16[512,1024]{1,0:T(8,128)(2,1)S(1)}, bf16[512,1024]{1,0:T(8,128)(2,1)S(1)}, u32[]{:S(2)}, u32[]{:S(2)}) collective-permute-start(bf16[512,1024]{1,0:T(8,128)(2,1)S(1)} %norm.1.left.refs_7_.refs_0_.rest_0_), channel_id=1, source_target_pairs={{0,1},{1,0},{2,3},{3,2},{4,5},{5,4},{6,7},{7,6},{8,9},{9,8},{10,11... | collective-permute-start | bytes 3145736 | tf_op jit(solution)/shard_map/ppermute | solution.py:33
  11.9 45.7 %collective-permute-start.17 = (bf16[256,512]{1,0:T(8,128)(2,1)S(1)}, bf16[256,512]{1,0:T(8,128)(2,1)S(1)}, u32[]{:S(2)}, u32[]{:S(2)}) collective-permute-start(bf16[256,512]{1,0:T(8,128)(2,1)S(1)} %get-tuple-element.258), channel_id=1, source_target_pairs={{0,3},{1,2},{2,1},{3,0},{4,7},{5,6},{6,5},{7,4},{8,11},{9,10},{10,... | collective-permute-start | bytes 786440 | tf_op jit(solution)/shard_map/ppermute | solution.py:33
  31.8 40.6 %collective-permute-start.20 = (bf16[512,1024]{1,0:T(8,128)(2,1)S(1)}, bf16[512,1024]{1,0:T(8,128)(2,1)S(1)}, u32[]{:S(2)}, u32[]{:S(2)}) collective-permute-start(bf16[512,1024]{1,0:T(8,128)(2,1)S(1)} %collective-permute-done.19.left.refs_9_.refs_2_), channel_id=1, source_target_pairs={{0,1},{1,0},{2,3},{3,2},{4,5},{5,4},{6,7},{7,6},{8,9},{9,8},{10,11... | collective-permute-start | bytes 3145736 | tf_op jit(solution)/shard_map/ppermute | solution.py:33
  37.4 38.2 %collective-permute-start.25 = (bf16[512,1024]{1,0:T(8,128)(2,1)S(1)}, bf16[512,1024]{1,0:T(8,128)(2,1)S(1)}, u32[]{:S(2)}, u32[]{:S(2)}) collective-permute-start(bf16[512,1024]{1,0:T(8,128)(2,1)S(1)} %bitcast.32), channel_id=1, source_target_pairs={{0,1},{1,0},{2,3},{3,2},{4,5},{5,4},{6,7},{7,6},{8,9},{9,8},{10,11... | collective-permute-start | bytes 3145736 | tf_op jit(solution)/shard_map/ppermute | solution.py:33
  57.6 10.7 %collective-permute-start.21 = (bf16[512,384]{1,0:T(8,128)(2,1)S(1)}, bf16[512,384]{1,0:T(8,128)(2,1)S(1)}, u32[]{:S(2)}, u32[]{:S(2)}) collective-permute-start(bf16[512,384]{1,0:T(8,128)(2,1)S(1)} %get-tuple-element.254.refs_0_.o0), channel_id=1, source_target_pairs={{0,2},{1,3},{2,0},{3,1},{4,6},{5,7},{6,4},{7,5},{8,10},{9,11},{10,... | collective-permute-start | bytes 1179656 | tf_op jit(solution)/shard_map/ppermute | solution.py:33
  59.1 16.5 %collective-permute-start.24 = (bf16[512,640]{1,0:T(8,128)(2,1)S(1)}, bf16[512,640]{1,0:T(8,128)(2,1)S(1)}, u32[]{:S(2)}, u32[]{:S(2)}) collective-permute-start(bf16[512,640]{1,0:T(8,128)(2,1)S(1)} %collective-permute-done.22.refs_3_.o2), channel_id=1, source_target_pairs={{0,1},{1,0},{2,3},{3,2},{4,5},{5,4},{6,7},{7,6},{8,9},{9,8},{10,11... | collective-permute-start | bytes 1966088 | tf_op jit(solution)/shard_map/ppermute | solution.py:33
  68.3 7.3 %collective-permute-start.23 = (bf16[512,384]{1,0:T(8,128)(2,1)S(1)}, bf16[512,384]{1,0:T(8,128)(2,1)S(1)}, u32[]{:S(2)}, u32[]{:S(2)}) collective-permute-start(bf16[512,384]{1,0:T(8,128)(2,1)S(1)} %collective-permute-done.21.refs_2_.o2), channel_id=1, source_target_pairs={{0,1},{1,0},{2,3},{3,2},{4,5},{5,4},{6,7},{7,6},{8,9},{9,8},{10,11... | collective-permute-start | bytes 1179656 | tf_op jit(solution)/shard_map/ppermute | solution.py:33
  72.3 3.3 %copy-start = (f32[1,512,1024]{2,1,0:T(8,128)S(1)}, f32[1,512,1024]{2,1,0:T(8,128)}, u32[]{:S(2)}) copy-start(f32[1,512,1024]{2,1,0:T(8,128)} %param.18) | copy-start | bytes 6291460
  79.7 3.6 %copy-start.1 = (f32[1,512,1024]{2,1,0:T(8,128)S(1)}, f32[1,512,1024]{2,1,0:T(8,128)}, u32[]{:S(2)}) copy-start(f32[1,512,1024]{2,1,0:T(8,128)} %param.20) | copy-start | bytes 6291460
  79.7 3.6 %copy-start.2 = (f32[1,512,1024]{2,1,0:T(8,128)S(1)}, f32[1,512,1024]{2,1,0:T(8,128)}, u32[]{:S(2)}) copy-start(f32[1,512,1024]{2,1,0:T(8,128)} %param.22) | copy-start | bytes 6291460
  81.0 12.8 %collective-permute-start.28 = (bf16[256,512]{1,0:T(8,128)(2,1)S(1)}, bf16[256,512]{1,0:T(8,128)(2,1)S(1)}, u32[]{:S(2)}, u32[]{:S(2)}) collective-permute-start(bf16[256,512]{1,0:T(8,128)(2,1)S(1)} %get-tuple-element.266), channel_id=1, source_target_pairs={{0,1},{1,0},{2,3},{3,2},{4,5},{5,4},{6,7},{7,6},{8,9},{9,8},{10,11... | collective-permute-start | bytes 786440 | tf_op jit(solution)/shard_map/ppermute | solution.py:33
  81.1 15.8 %collective-permute-start.26 = (bf16[256,512]{1,0:T(8,128)(2,1)S(1)}, bf16[256,512]{1,0:T(8,128)(2,1)S(1)}, u32[]{:S(2)}, u32[]{:S(2)}) collective-permute-start(bf16[256,512]{1,0:T(8,128)(2,1)S(1)} %get-tuple-element.262), channel_id=1, source_target_pairs={{0,2},{1,3},{2,0},{3,1},{4,6},{5,7},{6,4},{7,5},{8,10},{9,11},{10,... | collective-permute-start | bytes 786440 | tf_op jit(solution)/shard_map/ppermute | solution.py:33
  82.6 14.3 %collective-permute-start.27 = (bf16[256,512]{1,0:T(8,128)(2,1)S(1)}, bf16[256,512]{1,0:T(8,128)(2,1)S(1)}, u32[]{:S(2)}, u32[]{:S(2)}) collective-permute-start(bf16[256,512]{1,0:T(8,128)(2,1)S(1)} %get-tuple-element.263), channel_id=1, source_target_pairs={{0,3},{1,2},{2,1},{3,0},{4,7},{5,6},{6,5},{7,4},{8,11},{9,10},{10,... | collective-permute-start | bytes 786440 | tf_op jit(solution)/shard_map/ppermute | solution.py:33
  87.5 6.3 %copy-start.6 = (f32[1,256,2048]{2,1,0:T(8,128)S(1)}, f32[1,256,2048]{2,1,0:T(8,128)}, u32[]{:S(2)}) copy-start(f32[1,256,2048]{2,1,0:T(8,128)} %param.17) | copy-start | bytes 6291460
  87.6 6.3 %copy-start.12 = (f32[1,256,2048]{2,1,0:T(8,128)S(1)}, f32[1,256,2048]{2,1,0:T(8,128)}, u32[]{:S(2)}) copy-start(f32[1,256,2048]{2,1,0:T(8,128)} %param.19) | copy-start | bytes 6291460
  87.6 6.3 %copy-start.13 = (f32[1,256,2048]{2,1,0:T(8,128)S(1)}, f32[1,256,2048]{2,1,0:T(8,128)}, u32[]{:S(2)}) copy-start(f32[1,256,2048]{2,1,0:T(8,128)} %param.21) | copy-start | bytes 6291460
  97.0 50.6 %collective-permute-start.14 = (bf16[512,1024]{1,0:T(8,128)(2,1)S(1)}, bf16[512,1024]{1,0:T(8,128)(2,1)S(1)}, u32[]{:S(2)}, u32[]{:S(2)}) collective-permute-start(bf16[512,1024]{1,0:T(8,128)(2,1)S(1)} %get-tuple-element.216), channel_id=1, source_target_pairs={{0,64},{4,68},{8,72},{12,76},{16,80},{20,84},{24,88},{28,92},{32,9... | collective-permute-start | bytes 3145736 | tf_op jit(solution)/shard_map/cond/branch_4_fun/ppermute | solution.py:38
  100.5 34.8 %collective-permute-start.13 = (bf16[512,512]{1,0:T(8,128)(2,1)S(1)}, bf16[512,512]{1,0:T(8,128)(2,1)S(1)}, u32[]{:S(2)}, u32[]{:S(2)}) collective-permute-start(bf16[512,512]{1,0:T(8,128)(2,1)S(1)} %get-tuple-element.214), channel_id=1, source_target_pairs={{0,64},{4,68},{8,72},{12,76},{16,80},{20,84},{24,88},{28,92},{32,9... | collective-permute-start | bytes 1572872 | tf_op jit(solution)/shard_map/cond/branch_4_fun/ppermute | solution.py:38
  103.7 42.8 %collective-permute-start.12 = (bf16[512,512]{1,0:T(8,128)(2,1)S(1)}, bf16[512,512]{1,0:T(8,128)(2,1)S(1)}, u32[]{:S(2)}, u32[]{:S(2)}) collective-permute-start(bf16[512,512]{1,0:T(8,128)(2,1)S(1)} %get-tuple-element.212), channel_id=1, source_target_pairs={{0,64},{4,68},{8,72},{12,76},{16,80},{20,84},{24,88},{28,92},{32,9... | collective-permute-start | bytes 1572872 | tf_op jit(solution)/shard_map/cond/branch_4_fun/ppermute | solution.py:38
  (4 other events, 6.2 us)

commit v6 on v5

--- a/solution.py
+++ b/solution.py
@@ -8,7 +8,7 @@
 from jax.sharding import PartitionSpec as P
 
 
-WIDTHS = (384, 640)
+WIDTHS = (512, 512)
 STARTS = tuple(sum(WIDTHS[:c]) for c in range(len(WIDTHS)))
 CHUNKS = len(WIDTHS)
 LOW = jnp.bfloat16
@@ -216,12 +216,26 @@
     )(*ins)
 
 
-def back_kernel(place, param, sa, sb, *refs):
-    ogs, side, outs = refs[: 3 * CHUNKS], refs[3 * CHUNKS], refs[-4:-2]
+def lower_kernel(param, low):
+    low[...] = param[...].astype(LOW)
+
+
+def lower(param):
+    return pl.pallas_call(
+        lower_kernel,
+        out_shape=shape(*param.shape),
+        in_specs=[VMEM],
+        out_specs=VMEM,
+        compiler_params=params(),
+        name="lower",
+    )(param)
+
+
+def back_kernel(place, low, sa, sb, *refs):
+    ogs, side, outs = refs[: 3 * CHUNKS], refs[3 * CHUNKS], refs[-3:-1]
     normed = refs[3 * CHUNKS + 1 : 3 * CHUNKS + 5]
-    pre_grad, low = refs[-2:]
+    pre_grad = refs[-1]
     rows = normed[0].shape[0]
-    low[...] = param[...].astype(LOW)
     for k in range(4):
         got = None
         for c in range(CHUNKS):
@@ -270,7 +284,6 @@
         out_shape=[shape(full // 4, hidden_size)] * 2 + [shape(4 * rows, hidden_size)],
         in_specs=[SMEM] + [VMEM] * (3 + 3 * CHUNKS + 5),
         out_specs=[VMEM] * 3,
-        scratch_shapes=[pltpu.VMEM(param.shape, LOW)],
         compiler_params=params(),
         name="back",
     )(place, param, *slopes, *own, *far, *last, side, *normed)
@@ -398,8 +411,8 @@
 
 
 def prepare(place, fixes, level, tokens, grads, up_p, down_p, up_m, down_m, up_v, down_v):
-    own = pieces(grads, fixes, level)
-    first = cut(place, up_p, own[0])
+    own = pieces(grads)
+    first = cut(place, up_p, own[0], fixes, level)
     ups = [first[0]]
     for k in range(1, 4):
         ups.append(swap(first[k], k))
@@ -411,6 +424,7 @@
     for c in range(CHUNKS):
         far.append(swap(own[c], 2))
     near_act, near_slope = hidden(place, ups, n0, n1)
+    down_low = lower(down_p)
     n3 = swap(n2, 1)
     far_act, far_slope = hidden(place, ups, n2, n3)
     for c in range(CHUNKS):
@@ -421,7 +435,7 @@
         ogs = (own[c], side, far[c], last[c])
         news = down(c, fixes, *acts, ogs, down_p, down_m, down_v, news, n0)
     normed = (n0, n1, n2, n3)
-    g2, g3, pre_grad = back(place, down_p, slopes, own, side, far, last, normed)
+    g2, g3, pre_grad = back(place, down_low, slopes, own, side, far, last, normed)
     g2 = swap(g2, 2)
     g3 = swap(g3, 3)
     g0, g1 = rest_of_back(place, normed, pre_grad)

time: 154 us -> 151 us (0.981)
  waiting for transfers between devices: 89.6 us -> 87 us
    ppermute x14, waiting for transfers between devices: 50.8 us -> 48.2 us  [swap(): return lax.ppermute(array, 'zero', [(i, i ^ mask) for i in range(size)])]
  transfers between devices with their start and end apart: 17 -> 17, of which waited for: 6 -> 7; matrix products, arithmetic and copies ran while one was open for 0% -> 0% of each run, Pallas kernels for 16% -> 16%
where the time goes in v6:
time: 151 us
  waiting for transfers between devices  87 us (58%)
  Pallas kernels  38.7 us (26%)
  starting transfers between devices  21 us (14%)
  local copies, waits for them, and re-layouts  2.25 us (1%)
  between operations  1.72 us (1%)
    ppermute x14, waiting for transfers between devices, swap(): return lax.ppermute(array, 'zero', [(i, i ^ mask) for i in range(size)])  48.2 us
    ppermute x3, waiting for transfers between devices, from_partner(): lax.ppermute(array, 'peer', [(i, (i - by) % size) for i in range(size)])  38.9 us
    ppermute x14, starting transfers between devices, swap(): return lax.ppermute(array, 'zero', [(i, i ^ mask) for i in range(size)])  14.4 us
    pallas_call x2, Pallas kernels, down(): pl.pallas_call(partial(down_kernel, c), out_shape=[shape(rows, cols, dtyp...  10.2 us
    ppermute x3, starting transfers between devices, from_partner(): lax.ppermute(array, 'peer', [(i, (i - by) % size) for i in range(size)])  6.55 us
    pallas_call x2, Pallas kernels, hidden(): pl.pallas_call(hidden_kernel, out_shape=[shape(width, 2 * rows), shape(2...  6.41 us
    pallas_call x2, Pallas kernels, up(): pl.pallas_call(partial(up_kernel, base), in_specs=in_specs, out_specs=[VM...  6.12 us
    pallas_call x1, Pallas kernels, mean_down(): pl.pallas_call(mean_down_kernel, grid=(8,), out_shape=shape(rows, cols, d...  5.43 us
  transfers between devices with their start and end apart: 17, of which 7 were waited for; matrix products, arithmetic and copies ran while one was open for 0% of the time, Pallas kernels for 16%

profile of v6, /device:TPU:1, one launch (start us, length us, event | category | flops | bytes accessed | tf_op | source)
XLA Modules:
  0.0 151.1 jit_solution(18055208754237093804)
XLA Ops:
  2.9 1.9 %cut.1 = (bf16[256,512]{1,0:T(8,128)(2,1)S(1)}, bf16[256,512]{1,0:T(8,128)(2,1)S(1)}, bf16[256,512]{1,0:T(8,128)(2,1)S(1)}, bf16[256,512]{1,0:T(8,128)(2,1)S(1)}) custom-call(s32[1]{0:T(128)} %bitcast.11.place, f32[256,2048]{1,0:T(8,128)} %bitcast.34, bf16[512,512]{1,0:T(8,128)(2,1)S(1)} %get-tuple-element.254.refs_0_.o0, ...), custom_call_target="tpu_custom_call" | custom-call | tf_op jit(solution)/shard_map/cut/pallas_call | solution.py:69
  4.8 1.7 %norm.1.left.refs_7_.refs_0_.rest_0_ = bf16[512,1024]{1,0:T(8,128)(2,1)S(1)} custom-call(bf16[512,1024]{1,0:T(8,128)(2,1)S(1)} %bitcast.31, bf16[256,512]{1,0:T(8,128)(2,1)S(1)} %get-tuple-element.255._.u0), custom_call_target="tpu_custom_call" | custom-call | tf_op jit(solution)/shard_map/norm/pallas_call | solution.py:110
  6.5 2.5 %collective-permute-start.19 = (bf16[512,1024]{1,0:T(8,128)(2,1)S(1)}, bf16[512,1024]{1,0:T(8,128)(2,1)S(1)}, u32[]{:S(2)}, u32[]{:S(2)}) collective-permute-start(bf16[512,1024]{1,0:T(8,128)(2,1)S(1)} %norm.1.left.refs_7_.refs_0_.rest_0_), channel_id=1, source_target_pairs={{0,2},{1,3},{2,0},{3,1},{4,6},{5,7},{6,4},{7,5},{8,10},{9,11},{10,... | collective-permute-start | bytes 3145736 | tf_op jit(solution)/shard_map/ppermute | solution.py:33
  9.9 1.6 %collective-permute-start.17 = (bf16[256,512]{1,0:T(8,128)(2,1)S(1)}, bf16[256,512]{1,0:T(8,128)(2,1)S(1)}, u32[]{:S(2)}, u32[]{:S(2)}) collective-permute-start(bf16[256,512]{1,0:T(8,128)(2,1)S(1)} %get-tuple-element.258), channel_id=1, source_target_pairs={{0,3},{1,2},{2,1},{3,0},{4,7},{5,6},{6,5},{7,4},{8,11},{9,10},{10,... | collective-permute-start | bytes 786440 | tf_op jit(solution)/shard_map/ppermute | solution.py:33
  11.8 20.0 %collective-permute-done.19.left.refs_9_.refs_2_ = bf16[512,1024]{1,0:T(8,128)(2,1)S(1)} collective-permute-done((bf16[512,1024]{1,0:T(8,128)(2,1)S(1)}, bf16[512,1024]{1,0:T(8,128)(2,1)S(1)}, u32[]{:S(2)}, u32[]{:S(2)}) %collective-permute-start.19) | collective-permute-done | bytes 1048608 | tf_op jit(solution)/shard_map/ppermute | solution.py:33
  31.9 2.1 %collective-permute-start.20 = (bf16[512,1024]{1,0:T(8,128)(2,1)S(1)}, bf16[512,1024]{1,0:T(8,128)(2,1)S(1)}, u32[]{:S(2)}, u32[]{:S(2)}) collective-permute-start(bf16[512,1024]{1,0:T(8,128)(2,1)S(1)} %collective-permute-done.19.left.refs_9_.refs_2_), channel_id=1, source_target_pairs={{0,1},{1,0},{2,3},{3,2},{4,5},{5,4},{6,7},{7,6},{8,9},{9,8},{10,11... | collective-permute-start | bytes 3145736 | tf_op jit(solution)/shard_map/ppermute | solution.py:33
  34.0 3.5 %collective-permute-done.16.u2 = bf16[256,512]{1,0:T(8,128)(2,1)S(1)} collective-permute-done((bf16[256,512]{1,0:T(8,128)(2,1)S(1)}, bf16[256,512]{1,0:T(8,128)(2,1)S(1)}, u32[]{:S(2)}, u32[]{:S(2)}) %collective-permute-start.16) | collective-permute-done | bytes 262176 | tf_op jit(solution)/shard_map/ppermute | solution.py:33
  38.7 5.8 %collective-permute-done.17.u3 = bf16[256,512]{1,0:T(8,128)(2,1)S(1)} collective-permute-done((bf16[256,512]{1,0:T(8,128)(2,1)S(1)}, bf16[256,512]{1,0:T(8,128)(2,1)S(1)}, u32[]{:S(2)}, u32[]{:S(2)}) %collective-permute-start.17) | collective-permute-done | bytes 262176 | tf_op jit(solution)/shard_map/ppermute | solution.py:33
  44.7 9.6 %collective-permute-done.22.refs_3_.o2 = bf16[512,512]{1,0:T(8,128)(2,1)S(1)} collective-permute-done((bf16[512,512]{1,0:T(8,128)(2,1)S(1)}, bf16[512,512]{1,0:T(8,128)(2,1)S(1)}, u32[]{:S(2)}, u32[]{:S(2)}) %collective-permute-start.22) | collective-permute-done | bytes 524320 | tf_op jit(solution)/shard_map/ppermute | solution.py:33
  54.3 2.1 %collective-permute-start.24 = (bf16[512,512]{1,0:T(8,128)(2,1)S(1)}, bf16[512,512]{1,0:T(8,128)(2,1)S(1)}, u32[]{:S(2)}, u32[]{:S(2)}) collective-permute-start(bf16[512,512]{1,0:T(8,128)(2,1)S(1)} %collective-permute-done.22.refs_3_.o2), channel_id=1, source_target_pairs={{0,1},{1,0},{2,3},{3,2},{4,5},{5,4},{6,7},{7,6},{8,9},{9,8},{10,11... | collective-permute-start | bytes 1572872 | tf_op jit(solution)/shard_map/ppermute | solution.py:33
  56.4 9.1 %collective-permute-done.21.refs_2_.o2 = bf16[512,512]{1,0:T(8,128)(2,1)S(1)} collective-permute-done((bf16[512,512]{1,0:T(8,128)(2,1)S(1)}, bf16[512,512]{1,0:T(8,128)(2,1)S(1)}, u32[]{:S(2)}, u32[]{:S(2)}) %collective-permute-start.21) | collective-permute-done | bytes 524320 | tf_op jit(solution)/shard_map/ppermute | solution.py:33
  66.9 3.2 %hidden.2 = (bf16[512,1024]{1,0:T(8,128)(2,1)S(1)}, f32[1024,512]{1,0:T(8,128)S(1)}) custom-call(s32[1]{0:T(128)} %bitcast.11.place, bf16[256,512]{1,0:T(8,128)(2,1)S(1)} %get-tuple-element.255._.u0, bf16[256,512]{1,0:T(8,128)(2,1)S(1)} %collective-permute-done.15.u1, bf16[256,512]{1,0:T(8,128)(2,1)S(1)} %collective-permute-done.16.u2, ...), custom_call_target="tpu_custom_call" | custom-call | tf_op jit(solution)/shard_map/hidden/pallas_call | solution.py:147
  70.2 3.2 %hidden.3 = (bf16[512,1024]{1,0:T(8,128)(2,1)S(1)}, f32[1024,512]{1,0:T(8,128)S(1)}) custom-call(s32[1]{0:T(128)} %bitcast.11.place, bf16[256,512]{1,0:T(8,128)(2,1)S(1)} %get-tuple-element.255._.u0, bf16[256,512]{1,0:T(8,128)(2,1)S(1)} %collective-permute-done.15.u1, bf16[256,512]{1,0:T(8,128)(2,1)S(1)} %collective-permute-done.16.u2, ...), custom_call_target="tpu_custom_call" | custom-call | tf_op jit(solution)/shard_map/hidden/pallas_call | solution.py:147
  73.4 3.5 %back.1 = (bf16[256,512]{1,0:T(8,128)(2,1)S(1)}, bf16[256,512]{1,0:T(8,128)(2,1)S(1)}, bf16[2048,512]{1,0:T(8,128)(2,1)S(1)}) custom-call(s32[1]{0:T(128)} %bitcast.11.place, bf16[512,1024]{1,0:T(8,128)(2,1)S(1)} %lower.1.low, f32[1024,512]{1,0:T(8,128)S(1)} %get-tuple-element.259.sa, f32[1024,512]{1,0:T(8,128)S(1)} %get-tuple-element.260.sb, ...), custom_call_target="tpu_custom_call" | custom-call | tf_op jit(solution)/shard_map/back/pallas_call | solution.py:282
  80.5 5.1 %down.2 = (f32[512,1024]{1,0:T(8,128)}, bf16[512,1024]{1,0:T(8,128)(2,1)S(1)}, f32[512,1024]{1,0:T(8,128)}, f32[512,1024]{1,0:T(8,128)}) custom-call(f32[2]{0:T(128)S(1)} %pad_maximum_fusion.refs_1_.fixes, bf16[512,1024]{1,0:T(8,128)(2,1)S(1)} %get-tuple-element.271.near, bf16[512,1024]{1,0:T(8,128)(2,1)S(1)} %get-tuple-element.272.far, ...), custom_call_target="tpu_custom_call" | custom-call | tf_op jit(solution)/shard_map/down/pallas_call | solution.py:206
  85.6 5.1 %down.3 = (f32[512,1024]{1,0:T(8,128)}, bf16[512,1024]{1,0:T(8,128)(2,1)S(1)}, f32[512,1024]{1,0:T(8,128)}, f32[512,1024]{1,0:T(8,128)}) custom-call(f32[2]{0:T(128)S(1)} %pad_maximum_fusion.refs_1_.fixes, bf16[512,1024]{1,0:T(8,128)(2,1)S(1)} %get-tuple-element.271.near, ...), custom_call_target="tpu_custom_call", output_to_operand_aliasing={{0}: (11, {}), {1}: (12, {}), {2}: (13, {}), {3}: (14, {})} | custom-call | tf_op jit(solution)/shard_map/down/pallas_call | solution.py:206
  90.7 3.1 %up.11 = (f32[512,512]{1,0:T(8,128)S(1)}, bf16[512,512]{1,0:T(8,128)(2,1)S(1)}, f32[256,2048]{1,0:T(8,128)}, f32[256,2048]{1,0:T(8,128)}) custom-call(s32[1]{0:T(128)} %bitcast.11.place, f32[2]{0:T(128)S(1)} %pad_maximum_fusion.refs_1_.fixes, bf16[256,512]{1,0:T(8,128)(2,1)S(1)} %get-tuple-element.265.left.rest_0_, ...), custom_call_target="tpu_custom_call" | custom-call | tf_op jit(solution)/shard_map/up/pallas_call | solution.py:343
  93.8 57.2 %conditional.1 = (f32[256,2048]{1,0:T(8,128)}, f32[256,2048]{1,0:T(8,128)}, f32[1,256,2048]{2,1,0:T(8,128)}, f32[1,512,1024]{2,1,0:T(8,128)}) conditional(s32[]{:T(128)} %bitcast.10, (s32[1]{0:T(128)}, f32[2]{0:T(128)S(1)}, bf16[256,512]{1,0:T(8,128)(2,1)S(1)}, bf16[256,512]{1,0:T(8,128)(2,1)S(1)}, ...), branch_computations={%region_0.1_spmd, %region_1.2_spmd, %region_2.3_spmd, %region_3.4_... | conditional | bytes 20971728 | solution.py:477
  94.1 3.5 %collective-permute-start.14 = (bf16[512,1024]{1,0:T(8,128)(2,1)S(1)}, bf16[512,1024]{1,0:T(8,128)(2,1)S(1)}, u32[]{:S(2)}, u32[]{:S(2)}) collective-permute-start(bf16[512,1024]{1,0:T(8,128)(2,1)S(1)} %get-tuple-element.216), channel_id=1, source_target_pairs={{0,64},{4,68},{8,72},{12,76},{16,80},{20,84},{24,88},{28,92},{32,9... | collective-permute-start | bytes 3145736 | tf_op jit(solution)/shard_map/cond/branch_4_fun/ppermute | solution.py:38
  97.7 3.1 %up.10 = (f32[512,512]{1,0:T(8,128)S(1)}, bf16[512,512]{1,0:T(8,128)(2,1)S(1)}, f32[256,2048]{1,0:T(8,128)}, f32[256,2048]{1,0:T(8,128)}) custom-call(s32[1]{0:T(128)} %get-tuple-element.200.place, f32[2]{0:T(128)S(1)} %get-tuple-element.201.fixes, bf16[256,512]{1,0:T(8,128)(2,1)S(1)} %get-tuple-element.202.left, ...), custom_call_target="tpu_custom_call", output_to_operand_aliasing={{2}: (7, {}), {3}: (8, {})} | custom-call | tf_op jit(solution)/shard_map/cond/branch_4_fun/up/pallas_call | solution.py:343
  100.7 3.0 %collective-permute-start.12 = (bf16[512,512]{1,0:T(8,128)(2,1)S(1)}, bf16[512,512]{1,0:T(8,128)(2,1)S(1)}, u32[]{:S(2)}, u32[]{:S(2)}) collective-permute-start(bf16[512,512]{1,0:T(8,128)(2,1)S(1)} %get-tuple-element.212), channel_id=1, source_target_pairs={{0,64},{4,68},{8,72},{12,76},{16,80},{20,84},{24,88},{28,92},{32,9... | collective-permute-start | bytes 1572872 | tf_op jit(solution)/shard_map/cond/branch_4_fun/ppermute | solution.py:38
  103.7 28.7 %collective-permute-done.13.other = bf16[512,512]{1,0:T(8,128)(2,1)S(1)} collective-permute-done((bf16[512,512]{1,0:T(8,128)(2,1)S(1)}, bf16[512,512]{1,0:T(8,128)(2,1)S(1)}, u32[]{:S(2)}, u32[]{:S(2)}) %collective-permute-start.13) | collective-permute-done | bytes 524320 | tf_op jit(solution)/shard_map/cond/branch_4_fun/ppermute | solution.py:38
  133.4 10.2 %collective-permute-done.12.other = bf16[512,512]{1,0:T(8,128)(2,1)S(1)} collective-permute-done((bf16[512,512]{1,0:T(8,128)(2,1)S(1)}, bf16[512,512]{1,0:T(8,128)(2,1)S(1)}, u32[]{:S(2)}, u32[]{:S(2)}) %collective-permute-start.12) | collective-permute-done | bytes 524320 | tf_op jit(solution)/shard_map/cond/branch_4_fun/ppermute | solution.py:38
  145.6 5.4 %mean_down.9 = f32[512,1024]{1,0:T(8,128)} custom-call(f32[512,1024]{1,0:T(8,128)S(1)} %copy-done.11, bf16[512,1024]{1,0:T(8,128)(2,1)} %copy-done.18), custom_call_target="tpu_custom_call" | custom-call | tf_op jit(solution)/shard_map/cond/branch_4_fun/mean_down/pallas_call | solution.py:368
  (49 shorter events, 12.1 us)
Async XLA Ops:
  0.6 4.1 %copy-start.3 = (bf16[1,512,1024]{2,1,0:T(8,128)(2,1)S(1)}, bf16[1,512,1024]{2,1,0:T(8,128)(2,1)}, u32[]{:S(2)}) copy-start(bf16[1,512,1024]{2,1,0:T(8,128)(2,1)} %param.14) | copy-start | bytes 3145732
  2.9 41.6 %copy-start.5 = (bf16[1,512,1024]{2,1,0:T(8,128)(2,1)S(1)}, bf16[1,512,1024]{2,1,0:T(8,128)(2,1)}, u32[]{:S(2)}) copy-start(bf16[1,512,1024]{2,1,0:T(8,128)(2,1)} %param.15) | copy-start | bytes 3145732
  2.9 63.9 %copy-start = (f32[1,512,1024]{2,1,0:T(8,128)S(1)}, f32[1,512,1024]{2,1,0:T(8,128)}, u32[]{:S(2)}) copy-start(f32[1,512,1024]{2,1,0:T(8,128)} %param.18) | copy-start | bytes 6291460
  6.5 25.4 %collective-permute-start.19 = (bf16[512,1024]{1,0:T(8,128)(2,1)S(1)}, bf16[512,1024]{1,0:T(8,128)(2,1)S(1)}, u32[]{:S(2)}, u32[]{:S(2)}) collective-permute-start(bf16[512,1024]{1,0:T(8,128)(2,1)S(1)} %norm.1.left.refs_7_.refs_0_.rest_0_), channel_id=1, source_target_pairs={{0,2},{1,3},{2,0},{3,1},{4,6},{5,7},{6,4},{7,5},{8,10},{9,11},{10,... | collective-permute-start | bytes 3145736 | tf_op jit(solution)/shard_map/ppermute | solution.py:33
  9.0 2.8 %collective-permute-start.15 = (bf16[256,512]{1,0:T(8,128)(2,1)S(1)}, bf16[256,512]{1,0:T(8,128)(2,1)S(1)}, u32[]{:S(2)}, u32[]{:S(2)}) collective-permute-start(bf16[256,512]{1,0:T(8,128)(2,1)S(1)} %get-tuple-element.256), channel_id=1, source_target_pairs={{0,1},{1,0},{2,3},{3,2},{4,5},{5,4},{6,7},{7,6},{8,9},{9,8},{10,11... | collective-permute-start | bytes 786440 | tf_op jit(solution)/shard_map/ppermute | solution.py:33
  9.9 27.5 %collective-permute-start.16 = (bf16[256,512]{1,0:T(8,128)(2,1)S(1)}, bf16[256,512]{1,0:T(8,128)(2,1)S(1)}, u32[]{:S(2)}, u32[]{:S(2)}) collective-permute-start(bf16[256,512]{1,0:T(8,128)(2,1)S(1)} %get-tuple-element.257), channel_id=1, source_target_pairs={{0,2},{1,3},{2,0},{3,1},{4,6},{5,7},{6,4},{7,5},{8,10},{9,11},{10,... | collective-permute-start | bytes 786440 | tf_op jit(solution)/shard_map/ppermute | solution.py:33
  9.9 34.6 %collective-permute-start.17 = (bf16[256,512]{1,0:T(8,128)(2,1)S(1)}, bf16[256,512]{1,0:T(8,128)(2,1)S(1)}, u32[]{:S(2)}, u32[]{:S(2)}) collective-permute-start(bf16[256,512]{1,0:T(8,128)(2,1)S(1)} %get-tuple-element.258), channel_id=1, source_target_pairs={{0,3},{1,2},{2,1},{3,0},{4,7},{5,6},{6,5},{7,4},{8,11},{9,10},{10,... | collective-permute-start | bytes 786440 | tf_op jit(solution)/shard_map/ppermute | solution.py:33
  11.6 55.3 %collective-permute-start.18 = (bf16[512,1024]{1,0:T(8,128)(2,1)S(1)}, bf16[512,1024]{1,0:T(8,128)(2,1)S(1)}, u32[]{:S(2)}, u32[]{:S(2)}) collective-permute-start(bf16[512,1024]{1,0:T(8,128)(2,1)S(1)} %norm.1.left.refs_7_.refs_0_.rest_0_), channel_id=1, source_target_pairs={{0,1},{1,0},{2,3},{3,2},{4,5},{5,4},{6,7},{7,6},{8,9},{9,8},{10,11... | collective-permute-start | bytes 3145736 | tf_op jit(solution)/shard_map/ppermute | solution.py:33
  11.8 42.5 %collective-permute-start.22 = (bf16[512,512]{1,0:T(8,128)(2,1)S(1)}, bf16[512,512]{1,0:T(8,128)(2,1)S(1)}, u32[]{:S(2)}, u32[]{:S(2)}) collective-permute-start(bf16[512,512]{1,0:T(8,128)(2,1)S(1)} %get-tuple-element.261.refs_1_.o0), channel_id=1, source_target_pairs={{0,2},{1,3},{2,0},{3,1},{4,6},{5,7},{6,4},{7,5},{8,10},{9,11},{10,... | collective-permute-start | bytes 1572872 | tf_op jit(solution)/shard_map/ppermute | solution.py:33
  31.9 38.3 %collective-permute-start.20 = (bf16[512,1024]{1,0:T(8,128)(2,1)S(1)}, bf16[512,1024]{1,0:T(8,128)(2,1)S(1)}, u32[]{:S(2)}, u32[]{:S(2)}) collective-permute-start(bf16[512,1024]{1,0:T(8,128)(2,1)S(1)} %collective-permute-done.19.left.refs_9_.refs_2_), channel_id=1, source_target_pairs={{0,1},{1,0},{2,3},{3,2},{4,5},{5,4},{6,7},{7,6},{8,9},{9,8},{10,11... | collective-permute-start | bytes 3145736 | tf_op jit(solution)/shard_map/ppermute | solution.py:33
  37.5 28.1 %collective-permute-start.21 = (bf16[512,512]{1,0:T(8,128)(2,1)S(1)}, bf16[512,512]{1,0:T(8,128)(2,1)S(1)}, u32[]{:S(2)}, u32[]{:S(2)}) collective-permute-start(bf16[512,512]{1,0:T(8,128)(2,1)S(1)} %get-tuple-element.254.refs_0_.o0), channel_id=1, source_target_pairs={{0,2},{1,3},{2,0},{3,1},{4,6},{5,7},{6,4},{7,5},{8,10},{9,11},{10,... | collective-permute-start | bytes 1572872 | tf_op jit(solution)/shard_map/ppermute | solution.py:33
  44.5 28.9 %collective-permute-start.25 = (bf16[512,1024]{1,0:T(8,128)(2,1)S(1)}, bf16[512,1024]{1,0:T(8,128)(2,1)S(1)}, u32[]{:S(2)}, u32[]{:S(2)}) collective-permute-start(bf16[512,1024]{1,0:T(8,128)(2,1)S(1)} %bitcast.33), channel_id=1, source_target_pairs={{0,1},{1,0},{2,3},{3,2},{4,5},{5,4},{6,7},{7,6},{8,9},{9,8},{10,11... | collective-permute-start | bytes 3145736 | tf_op jit(solution)/shard_map/ppermute | solution.py:33
  54.3 19.0 %collective-permute-start.24 = (bf16[512,512]{1,0:T(8,128)(2,1)S(1)}, bf16[512,512]{1,0:T(8,128)(2,1)S(1)}, u32[]{:S(2)}, u32[]{:S(2)}) collective-permute-start(bf16[512,512]{1,0:T(8,128)(2,1)S(1)} %collective-permute-done.22.refs_3_.o2), channel_id=1, source_target_pairs={{0,1},{1,0},{2,3},{3,2},{4,5},{5,4},{6,7},{7,6},{8,9},{9,8},{10,11... | collective-permute-start | bytes 1572872 | tf_op jit(solution)/shard_map/ppermute | solution.py:33
  65.6 7.8 %collective-permute-start.23 = (bf16[512,512]{1,0:T(8,128)(2,1)S(1)}, bf16[512,512]{1,0:T(8,128)(2,1)S(1)}, u32[]{:S(2)}, u32[]{:S(2)}) collective-permute-start(bf16[512,512]{1,0:T(8,128)(2,1)S(1)} %collective-permute-done.21.refs_2_.o2), channel_id=1, source_target_pairs={{0,1},{1,0},{2,3},{3,2},{4,5},{5,4},{6,7},{7,6},{8,9},{9,8},{10,11... | collective-permute-start | bytes 1572872 | tf_op jit(solution)/shard_map/ppermute | solution.py:33
  76.9 3.6 %copy-start.1 = (f32[1,512,1024]{2,1,0:T(8,128)S(1)}, f32[1,512,1024]{2,1,0:T(8,128)}, u32[]{:S(2)}) copy-start(f32[1,512,1024]{2,1,0:T(8,128)} %param.20) | copy-start | bytes 6291460
  78.2 12.5 %collective-permute-start.28 = (bf16[256,512]{1,0:T(8,128)(2,1)S(1)}, bf16[256,512]{1,0:T(8,128)(2,1)S(1)}, u32[]{:S(2)}, u32[]{:S(2)}) collective-permute-start(bf16[256,512]{1,0:T(8,128)(2,1)S(1)} %get-tuple-element.266), channel_id=1, source_target_pairs={{0,1},{1,0},{2,3},{3,2},{4,5},{5,4},{6,7},{7,6},{8,9},{9,8},{10,11... | collective-permute-start | bytes 786440 | tf_op jit(solution)/shard_map/ppermute | solution.py:33
  78.3 15.5 %collective-permute-start.26 = (bf16[256,512]{1,0:T(8,128)(2,1)S(1)}, bf16[256,512]{1,0:T(8,128)(2,1)S(1)}, u32[]{:S(2)}, u32[]{:S(2)}) collective-permute-start(bf16[256,512]{1,0:T(8,128)(2,1)S(1)} %get-tuple-element.262), channel_id=1, source_target_pairs={{0,2},{1,3},{2,0},{3,1},{4,6},{5,7},{6,4},{7,5},{8,10},{9,11},{10,... | collective-permute-start | bytes 786440 | tf_op jit(solution)/shard_map/ppermute | solution.py:33
  79.9 14.0 %collective-permute-start.27 = (bf16[256,512]{1,0:T(8,128)(2,1)S(1)}, bf16[256,512]{1,0:T(8,128)(2,1)S(1)}, u32[]{:S(2)}, u32[]{:S(2)}) collective-permute-start(bf16[256,512]{1,0:T(8,128)(2,1)S(1)} %get-tuple-element.263), channel_id=1, source_target_pairs={{0,3},{1,2},{2,1},{3,0},{4,7},{5,6},{6,5},{7,4},{8,11},{9,10},{10,... | collective-permute-start | bytes 786440 | tf_op jit(solution)/shard_map/ppermute | solution.py:33
  85.6 5.2 %copy-start.6 = (f32[1,256,2048]{2,1,0:T(8,128)S(1)}, f32[1,256,2048]{2,1,0:T(8,128)}, u32[]{:S(2)}) copy-start(f32[1,256,2048]{2,1,0:T(8,128)} %param.17) | copy-start | bytes 6291460
  85.6 5.2 %copy-start.12 = (f32[1,256,2048]{2,1,0:T(8,128)S(1)}, f32[1,256,2048]{2,1,0:T(8,128)}, u32[]{:S(2)}) copy-start(f32[1,256,2048]{2,1,0:T(8,128)} %param.19) | copy-start | bytes 6291460
  85.6 5.1 %copy-start.13 = (f32[1,256,2048]{2,1,0:T(8,128)S(1)}, f32[1,256,2048]{2,1,0:T(8,128)}, u32[]{:S(2)}) copy-start(f32[1,256,2048]{2,1,0:T(8,128)} %param.21) | copy-start | bytes 6291460
  94.1 50.6 %collective-permute-start.14 = (bf16[512,1024]{1,0:T(8,128)(2,1)S(1)}, bf16[512,1024]{1,0:T(8,128)(2,1)S(1)}, u32[]{:S(2)}, u32[]{:S(2)}) collective-permute-start(bf16[512,1024]{1,0:T(8,128)(2,1)S(1)} %get-tuple-element.216), channel_id=1, source_target_pairs={{0,64},{4,68},{8,72},{12,76},{16,80},{20,84},{24,88},{28,92},{32,9... | collective-permute-start | bytes 3145736 | tf_op jit(solution)/shard_map/cond/branch_4_fun/ppermute | solution.py:38
  97.6 34.8 %collective-permute-start.13 = (bf16[512,512]{1,0:T(8,128)(2,1)S(1)}, bf16[512,512]{1,0:T(8,128)(2,1)S(1)}, u32[]{:S(2)}, u32[]{:S(2)}) collective-permute-start(bf16[512,512]{1,0:T(8,128)(2,1)S(1)} %get-tuple-element.214), channel_id=1, source_target_pairs={{0,64},{4,68},{8,72},{12,76},{16,80},{20,84},{24,88},{28,92},{32,9... | collective-permute-start | bytes 1572872 | tf_op jit(solution)/shard_map/cond/branch_4_fun/ppermute | solution.py:38
  100.7 42.9 %collective-permute-start.12 = (bf16[512,512]{1,0:T(8,128)(2,1)S(1)}, bf16[512,512]{1,0:T(8,128)(2,1)S(1)}, u32[]{:S(2)}, u32[]{:S(2)}) collective-permute-start(bf16[512,512]{1,0:T(8,128)(2,1)S(1)} %get-tuple-element.212), channel_id=1, source_target_pairs={{0,64},{4,68},{8,72},{12,76},{16,80},{20,84},{24,88},{28,92},{32,9... | collective-permute-start | bytes 1572872 | tf_op jit(solution)/shard_map/cond/branch_4_fun/ppermute | solution.py:38
  (4 other events, 7.8 us)
